TPU v7x, 256 devices: a whole 4x4x8 slice. The times are simulated.
256 devices in a mesh: row: 8 (over x, core), col: 32 (over y, z).
Axes of the slice: x: 4, y: 4, z: 8, core: 2. Of those that a mesh axis runs over, the one named last changes fastest.
Arguments:
- velocity_start: float32 [2, 512, 4096], P(None, 'row', 'col'), may hold values from -3 to 3
- stress_start: float32 [3, 512, 4096], P(None, 'row', 'col'), may hold values from -3 to 3
- wind_stress: float32 [2, 512, 4096], P(None, 'row', 'col'), may hold values from -6 to 6
- ocean_current: float32 [2, 512, 4096], P(None, 'row', 'col'), may hold values from -3 to 3
- ice_area: float32 [5, 512, 4096], P(None, 'row', 'col'), may hold values from 0.15 to 0.2
- ice_volume: float32 [5, 512, 4096], P(None, 'row', 'col'), may hold values from 0.05 to 0.6
- inverse_width: float32 [512, 4096], P('row', 'col'), may hold values from 0.7 to 1.4
- inverse_height: float32 [512, 4096], P('row', 'col'), may hold values from 0.7 to 1.4
- land_block: int32 [128, 128], P('row', 'col'), may hold values 0 or 1
- ice_block: int32 [128, 128], P('row', 'col'), may hold values 0 or 1
- writer: int32 [32], replicated, may hold values from 0 to 7
Outputs:
- velocity: float32 [2, 512, 4096], P(None, 'row', 'col')
- stress: float32 [3, 512, 4096], P(None, 'row', 'col')
- restart: float32 [8, 10, 512, 4096], P('row', None, None, 'col')
All inputs are finite; a program needn't handle non-finite values. No bound on the sum of `land_block` or of `ice_block` on one device may be relied on, other than what follows from the above.
Results may differ from a plain program's by a relative error of at most 0.00002.
Values sent between devices are 32-bit elements; how exact they have to be, the bound alone decides.
No kernel may reach another device: no remote copies, remote signals or barrier semaphores. Data moves between devices by JAX's collectives and lax.ppermute only.
A program may use at most 64 MiB of HBM per device.

v0:
```python
import jax
import jax.numpy as jnp
from jax import lax
from jax.sharding import PartitionSpec as P

SUB = 12


strength_scale = 4.0
hibler_decay = 20.0
mass_rate = 16.0
water_drag = 1.0
coriolis = 0.5
relax_rate = 0.5
ellipse_square = 4.0
delta_margin = 0.5


def shifted(value, axis, steps):
    count = lax.axis_size(axis)
    pairs = [(source, (source + steps) % count) for source in range(count)]
    return lax.ppermute(value, axis, pairs)


def from_behind(value, axis, by):
    count = lax.axis_size(axis)
    pairs = [(i, i + by) for i in range(count) if 0 <= i + by < count]
    return lax.ppermute(value, axis, pairs)


def sent_to_all(value, axis):
    count = lax.axis_size(axis)
    return lax.all_to_all(
        jnp.broadcast_to(value[None], (count, *value.shape)), axis, 0, 0, tiled=True
    )


def joined_along(tiles, dim):
    tiles = jnp.moveaxis(tiles, 0, dim)
    lengths = tiles.shape
    return tiles.reshape(*lengths[:dim], lengths[dim] * lengths[dim + 1], *lengths[dim + 2 :])


def gather_directly(value, axis, dim):
    tiles = sent_to_all(value, axis)
    return joined_along(tiles, dim)


def expand_blocks(blocks, height, breadth):
    counted = blocks.astype(jnp.float32)
    block_rows, block_cols = counted.shape
    spread = jnp.broadcast_to(
        counted[:, None, :, None],
        (block_rows, height // block_rows, block_cols, breadth // block_cols),
    )
    return spread.reshape(height, breadth)


def stress_update(
    stresses, strength, across_scale, along_scale, north_east, north_west, south_east, south_west
):
    grad_ux = 0.5 * across_scale * (north_east[0] + south_east[0] - (north_west[0] + south_west[0]))
    grad_vy = 0.5 * along_scale * (north_east[1] + north_west[1] - (south_east[1] + south_west[1]))
    grad_uy = 0.5 * along_scale * (north_east[0] + north_west[0] - (south_east[0] + south_west[0]))
    grad_vx = 0.5 * across_scale * (north_east[1] + south_east[1] - (north_west[1] + south_west[1]))
    divergence = grad_ux + grad_vy
    tension = grad_ux - grad_vy
    shearing = grad_uy + grad_vx
    deform = jnp.sqrt(
        divergence * divergence + (tension * tension + shearing * shearing) / ellipse_square
    )
    viscous = strength / (deform + delta_margin)
    normal_sum = (stresses[0] + relax_rate * viscous * (divergence - deform)) / (1.0 + relax_rate)
    normal_diff = (stresses[1] + relax_rate * viscous * tension / ellipse_square) / (
        1.0 + relax_rate
    )
    shear_new = (stresses[2] + relax_rate * viscous * shearing / (2.0 * ellipse_square)) / (
        1.0 + relax_rate
    )
    return jnp.stack([normal_sum, normal_diff, shear_new])


def normal_xx(stresses):
    return 0.5 * (stresses[0] + stresses[1])


def normal_yy(stresses):
    return 0.5 * (stresses[0] - stresses[1])


def stress_force(across_scale, along_scale, south_west, south_east, north_west, north_east):
    force_x = 0.5 * across_scale * (
        normal_xx(south_east)
        + normal_xx(north_east)
        - (normal_xx(south_west) + normal_xx(north_west))
    ) + 0.5 * along_scale * (north_west[2] + north_east[2] - (south_west[2] + south_east[2]))
    force_y = 0.5 * across_scale * (
        south_east[2] + north_east[2] - (south_west[2] + north_west[2])
    ) + 0.5 * along_scale * (
        normal_yy(north_west)
        + normal_yy(north_east)
        - (normal_yy(south_west) + normal_yy(south_east))
    )
    return (force_x, force_y)


def momentum(
    velocity, force_x, force_y, inertia, turning, wind_stress, ocean_current, land_cells, ice_cells
):
    damped = inertia + water_drag
    right_x = inertia * velocity[0] + force_x + wind_stress[0] + water_drag * ocean_current[0]
    right_y = inertia * velocity[1] + force_y + wind_stress[1] + water_drag * ocean_current[1]
    denominator = damped * damped + turning * turning
    next_u = (damped * right_x + turning * right_y) / denominator
    next_v = (damped * right_y - turning * right_x) / denominator
    moving = jnp.stack([next_u, next_v])
    return land_cells * (ice_cells * moving + (1.0 - ice_cells) * ocean_current)


def neighbour_views(stacked, offset):
    members = stacked.shape[0]
    if offset == 1:
        edge_line = stacked[:, :, -1]
    else:
        edge_line = stacked[:, :, 0]
    arrived = shifted(edge_line, "col", offset)
    if offset == 1:
        beside = jnp.concatenate([arrived[:, :, None], stacked[:, :, :-1]], axis=2)
        rows_out = jnp.concatenate([stacked[:, -1], beside[:, -1]], axis=0)
    else:
        beside = jnp.concatenate([stacked[:, :, 1:], arrived[:, :, None]], axis=2)
        rows_out = jnp.concatenate([stacked[:, 0], beside[:, 0]], axis=0)
    landed = from_behind(rows_out, "row", offset)
    if offset == 1:
        vertical = jnp.concatenate([landed[:members, None], stacked[:, :-1]], axis=1)
        diagonal = jnp.concatenate([landed[members:, None], beside[:, :-1]], axis=1)
    else:
        vertical = jnp.concatenate([stacked[:, 1:], landed[:members, None]], axis=1)
        diagonal = jnp.concatenate([beside[:, 1:], landed[members:, None]], axis=1)
    return (beside, vertical, diagonal)


def fold_ghost(stresses):
    top_row = stresses[:, -1, :]
    whole_row = gather_directly(top_row, "col", 1)
    turned = whole_row[:, ::-1]
    looped = jnp.concatenate([turned, turned[:, :1]], axis=1)
    offset_start = lax.axis_index("col") * top_row.shape[1]
    return lax.dynamic_slice_in_dim(looped, offset_start, top_row.shape[1] + 1, 1)


def restart_strip(ice_area, ice_volume, writer):
    snapshot = jnp.concatenate([ice_area, ice_volume], axis=0)
    strip_rows = lax.all_gather(snapshot, "row", axis=1, tiled=True)
    strips = jnp.arange(writer.shape[0], dtype=jnp.int32)
    chosen = jnp.sum(jnp.where(strips == lax.axis_index("col"), writer, 0))
    is_writer = chosen == lax.axis_index("row")
    return jnp.where(is_writer, strip_rows, jnp.zeros_like(strip_rows))[None]


def shards(
    velocity_start,
    stress_start,
    wind_stress,
    ocean_current,
    ice_area,
    ice_volume,
    inverse_width,
    inverse_height,
    land_block,
    ice_block,
    writer,
):
    height, breadth = inverse_width.shape
    land_cells = expand_blocks(land_block, height, breadth)
    ice_cells = expand_blocks(ice_block, height, breadth)
    area_total = jnp.sum(ice_area, axis=0)
    volume_total = jnp.sum(ice_volume, axis=0)
    strength = (
        strength_scale * volume_total * jnp.exp(-hibler_decay * (1.0 - area_total)) * land_cells
    )
    inertia = mass_rate * (1.0 + volume_total)
    turning = coriolis * (1.0 + volume_total)
    is_top = lax.axis_index("row") == lax.axis_size("row") - 1

    def exchange_cycle(subcycle, carried):
        velocity, stresses = carried
        west_side, south_side, south_west = neighbour_views(velocity, 1)
        stresses = stress_update(
            stresses,
            strength,
            inverse_width,
            inverse_height,
            velocity,
            west_side,
            south_side,
            south_west,
        )
        east_side, north_side, north_east = neighbour_views(stresses, -1)
        ghost_row = fold_ghost(stresses)
        north_side = north_side.at[:, -1].set(
            jnp.where(is_top, ghost_row[:, :-1], north_side[:, -1])
        )
        north_east = north_east.at[:, -1].set(
            jnp.where(is_top, ghost_row[:, 1:], north_east[:, -1])
        )
        force_x, force_y = stress_force(
            inverse_width, inverse_height, stresses, east_side, north_side, north_east
        )
        velocity = momentum(
            velocity,
            force_x,
            force_y,
            inertia,
            turning,
            wind_stress,
            ocean_current,
            land_cells,
            ice_cells,
        )
        return (velocity, stresses)

    velocity, stresses = lax.fori_loop(0, SUB, exchange_cycle, (velocity_start, stress_start))
    restart = restart_strip(ice_area, ice_volume, writer)
    return (velocity, stresses, restart)


def solution(mesh):
    return jax.shard_map(
        shards,
        mesh=mesh,
        in_specs=(
            P(None, "row", "col"),
            P(None, "row", "col"),
            P(None, "row", "col"),
            P(None, "row", "col"),
            P(None, "row", "col"),
            P(None, "row", "col"),
            P("row", "col"),
            P("row", "col"),
            P("row", "col"),
            P("row", "col"),
            P(),
        ),
        out_specs=(P(None, "row", "col"), P(None, "row", "col"), P("row", None, None, "col")),
        check_vma=False,
    )
```

profile of v0, /device:TPU:6, one launch (start us, length us, event | category | flops | bytes accessed | tf_op | source)
XLA Modules:
  0.0 414.2 jit_solution(4949985804003498587)
XLA Ops:
  16.4 386.9 %while.19 = (s32[]{:T(128)}, f32[2,64,128]{2,1,0:T(8,128)S(1)}, f32[3,64,128]{2,0,1:T(4,128)S(1)}, f32[64,128]{1,0:T(8,128)S(1)}, f32[64,128]{1,0:T(8,128)}, /*i...) while((s32[]{:T(128)}, f32[2,64,128]{2,1,0:T(8,128)S(1)}, ...), condition=%wide.region_3.0_spmd.clone.clone, body=%wide.region_2.3_spmd.clone.clone.sunk | while | flops 1149323 | bytes 6511213 | solution.py:223
  16.6 2.0 collective-permute-start
  20.0 6.5 %collective-permute-done = f32[2,64]{1,0:T(2,128)S(1)} collective-permute-done((f32[2,64]{1,0:T(2,128)S(1)}, f32[2,64]{1,0:T(2,128)S(1)}, u32[]{:S(2)}, u32[]{:S(2)}) %collective-permute-start) | collective-permute-done | bytes 544 | tf_op jit(solution)/shard_map/while/body/eval_jaxpr/ppermute | solution.py:22
  26.7 1.9 collective-permute-start.1
  28.8 3.0 collective-permute-done.1
  35.4 5.0 %all-to-all-start = ((f32[32,3,128]{2,1,0:T(4,128)}), f32[32,3,128]{2,1,0:T(4,128)S(1)}, u32[]{:S(2)}, u32[]{:S(2)}) async-start(f32[32,3,128]{2,1,0:T(4,128)} %broadcast_in_dim.121), calls=%async_computation | async-start | bytes 131072 | tf_op jit(solution)/shard_map/while/body/eval_jaxpr/all_to_all | solution.py:33
  42.7 7.8 %all-to-all-done = f32[32,3,128]{2,1,0:T(4,128)S(1)} async-done(((f32[32,3,128]{2,1,0:T(4,128)}), f32[32,3,128]{2,1,0:T(4,128)S(1)}, u32[]{:S(2)}, u32[]{:S(2)}) %all-to-all-start) | async-done | bytes 49184 | tf_op jit(solution)/shard_map/while/body/eval_jaxpr/all_to_all | solution.py:33
  50.5 2.8 rev.10
  56.7 4.6 %collective-permute-done = f32[2,64]{1,0:T(2,128)S(1)} collective-permute-done((f32[2,64]{1,0:T(2,128)S(1)}, f32[2,64]{1,0:T(2,128)S(1)}, u32[]{:S(2)}, u32[]{:S(2)}) %collective-permute-start) | collective-permute-done | bytes 544 | tf_op jit(solution)/shard_map/while/body/eval_jaxpr/ppermute | solution.py:22
  63.6 2.8 collective-permute-done.1
  68.3 3.9 all-to-all-start
  74.5 7.7 %all-to-all-done = f32[32,3,128]{2,1,0:T(4,128)S(1)} async-done(((f32[32,3,128]{2,1,0:T(4,128)}), f32[32,3,128]{2,1,0:T(4,128)S(1)}, u32[]{:S(2)}, u32[]{:S(2)}) %all-to-all-start) | async-done | bytes 49184 | tf_op jit(solution)/shard_map/while/body/eval_jaxpr/all_to_all | solution.py:33
  82.3 2.8 rev.10
  88.5 4.6 %collective-permute-done = f32[2,64]{1,0:T(2,128)S(1)} collective-permute-done((f32[2,64]{1,0:T(2,128)S(1)}, f32[2,64]{1,0:T(2,128)S(1)}, u32[]{:S(2)}, u32[]{:S(2)}) %collective-permute-start) | collective-permute-done | bytes 544 | tf_op jit(solution)/shard_map/while/body/eval_jaxpr/ppermute | solution.py:22
  95.4 2.8 collective-permute-done.1
  100.0 3.9 all-to-all-start
  106.2 7.7 %all-to-all-done = f32[32,3,128]{2,1,0:T(4,128)S(1)} async-done(((f32[32,3,128]{2,1,0:T(4,128)}), f32[32,3,128]{2,1,0:T(4,128)S(1)}, u32[]{:S(2)}, u32[]{:S(2)}) %all-to-all-start) | async-done | bytes 49184 | tf_op jit(solution)/shard_map/while/body/eval_jaxpr/all_to_all | solution.py:33
  114.0 2.8 rev.10
  120.2 4.6 %collective-permute-done = f32[2,64]{1,0:T(2,128)S(1)} collective-permute-done((f32[2,64]{1,0:T(2,128)S(1)}, f32[2,64]{1,0:T(2,128)S(1)}, u32[]{:S(2)}, u32[]{:S(2)}) %collective-permute-start) | collective-permute-done | bytes 544 | tf_op jit(solution)/shard_map/while/body/eval_jaxpr/ppermute | solution.py:22
  127.1 2.8 collective-permute-done.1
  131.8 3.9 all-to-all-start
  137.9 7.7 %all-to-all-done = f32[32,3,128]{2,1,0:T(4,128)S(1)} async-done(((f32[32,3,128]{2,1,0:T(4,128)}), f32[32,3,128]{2,1,0:T(4,128)S(1)}, u32[]{:S(2)}, u32[]{:S(2)}) %all-to-all-start) | async-done | bytes 49184 | tf_op jit(solution)/shard_map/while/body/eval_jaxpr/all_to_all | solution.py:33
  145.7 2.8 rev.10
  152.0 4.6 %collective-permute-done = f32[2,64]{1,0:T(2,128)S(1)} collective-permute-done((f32[2,64]{1,0:T(2,128)S(1)}, f32[2,64]{1,0:T(2,128)S(1)}, u32[]{:S(2)}, u32[]{:S(2)}) %collective-permute-start) | collective-permute-done | bytes 544 | tf_op jit(solution)/shard_map/while/body/eval_jaxpr/ppermute | solution.py:22
  158.8 2.8 collective-permute-done.1
  163.5 3.9 all-to-all-start
  169.7 7.7 %all-to-all-done = f32[32,3,128]{2,1,0:T(4,128)S(1)} async-done(((f32[32,3,128]{2,1,0:T(4,128)}), f32[32,3,128]{2,1,0:T(4,128)S(1)}, u32[]{:S(2)}, u32[]{:S(2)}) %all-to-all-start) | async-done | bytes 49184 | tf_op jit(solution)/shard_map/while/body/eval_jaxpr/all_to_all | solution.py:33
  177.5 2.8 rev.10
  183.7 4.6 %collective-permute-done = f32[2,64]{1,0:T(2,128)S(1)} collective-permute-done((f32[2,64]{1,0:T(2,128)S(1)}, f32[2,64]{1,0:T(2,128)S(1)}, u32[]{:S(2)}, u32[]{:S(2)}) %collective-permute-start) | collective-permute-done | bytes 544 | tf_op jit(solution)/shard_map/while/body/eval_jaxpr/ppermute | solution.py:22
  190.6 2.8 collective-permute-done.1
  195.2 3.9 all-to-all-start
  201.4 7.7 %all-to-all-done = f32[32,3,128]{2,1,0:T(4,128)S(1)} async-done(((f32[32,3,128]{2,1,0:T(4,128)}), f32[32,3,128]{2,1,0:T(4,128)S(1)}, u32[]{:S(2)}, u32[]{:S(2)}) %all-to-all-start) | async-done | bytes 49184 | tf_op jit(solution)/shard_map/while/body/eval_jaxpr/all_to_all | solution.py:33
  209.2 2.8 rev.10
  215.4 4.6 %collective-permute-done = f32[2,64]{1,0:T(2,128)S(1)} collective-permute-done((f32[2,64]{1,0:T(2,128)S(1)}, f32[2,64]{1,0:T(2,128)S(1)}, u32[]{:S(2)}, u32[]{:S(2)}) %collective-permute-start) | collective-permute-done | bytes 544 | tf_op jit(solution)/shard_map/while/body/eval_jaxpr/ppermute | solution.py:22
  222.3 2.8 collective-permute-done.1
  227.0 3.9 all-to-all-start
  233.1 7.7 %all-to-all-done = f32[32,3,128]{2,1,0:T(4,128)S(1)} async-done(((f32[32,3,128]{2,1,0:T(4,128)}), f32[32,3,128]{2,1,0:T(4,128)S(1)}, u32[]{:S(2)}, u32[]{:S(2)}) %all-to-all-start) | async-done | bytes 49184 | tf_op jit(solution)/shard_map/while/body/eval_jaxpr/all_to_all | solution.py:33
  240.9 2.8 rev.10
  247.2 4.6 %collective-permute-done = f32[2,64]{1,0:T(2,128)S(1)} collective-permute-done((f32[2,64]{1,0:T(2,128)S(1)}, f32[2,64]{1,0:T(2,128)S(1)}, u32[]{:S(2)}, u32[]{:S(2)}) %collective-permute-start) | collective-permute-done | bytes 544 | tf_op jit(solution)/shard_map/while/body/eval_jaxpr/ppermute | solution.py:22
  254.0 2.8 collective-permute-done.1
  258.7 3.9 all-to-all-start
  264.9 7.7 %all-to-all-done = f32[32,3,128]{2,1,0:T(4,128)S(1)} async-done(((f32[32,3,128]{2,1,0:T(4,128)}), f32[32,3,128]{2,1,0:T(4,128)S(1)}, u32[]{:S(2)}, u32[]{:S(2)}) %all-to-all-start) | async-done | bytes 49184 | tf_op jit(solution)/shard_map/while/body/eval_jaxpr/all_to_all | solution.py:33
  272.7 2.8 rev.10
  278.9 4.6 %collective-permute-done = f32[2,64]{1,0:T(2,128)S(1)} collective-permute-done((f32[2,64]{1,0:T(2,128)S(1)}, f32[2,64]{1,0:T(2,128)S(1)}, u32[]{:S(2)}, u32[]{:S(2)}) %collective-permute-start) | collective-permute-done | bytes 544 | tf_op jit(solution)/shard_map/while/body/eval_jaxpr/ppermute | solution.py:22
  285.8 2.8 collective-permute-done.1
  290.4 3.9 all-to-all-start
  296.6 7.7 %all-to-all-done = f32[32,3,128]{2,1,0:T(4,128)S(1)} async-done(((f32[32,3,128]{2,1,0:T(4,128)}), f32[32,3,128]{2,1,0:T(4,128)S(1)}, u32[]{:S(2)}, u32[]{:S(2)}) %all-to-all-start) | async-done | bytes 49184 | tf_op jit(solution)/shard_map/while/body/eval_jaxpr/all_to_all | solution.py:33
  304.4 2.8 rev.10
  310.6 4.6 %collective-permute-done = f32[2,64]{1,0:T(2,128)S(1)} collective-permute-done((f32[2,64]{1,0:T(2,128)S(1)}, f32[2,64]{1,0:T(2,128)S(1)}, u32[]{:S(2)}, u32[]{:S(2)}) %collective-permute-start) | collective-permute-done | bytes 544 | tf_op jit(solution)/shard_map/while/body/eval_jaxpr/ppermute | solution.py:22
  317.5 2.8 collective-permute-done.1
  322.2 3.9 all-to-all-start
  328.3 7.7 %all-to-all-done = f32[32,3,128]{2,1,0:T(4,128)S(1)} async-done(((f32[32,3,128]{2,1,0:T(4,128)}), f32[32,3,128]{2,1,0:T(4,128)S(1)}, u32[]{:S(2)}, u32[]{:S(2)}) %all-to-all-start) | async-done | bytes 49184 | tf_op jit(solution)/shard_map/while/body/eval_jaxpr/all_to_all | solution.py:33
  336.1 2.8 rev.10
  342.4 4.6 %collective-permute-done = f32[2,64]{1,0:T(2,128)S(1)} collective-permute-done((f32[2,64]{1,0:T(2,128)S(1)}, f32[2,64]{1,0:T(2,128)S(1)}, u32[]{:S(2)}, u32[]{:S(2)}) %collective-permute-start) | collective-permute-done | bytes 544 | tf_op jit(solution)/shard_map/while/body/eval_jaxpr/ppermute | solution.py:22
  349.2 2.8 collective-permute-done.1
  353.9 3.9 all-to-all-start
  360.1 7.7 %all-to-all-done = f32[32,3,128]{2,1,0:T(4,128)S(1)} async-done(((f32[32,3,128]{2,1,0:T(4,128)}), f32[32,3,128]{2,1,0:T(4,128)S(1)}, u32[]{:S(2)}, u32[]{:S(2)}) %all-to-all-start) | async-done | bytes 49184 | tf_op jit(solution)/shard_map/while/body/eval_jaxpr/all_to_all | solution.py:33
  367.8 2.8 rev.10
  374.1 4.6 %collective-permute-done = f32[2,64]{1,0:T(2,128)S(1)} collective-permute-done((f32[2,64]{1,0:T(2,128)S(1)}, f32[2,64]{1,0:T(2,128)S(1)}, u32[]{:S(2)}, u32[]{:S(2)}) %collective-permute-start) | collective-permute-done | bytes 544 | tf_op jit(solution)/shard_map/while/body/eval_jaxpr/ppermute | solution.py:22
  381.0 2.8 collective-permute-done.1
  385.6 3.9 all-to-all-start
  391.8 7.7 %all-to-all-done = f32[32,3,128]{2,1,0:T(4,128)S(1)} async-done(((f32[32,3,128]{2,1,0:T(4,128)}), f32[32,3,128]{2,1,0:T(4,128)S(1)}, u32[]{:S(2)}, u32[]{:S(2)}) %all-to-all-start) | async-done | bytes 49184 | tf_op jit(solution)/shard_map/while/body/eval_jaxpr/all_to_all | solution.py:33
  399.6 2.8 rev.10
  403.9 3.4 select_bitcast_fusion
  (701 shorter events, 123.4 us)
Async XLA Ops:
  7.2 396.8 %all-gather.2.cloned.1.call-start = ((), (), s32[]{:S(2)}) async-start(), calls=%async_computation.1 | async-start | bytes 2949120 | tf_op jit(solution)/shard_map/all_gather | solution.py:154
  16.6 9.9 %collective-permute-start = (f32[2,64]{1,0:T(2,128)S(1)}, f32[2,64]{1,0:T(2,128)S(1)}, u32[]{:S(2)}, u32[]{:S(2)}) collective-permute-start(f32[2,64]{1,0:T(2,128)S(1)} %slice_reduce_fusion.2), channel_id=1, source_target_pairs={{0,1},{1,2},{2,3},{3,4},{4,5},{5,6},{6,7},{7,8},{8,9},{9,10},{10,1... | collective-permute-start | bytes 1544 | tf_op jit(solution)/shard_map/while/body/eval_jaxpr/ppermute | solution.py:22
  19.8 34.3 %copy-start.1 = (f32[2,64,128]{2,1,0:T(8,128)S(1)}, f32[2,64,128]{2,1,0:T(8,128)}, u32[]{:S(2)}) copy-start(f32[2,64,128]{2,1,0:T(8,128)} %get-tuple-element.622) | copy-start | bytes 196612 | tf_op jit(solution)/shard_map/while
  19.8 34.3 %copy-start.2 = (f32[64,128]{1,0:T(8,128)S(1)}, f32[64,128]{1,0:T(8,128)}, u32[]{:S(2)}) copy-start(f32[64,128]{1,0:T(8,128)} %get-tuple-element.617) | copy-start | bytes 98308 | tf_op jit(solution)/shard_map/while
  19.8 34.3 %copy-start.3 = (f32[64,128]{1,0:T(8,128)S(1)}, f32[64,128]{1,0:T(8,128)}, u32[]{:S(2)}) copy-start(f32[64,128]{1,0:T(8,128)} %get-tuple-element.619) | copy-start | bytes 98308 | tf_op jit(solution)/shard_map/while
  26.7 5.1 %collective-permute-start.1 = (f32[4,128]{1,0:T(4,128)S(1)}, f32[4,128]{1,0:T(4,128)S(1)}, u32[]{:S(2)}, u32[]{:S(2)}) collective-permute-start(f32[4,128]{1,0:T(4,128)S(1)} %pad_maximum_fusion.15), channel_id=1, source_target_pairs={{0,32},{32,64},{64,96},{96,128},{128,160},{160,192},{192,224},{1,3... | collective-permute-start | bytes 6152 | tf_op jit(solution)/shard_map/while/body/eval_jaxpr/ppermute | solution.py:28
  32.7 7.7 %collective-permute-start.2 = (f32[3,64]{1,0:T(4,128)S(1)}, f32[3,64]{1,0:T(4,128)S(1)}, u32[]{:S(2)}, u32[]{:S(2)}) collective-permute-start(f32[3,64]{1,0:T(4,128)S(1)} %bitcast.186), channel_id=1, source_target_pairs={{0,31},{1,0},{2,1},{3,2},{4,3},{5,4},{6,5},{7,6},{8,7},{9,8},{10,9... | collective-permute-start | bytes 2312 | tf_op jit(solution)/shard_map/while/body/eval_jaxpr/ppermute | solution.py:22
  35.4 15.0 %all-to-all-start = ((f32[32,3,128]{2,1,0:T(4,128)}), f32[32,3,128]{2,1,0:T(4,128)S(1)}, u32[]{:S(2)}, u32[]{:S(2)}) async-start(f32[32,3,128]{2,1,0:T(4,128)} %broadcast_in_dim.121), calls=%async_computation | async-start | bytes 131072 | tf_op jit(solution)/shard_map/while/body/eval_jaxpr/all_to_all | solution.py:33
  40.6 12.8 %collective-permute-start.3 = (f32[6,128]{1,0:T(8,128)S(1)}, f32[6,128]{1,0:T(8,128)S(1)}, u32[]{:S(2)}, u32[]{:S(2)}) collective-permute-start(f32[6,128]{1,0:T(8,128)S(1)} %pad_maximum_fusion.17), channel_id=1, source_target_pairs={{32,0},{64,32},{96,64},{128,96},{160,128},{192,160},{224,192},{33,... | collective-permute-start | bytes 9224 | tf_op jit(solution)/shard_map/while/body/eval_jaxpr/ppermute | solution.py:28
  54.4 7.0 %collective-permute-start = (f32[2,64]{1,0:T(2,128)S(1)}, f32[2,64]{1,0:T(2,128)S(1)}, u32[]{:S(2)}, u32[]{:S(2)}) collective-permute-start(f32[2,64]{1,0:T(2,128)S(1)} %slice_reduce_fusion.2), channel_id=1, source_target_pairs={{0,1},{1,2},{2,3},{3,4},{4,5},{5,6},{6,7},{7,8},{8,9},{9,10},{10,1... | collective-permute-start | bytes 1544 | tf_op jit(solution)/shard_map/while/body/eval_jaxpr/ppermute | solution.py:22
  61.6 4.9 %collective-permute-start.1 = (f32[4,128]{1,0:T(4,128)S(1)}, f32[4,128]{1,0:T(4,128)S(1)}, u32[]{:S(2)}, u32[]{:S(2)}) collective-permute-start(f32[4,128]{1,0:T(4,128)S(1)} %pad_maximum_fusion.15), channel_id=1, source_target_pairs={{0,32},{32,64},{64,96},{96,128},{128,160},{160,192},{192,224},{1,3... | collective-permute-start | bytes 6152 | tf_op jit(solution)/shard_map/while/body/eval_jaxpr/ppermute | solution.py:28
  67.4 4.7 %collective-permute-start.2 = (f32[3,64]{1,0:T(4,128)S(1)}, f32[3,64]{1,0:T(4,128)S(1)}, u32[]{:S(2)}, u32[]{:S(2)}) collective-permute-start(f32[3,64]{1,0:T(4,128)S(1)} %bitcast.186), channel_id=1, source_target_pairs={{0,31},{1,0},{2,1},{3,2},{4,3},{5,4},{6,5},{7,6},{8,7},{9,8},{10,9... | collective-permute-start | bytes 2312 | tf_op jit(solution)/shard_map/while/body/eval_jaxpr/ppermute | solution.py:22
  68.3 13.9 %all-to-all-start = ((f32[32,3,128]{2,1,0:T(4,128)}), f32[32,3,128]{2,1,0:T(4,128)S(1)}, u32[]{:S(2)}, u32[]{:S(2)}) async-start(f32[32,3,128]{2,1,0:T(4,128)} %broadcast_in_dim.121), calls=%async_computation | async-start | bytes 131072 | tf_op jit(solution)/shard_map/while/body/eval_jaxpr/all_to_all | solution.py:33
  72.4 12.7 %collective-permute-start.3 = (f32[6,128]{1,0:T(8,128)S(1)}, f32[6,128]{1,0:T(8,128)S(1)}, u32[]{:S(2)}, u32[]{:S(2)}) collective-permute-start(f32[6,128]{1,0:T(8,128)S(1)} %pad_maximum_fusion.17), channel_id=1, source_target_pairs={{32,0},{64,32},{96,64},{128,96},{160,128},{192,160},{224,192},{33,... | collective-permute-start | bytes 9224 | tf_op jit(solution)/shard_map/while/body/eval_jaxpr/ppermute | solution.py:28
  86.1 7.0 %collective-permute-start = (f32[2,64]{1,0:T(2,128)S(1)}, f32[2,64]{1,0:T(2,128)S(1)}, u32[]{:S(2)}, u32[]{:S(2)}) collective-permute-start(f32[2,64]{1,0:T(2,128)S(1)} %slice_reduce_fusion.2), channel_id=1, source_target_pairs={{0,1},{1,2},{2,3},{3,4},{4,5},{5,6},{6,7},{7,8},{8,9},{9,10},{10,1... | collective-permute-start | bytes 1544 | tf_op jit(solution)/shard_map/while/body/eval_jaxpr/ppermute | solution.py:22
  93.3 4.9 %collective-permute-start.1 = (f32[4,128]{1,0:T(4,128)S(1)}, f32[4,128]{1,0:T(4,128)S(1)}, u32[]{:S(2)}, u32[]{:S(2)}) collective-permute-start(f32[4,128]{1,0:T(4,128)S(1)} %pad_maximum_fusion.15), channel_id=1, source_target_pairs={{0,32},{32,64},{64,96},{96,128},{128,160},{160,192},{192,224},{1,3... | collective-permute-start | bytes 6152 | tf_op jit(solution)/shard_map/while/body/eval_jaxpr/ppermute | solution.py:28
  99.2 4.7 %collective-permute-start.2 = (f32[3,64]{1,0:T(4,128)S(1)}, f32[3,64]{1,0:T(4,128)S(1)}, u32[]{:S(2)}, u32[]{:S(2)}) collective-permute-start(f32[3,64]{1,0:T(4,128)S(1)} %bitcast.186), channel_id=1, source_target_pairs={{0,31},{1,0},{2,1},{3,2},{4,3},{5,4},{6,5},{7,6},{8,7},{9,8},{10,9... | collective-permute-start | bytes 2312 | tf_op jit(solution)/shard_map/while/body/eval_jaxpr/ppermute | solution.py:22
  100.0 13.9 %all-to-all-start = ((f32[32,3,128]{2,1,0:T(4,128)}), f32[32,3,128]{2,1,0:T(4,128)S(1)}, u32[]{:S(2)}, u32[]{:S(2)}) async-start(f32[32,3,128]{2,1,0:T(4,128)} %broadcast_in_dim.121), calls=%async_computation | async-start | bytes 131072 | tf_op jit(solution)/shard_map/while/body/eval_jaxpr/all_to_all | solution.py:33
  104.1 12.7 %collective-permute-start.3 = (f32[6,128]{1,0:T(8,128)S(1)}, f32[6,128]{1,0:T(8,128)S(1)}, u32[]{:S(2)}, u32[]{:S(2)}) collective-permute-start(f32[6,128]{1,0:T(8,128)S(1)} %pad_maximum_fusion.17), channel_id=1, source_target_pairs={{32,0},{64,32},{96,64},{128,96},{160,128},{192,160},{224,192},{33,... | collective-permute-start | bytes 9224 | tf_op jit(solution)/shard_map/while/body/eval_jaxpr/ppermute | solution.py:28
  117.9 7.0 %collective-permute-start = (f32[2,64]{1,0:T(2,128)S(1)}, f32[2,64]{1,0:T(2,128)S(1)}, u32[]{:S(2)}, u32[]{:S(2)}) collective-permute-start(f32[2,64]{1,0:T(2,128)S(1)} %slice_reduce_fusion.2), channel_id=1, source_target_pairs={{0,1},{1,2},{2,3},{3,4},{4,5},{5,6},{6,7},{7,8},{8,9},{9,10},{10,1... | collective-permute-start | bytes 1544 | tf_op jit(solution)/shard_map/while/body/eval_jaxpr/ppermute | solution.py:22
  125.0 4.9 %collective-permute-start.1 = (f32[4,128]{1,0:T(4,128)S(1)}, f32[4,128]{1,0:T(4,128)S(1)}, u32[]{:S(2)}, u32[]{:S(2)}) collective-permute-start(f32[4,128]{1,0:T(4,128)S(1)} %pad_maximum_fusion.15), channel_id=1, source_target_pairs={{0,32},{32,64},{64,96},{96,128},{128,160},{160,192},{192,224},{1,3... | collective-permute-start | bytes 6152 | tf_op jit(solution)/shard_map/while/body/eval_jaxpr/ppermute | solution.py:28
  130.9 4.7 %collective-permute-start.2 = (f32[3,64]{1,0:T(4,128)S(1)}, f32[3,64]{1,0:T(4,128)S(1)}, u32[]{:S(2)}, u32[]{:S(2)}) collective-permute-start(f32[3,64]{1,0:T(4,128)S(1)} %bitcast.186), channel_id=1, source_target_pairs={{0,31},{1,0},{2,1},{3,2},{4,3},{5,4},{6,5},{7,6},{8,7},{9,8},{10,9... | collective-permute-start | bytes 2312 | tf_op jit(solution)/shard_map/while/body/eval_jaxpr/ppermute | solution.py:22
  131.8 13.9 %all-to-all-start = ((f32[32,3,128]{2,1,0:T(4,128)}), f32[32,3,128]{2,1,0:T(4,128)S(1)}, u32[]{:S(2)}, u32[]{:S(2)}) async-start(f32[32,3,128]{2,1,0:T(4,128)} %broadcast_in_dim.121), calls=%async_computation | async-start | bytes 131072 | tf_op jit(solution)/shard_map/while/body/eval_jaxpr/all_to_all | solution.py:33
  135.9 12.7 %collective-permute-start.3 = (f32[6,128]{1,0:T(8,128)S(1)}, f32[6,128]{1,0:T(8,128)S(1)}, u32[]{:S(2)}, u32[]{:S(2)}) collective-permute-start(f32[6,128]{1,0:T(8,128)S(1)} %pad_maximum_fusion.17), channel_id=1, source_target_pairs={{32,0},{64,32},{96,64},{128,96},{160,128},{192,160},{224,192},{33,... | collective-permute-start | bytes 9224 | tf_op jit(solution)/shard_map/while/body/eval_jaxpr/ppermute | solution.py:28
  149.6 7.0 %collective-permute-start = (f32[2,64]{1,0:T(2,128)S(1)}, f32[2,64]{1,0:T(2,128)S(1)}, u32[]{:S(2)}, u32[]{:S(2)}) collective-permute-start(f32[2,64]{1,0:T(2,128)S(1)} %slice_reduce_fusion.2), channel_id=1, source_target_pairs={{0,1},{1,2},{2,3},{3,4},{4,5},{5,6},{6,7},{7,8},{8,9},{9,10},{10,1... | collective-permute-start | bytes 1544 | tf_op jit(solution)/shard_map/while/body/eval_jaxpr/ppermute | solution.py:22
  156.8 4.9 %collective-permute-start.1 = (f32[4,128]{1,0:T(4,128)S(1)}, f32[4,128]{1,0:T(4,128)S(1)}, u32[]{:S(2)}, u32[]{:S(2)}) collective-permute-start(f32[4,128]{1,0:T(4,128)S(1)} %pad_maximum_fusion.15), channel_id=1, source_target_pairs={{0,32},{32,64},{64,96},{96,128},{128,160},{160,192},{192,224},{1,3... | collective-permute-start | bytes 6152 | tf_op jit(solution)/shard_map/while/body/eval_jaxpr/ppermute | solution.py:28
  162.6 4.7 %collective-permute-start.2 = (f32[3,64]{1,0:T(4,128)S(1)}, f32[3,64]{1,0:T(4,128)S(1)}, u32[]{:S(2)}, u32[]{:S(2)}) collective-permute-start(f32[3,64]{1,0:T(4,128)S(1)} %bitcast.186), channel_id=1, source_target_pairs={{0,31},{1,0},{2,1},{3,2},{4,3},{5,4},{6,5},{7,6},{8,7},{9,8},{10,9... | collective-permute-start | bytes 2312 | tf_op jit(solution)/shard_map/while/body/eval_jaxpr/ppermute | solution.py:22
  163.5 13.9 %all-to-all-start = ((f32[32,3,128]{2,1,0:T(4,128)}), f32[32,3,128]{2,1,0:T(4,128)S(1)}, u32[]{:S(2)}, u32[]{:S(2)}) async-start(f32[32,3,128]{2,1,0:T(4,128)} %broadcast_in_dim.121), calls=%async_computation | async-start | bytes 131072 | tf_op jit(solution)/shard_map/while/body/eval_jaxpr/all_to_all | solution.py:33
  167.6 12.7 %collective-permute-start.3 = (f32[6,128]{1,0:T(8,128)S(1)}, f32[6,128]{1,0:T(8,128)S(1)}, u32[]{:S(2)}, u32[]{:S(2)}) collective-permute-start(f32[6,128]{1,0:T(8,128)S(1)} %pad_maximum_fusion.17), channel_id=1, source_target_pairs={{32,0},{64,32},{96,64},{128,96},{160,128},{192,160},{224,192},{33,... | collective-permute-start | bytes 9224 | tf_op jit(solution)/shard_map/while/body/eval_jaxpr/ppermute | solution.py:28
  181.3 7.0 %collective-permute-start = (f32[2,64]{1,0:T(2,128)S(1)}, f32[2,64]{1,0:T(2,128)S(1)}, u32[]{:S(2)}, u32[]{:S(2)}) collective-permute-start(f32[2,64]{1,0:T(2,128)S(1)} %slice_reduce_fusion.2), channel_id=1, source_target_pairs={{0,1},{1,2},{2,3},{3,4},{4,5},{5,6},{6,7},{7,8},{8,9},{9,10},{10,1... | collective-permute-start | bytes 1544 | tf_op jit(solution)/shard_map/while/body/eval_jaxpr/ppermute | solution.py:22
  188.5 4.9 %collective-permute-start.1 = (f32[4,128]{1,0:T(4,128)S(1)}, f32[4,128]{1,0:T(4,128)S(1)}, u32[]{:S(2)}, u32[]{:S(2)}) collective-permute-start(f32[4,128]{1,0:T(4,128)S(1)} %pad_maximum_fusion.15), channel_id=1, source_target_pairs={{0,32},{32,64},{64,96},{96,128},{128,160},{160,192},{192,224},{1,3... | collective-permute-start | bytes 6152 | tf_op jit(solution)/shard_map/while/body/eval_jaxpr/ppermute | solution.py:28
  194.4 4.7 %collective-permute-start.2 = (f32[3,64]{1,0:T(4,128)S(1)}, f32[3,64]{1,0:T(4,128)S(1)}, u32[]{:S(2)}, u32[]{:S(2)}) collective-permute-start(f32[3,64]{1,0:T(4,128)S(1)} %bitcast.186), channel_id=1, source_target_pairs={{0,31},{1,0},{2,1},{3,2},{4,3},{5,4},{6,5},{7,6},{8,7},{9,8},{10,9... | collective-permute-start | bytes 2312 | tf_op jit(solution)/shard_map/while/body/eval_jaxpr/ppermute | solution.py:22
  195.2 13.9 %all-to-all-start = ((f32[32,3,128]{2,1,0:T(4,128)}), f32[32,3,128]{2,1,0:T(4,128)S(1)}, u32[]{:S(2)}, u32[]{:S(2)}) async-start(f32[32,3,128]{2,1,0:T(4,128)} %broadcast_in_dim.121), calls=%async_computation | async-start | bytes 131072 | tf_op jit(solution)/shard_map/while/body/eval_jaxpr/all_to_all | solution.py:33
  199.3 12.7 %collective-permute-start.3 = (f32[6,128]{1,0:T(8,128)S(1)}, f32[6,128]{1,0:T(8,128)S(1)}, u32[]{:S(2)}, u32[]{:S(2)}) collective-permute-start(f32[6,128]{1,0:T(8,128)S(1)} %pad_maximum_fusion.17), channel_id=1, source_target_pairs={{32,0},{64,32},{96,64},{128,96},{160,128},{192,160},{224,192},{33,... | collective-permute-start | bytes 9224 | tf_op jit(solution)/shard_map/while/body/eval_jaxpr/ppermute | solution.py:28
  213.1 7.0 %collective-permute-start = (f32[2,64]{1,0:T(2,128)S(1)}, f32[2,64]{1,0:T(2,128)S(1)}, u32[]{:S(2)}, u32[]{:S(2)}) collective-permute-start(f32[2,64]{1,0:T(2,128)S(1)} %slice_reduce_fusion.2), channel_id=1, source_target_pairs={{0,1},{1,2},{2,3},{3,4},{4,5},{5,6},{6,7},{7,8},{8,9},{9,10},{10,1... | collective-permute-start | bytes 1544 | tf_op jit(solution)/shard_map/while/body/eval_jaxpr/ppermute | solution.py:22
  220.2 4.9 %collective-permute-start.1 = (f32[4,128]{1,0:T(4,128)S(1)}, f32[4,128]{1,0:T(4,128)S(1)}, u32[]{:S(2)}, u32[]{:S(2)}) collective-permute-start(f32[4,128]{1,0:T(4,128)S(1)} %pad_maximum_fusion.15), channel_id=1, source_target_pairs={{0,32},{32,64},{64,96},{96,128},{128,160},{160,192},{192,224},{1,3... | collective-permute-start | bytes 6152 | tf_op jit(solution)/shard_map/while/body/eval_jaxpr/ppermute | solution.py:28
  226.1 4.7 %collective-permute-start.2 = (f32[3,64]{1,0:T(4,128)S(1)}, f32[3,64]{1,0:T(4,128)S(1)}, u32[]{:S(2)}, u32[]{:S(2)}) collective-permute-start(f32[3,64]{1,0:T(4,128)S(1)} %bitcast.186), channel_id=1, source_target_pairs={{0,31},{1,0},{2,1},{3,2},{4,3},{5,4},{6,5},{7,6},{8,7},{9,8},{10,9... | collective-permute-start | bytes 2312 | tf_op jit(solution)/shard_map/while/body/eval_jaxpr/ppermute | solution.py:22
  227.0 13.9 %all-to-all-start = ((f32[32,3,128]{2,1,0:T(4,128)}), f32[32,3,128]{2,1,0:T(4,128)S(1)}, u32[]{:S(2)}, u32[]{:S(2)}) async-start(f32[32,3,128]{2,1,0:T(4,128)} %broadcast_in_dim.121), calls=%async_computation | async-start | bytes 131072 | tf_op jit(solution)/shard_map/while/body/eval_jaxpr/all_to_all | solution.py:33
  231.1 12.7 %collective-permute-start.3 = (f32[6,128]{1,0:T(8,128)S(1)}, f32[6,128]{1,0:T(8,128)S(1)}, u32[]{:S(2)}, u32[]{:S(2)}) collective-permute-start(f32[6,128]{1,0:T(8,128)S(1)} %pad_maximum_fusion.17), channel_id=1, source_target_pairs={{32,0},{64,32},{96,64},{128,96},{160,128},{192,160},{224,192},{33,... | collective-permute-start | bytes 9224 | tf_op jit(solution)/shard_map/while/body/eval_jaxpr/ppermute | solution.py:28
  244.8 7.0 %collective-permute-start = (f32[2,64]{1,0:T(2,128)S(1)}, f32[2,64]{1,0:T(2,128)S(1)}, u32[]{:S(2)}, u32[]{:S(2)}) collective-permute-start(f32[2,64]{1,0:T(2,128)S(1)} %slice_reduce_fusion.2), channel_id=1, source_target_pairs={{0,1},{1,2},{2,3},{3,4},{4,5},{5,6},{6,7},{7,8},{8,9},{9,10},{10,1... | collective-permute-start | bytes 1544 | tf_op jit(solution)/shard_map/while/body/eval_jaxpr/ppermute | solution.py:22
  252.0 4.9 %collective-permute-start.1 = (f32[4,128]{1,0:T(4,128)S(1)}, f32[4,128]{1,0:T(4,128)S(1)}, u32[]{:S(2)}, u32[]{:S(2)}) collective-permute-start(f32[4,128]{1,0:T(4,128)S(1)} %pad_maximum_fusion.15), channel_id=1, source_target_pairs={{0,32},{32,64},{64,96},{96,128},{128,160},{160,192},{192,224},{1,3... | collective-permute-start | bytes 6152 | tf_op jit(solution)/shard_map/while/body/eval_jaxpr/ppermute | solution.py:28
  257.8 4.7 %collective-permute-start.2 = (f32[3,64]{1,0:T(4,128)S(1)}, f32[3,64]{1,0:T(4,128)S(1)}, u32[]{:S(2)}, u32[]{:S(2)}) collective-permute-start(f32[3,64]{1,0:T(4,128)S(1)} %bitcast.186), channel_id=1, source_target_pairs={{0,31},{1,0},{2,1},{3,2},{4,3},{5,4},{6,5},{7,6},{8,7},{9,8},{10,9... | collective-permute-start | bytes 2312 | tf_op jit(solution)/shard_map/while/body/eval_jaxpr/ppermute | solution.py:22
  258.7 13.9 %all-to-all-start = ((f32[32,3,128]{2,1,0:T(4,128)}), f32[32,3,128]{2,1,0:T(4,128)S(1)}, u32[]{:S(2)}, u32[]{:S(2)}) async-start(f32[32,3,128]{2,1,0:T(4,128)} %broadcast_in_dim.121), calls=%async_computation | async-start | bytes 131072 | tf_op jit(solution)/shard_map/while/body/eval_jaxpr/all_to_all | solution.py:33
  262.8 12.7 %collective-permute-start.3 = (f32[6,128]{1,0:T(8,128)S(1)}, f32[6,128]{1,0:T(8,128)S(1)}, u32[]{:S(2)}, u32[]{:S(2)}) collective-permute-start(f32[6,128]{1,0:T(8,128)S(1)} %pad_maximum_fusion.17), channel_id=1, source_target_pairs={{32,0},{64,32},{96,64},{128,96},{160,128},{192,160},{224,192},{33,... | collective-permute-start | bytes 9224 | tf_op jit(solution)/shard_map/while/body/eval_jaxpr/ppermute | solution.py:28
  276.5 7.0 %collective-permute-start = (f32[2,64]{1,0:T(2,128)S(1)}, f32[2,64]{1,0:T(2,128)S(1)}, u32[]{:S(2)}, u32[]{:S(2)}) collective-permute-start(f32[2,64]{1,0:T(2,128)S(1)} %slice_reduce_fusion.2), channel_id=1, source_target_pairs={{0,1},{1,2},{2,3},{3,4},{4,5},{5,6},{6,7},{7,8},{8,9},{9,10},{10,1... | collective-permute-start | bytes 1544 | tf_op jit(solution)/shard_map/while/body/eval_jaxpr/ppermute | solution.py:22
  283.7 4.9 %collective-permute-start.1 = (f32[4,128]{1,0:T(4,128)S(1)}, f32[4,128]{1,0:T(4,128)S(1)}, u32[]{:S(2)}, u32[]{:S(2)}) collective-permute-start(f32[4,128]{1,0:T(4,128)S(1)} %pad_maximum_fusion.15), channel_id=1, source_target_pairs={{0,32},{32,64},{64,96},{96,128},{128,160},{160,192},{192,224},{1,3... | collective-permute-start | bytes 6152 | tf_op jit(solution)/shard_map/while/body/eval_jaxpr/ppermute | solution.py:28
  289.6 4.7 %collective-permute-start.2 = (f32[3,64]{1,0:T(4,128)S(1)}, f32[3,64]{1,0:T(4,128)S(1)}, u32[]{:S(2)}, u32[]{:S(2)}) collective-permute-start(f32[3,64]{1,0:T(4,128)S(1)} %bitcast.186), channel_id=1, source_target_pairs={{0,31},{1,0},{2,1},{3,2},{4,3},{5,4},{6,5},{7,6},{8,7},{9,8},{10,9... | collective-permute-start | bytes 2312 | tf_op jit(solution)/shard_map/while/body/eval_jaxpr/ppermute | solution.py:22
  290.4 13.9 %all-to-all-start = ((f32[32,3,128]{2,1,0:T(4,128)}), f32[32,3,128]{2,1,0:T(4,128)S(1)}, u32[]{:S(2)}, u32[]{:S(2)}) async-start(f32[32,3,128]{2,1,0:T(4,128)} %broadcast_in_dim.121), calls=%async_computation | async-start | bytes 131072 | tf_op jit(solution)/shard_map/while/body/eval_jaxpr/all_to_all | solution.py:33
  294.5 12.7 %collective-permute-start.3 = (f32[6,128]{1,0:T(8,128)S(1)}, f32[6,128]{1,0:T(8,128)S(1)}, u32[]{:S(2)}, u32[]{:S(2)}) collective-permute-start(f32[6,128]{1,0:T(8,128)S(1)} %pad_maximum_fusion.17), channel_id=1, source_target_pairs={{32,0},{64,32},{96,64},{128,96},{160,128},{192,160},{224,192},{33,... | collective-permute-start | bytes 9224 | tf_op jit(solution)/shard_map/while/body/eval_jaxpr/ppermute | solution.py:28
  308.3 7.0 %collective-permute-start = (f32[2,64]{1,0:T(2,128)S(1)}, f32[2,64]{1,0:T(2,128)S(1)}, u32[]{:S(2)}, u32[]{:S(2)}) collective-permute-start(f32[2,64]{1,0:T(2,128)S(1)} %slice_reduce_fusion.2), channel_id=1, source_target_pairs={{0,1},{1,2},{2,3},{3,4},{4,5},{5,6},{6,7},{7,8},{8,9},{9,10},{10,1... | collective-permute-start | bytes 1544 | tf_op jit(solution)/shard_map/while/body/eval_jaxpr/ppermute | solution.py:22
  315.4 4.9 %collective-permute-start.1 = (f32[4,128]{1,0:T(4,128)S(1)}, f32[4,128]{1,0:T(4,128)S(1)}, u32[]{:S(2)}, u32[]{:S(2)}) collective-permute-start(f32[4,128]{1,0:T(4,128)S(1)} %pad_maximum_fusion.15), channel_id=1, source_target_pairs={{0,32},{32,64},{64,96},{96,128},{128,160},{160,192},{192,224},{1,3... | collective-permute-start | bytes 6152 | tf_op jit(solution)/shard_map/while/body/eval_jaxpr/ppermute | solution.py:28
  321.3 4.7 %collective-permute-start.2 = (f32[3,64]{1,0:T(4,128)S(1)}, f32[3,64]{1,0:T(4,128)S(1)}, u32[]{:S(2)}, u32[]{:S(2)}) collective-permute-start(f32[3,64]{1,0:T(4,128)S(1)} %bitcast.186), channel_id=1, source_target_pairs={{0,31},{1,0},{2,1},{3,2},{4,3},{5,4},{6,5},{7,6},{8,7},{9,8},{10,9... | collective-permute-start | bytes 2312 | tf_op jit(solution)/shard_map/while/body/eval_jaxpr/ppermute | solution.py:22
  322.2 13.9 %all-to-all-start = ((f32[32,3,128]{2,1,0:T(4,128)}), f32[32,3,128]{2,1,0:T(4,128)S(1)}, u32[]{:S(2)}, u32[]{:S(2)}) async-start(f32[32,3,128]{2,1,0:T(4,128)} %broadcast_in_dim.121), calls=%async_computation | async-start | bytes 131072 | tf_op jit(solution)/shard_map/while/body/eval_jaxpr/all_to_all | solution.py:33
  326.3 12.7 %collective-permute-start.3 = (f32[6,128]{1,0:T(8,128)S(1)}, f32[6,128]{1,0:T(8,128)S(1)}, u32[]{:S(2)}, u32[]{:S(2)}) collective-permute-start(f32[6,128]{1,0:T(8,128)S(1)} %pad_maximum_fusion.17), channel_id=1, source_target_pairs={{32,0},{64,32},{96,64},{128,96},{160,128},{192,160},{224,192},{33,... | collective-permute-start | bytes 9224 | tf_op jit(solution)/shard_map/while/body/eval_jaxpr/ppermute | solution.py:28
  340.0 7.0 %collective-permute-start = (f32[2,64]{1,0:T(2,128)S(1)}, f32[2,64]{1,0:T(2,128)S(1)}, u32[]{:S(2)}, u32[]{:S(2)}) collective-permute-start(f32[2,64]{1,0:T(2,128)S(1)} %slice_reduce_fusion.2), channel_id=1, source_target_pairs={{0,1},{1,2},{2,3},{3,4},{4,5},{5,6},{6,7},{7,8},{8,9},{9,10},{10,1... | collective-permute-start | bytes 1544 | tf_op jit(solution)/shard_map/while/body/eval_jaxpr/ppermute | solution.py:22
  347.2 4.9 %collective-permute-start.1 = (f32[4,128]{1,0:T(4,128)S(1)}, f32[4,128]{1,0:T(4,128)S(1)}, u32[]{:S(2)}, u32[]{:S(2)}) collective-permute-start(f32[4,128]{1,0:T(4,128)S(1)} %pad_maximum_fusion.15), channel_id=1, source_target_pairs={{0,32},{32,64},{64,96},{96,128},{128,160},{160,192},{192,224},{1,3... | collective-permute-start | bytes 6152 | tf_op jit(solution)/shard_map/while/body/eval_jaxpr/ppermute | solution.py:28
  353.0 4.7 %collective-permute-start.2 = (f32[3,64]{1,0:T(4,128)S(1)}, f32[3,64]{1,0:T(4,128)S(1)}, u32[]{:S(2)}, u32[]{:S(2)}) collective-permute-start(f32[3,64]{1,0:T(4,128)S(1)} %bitcast.186), channel_id=1, source_target_pairs={{0,31},{1,0},{2,1},{3,2},{4,3},{5,4},{6,5},{7,6},{8,7},{9,8},{10,9... | collective-permute-start | bytes 2312 | tf_op jit(solution)/shard_map/while/body/eval_jaxpr/ppermute | solution.py:22
  353.9 13.9 %all-to-all-start = ((f32[32,3,128]{2,1,0:T(4,128)}), f32[32,3,128]{2,1,0:T(4,128)S(1)}, u32[]{:S(2)}, u32[]{:S(2)}) async-start(f32[32,3,128]{2,1,0:T(4,128)} %broadcast_in_dim.121), calls=%async_computation | async-start | bytes 131072 | tf_op jit(solution)/shard_map/while/body/eval_jaxpr/all_to_all | solution.py:33
  358.0 12.7 %collective-permute-start.3 = (f32[6,128]{1,0:T(8,128)S(1)}, f32[6,128]{1,0:T(8,128)S(1)}, u32[]{:S(2)}, u32[]{:S(2)}) collective-permute-start(f32[6,128]{1,0:T(8,128)S(1)} %pad_maximum_fusion.17), channel_id=1, source_target_pairs={{32,0},{64,32},{96,64},{128,96},{160,128},{192,160},{224,192},{33,... | collective-permute-start | bytes 9224 | tf_op jit(solution)/shard_map/while/body/eval_jaxpr/ppermute | solution.py:28
  371.7 7.0 %collective-permute-start = (f32[2,64]{1,0:T(2,128)S(1)}, f32[2,64]{1,0:T(2,128)S(1)}, u32[]{:S(2)}, u32[]{:S(2)}) collective-permute-start(f32[2,64]{1,0:T(2,128)S(1)} %slice_reduce_fusion.2), channel_id=1, source_target_pairs={{0,1},{1,2},{2,3},{3,4},{4,5},{5,6},{6,7},{7,8},{8,9},{9,10},{10,1... | collective-permute-start | bytes 1544 | tf_op jit(solution)/shard_map/while/body/eval_jaxpr/ppermute | solution.py:22
  378.9 4.9 %collective-permute-start.1 = (f32[4,128]{1,0:T(4,128)S(1)}, f32[4,128]{1,0:T(4,128)S(1)}, u32[]{:S(2)}, u32[]{:S(2)}) collective-permute-start(f32[4,128]{1,0:T(4,128)S(1)} %pad_maximum_fusion.15), channel_id=1, source_target_pairs={{0,32},{32,64},{64,96},{96,128},{128,160},{160,192},{192,224},{1,3... | collective-permute-start | bytes 6152 | tf_op jit(solution)/shard_map/while/body/eval_jaxpr/ppermute | solution.py:28
  384.8 4.7 %collective-permute-start.2 = (f32[3,64]{1,0:T(4,128)S(1)}, f32[3,64]{1,0:T(4,128)S(1)}, u32[]{:S(2)}, u32[]{:S(2)}) collective-permute-start(f32[3,64]{1,0:T(4,128)S(1)} %bitcast.186), channel_id=1, source_target_pairs={{0,31},{1,0},{2,1},{3,2},{4,3},{5,4},{6,5},{7,6},{8,7},{9,8},{10,9... | collective-permute-start | bytes 2312 | tf_op jit(solution)/shard_map/while/body/eval_jaxpr/ppermute | solution.py:22
  385.6 13.9 %all-to-all-start = ((f32[32,3,128]{2,1,0:T(4,128)}), f32[32,3,128]{2,1,0:T(4,128)S(1)}, u32[]{:S(2)}, u32[]{:S(2)}) async-start(f32[32,3,128]{2,1,0:T(4,128)} %broadcast_in_dim.121), calls=%async_computation | async-start | bytes 131072 | tf_op jit(solution)/shard_map/while/body/eval_jaxpr/all_to_all | solution.py:33
  389.7 12.7 %collective-permute-start.3 = (f32[6,128]{1,0:T(8,128)S(1)}, f32[6,128]{1,0:T(8,128)S(1)}, u32[]{:S(2)}, u32[]{:S(2)}) collective-permute-start(f32[6,128]{1,0:T(8,128)S(1)} %pad_maximum_fusion.17), channel_id=1, source_target_pairs={{32,0},{64,32},{96,64},{128,96},{160,128},{192,160},{224,192},{33,... | collective-permute-start | bytes 9224 | tf_op jit(solution)/shard_map/while/body/eval_jaxpr/ppermute | solution.py:28
  (46 other events, 1322.7 us)
Sparse Core Ops, SparseCore 0:
  10.4 30.6 all-gather.1
where the time goes:
time: 417 us; the launch traced here: 414 us
  waiting for transfers between devices  184 us (44%)
  starting transfers between devices  108 us (26%)
  local copies, waits for them, and re-layouts  60.6 us (15%)
  other arithmetic  42.9 us (10%)
  between operations  14.7 us (4%)
    all_to_all x12, waiting for transfers between devices, sent_to_all(): lax.all_to_all(jnp.broadcast_to(value[None], (count, *value.shape)), axis...  92.6 us
    ppermute x24, waiting for transfers between devices, shifted(): return lax.ppermute(value, axis, pairs)  57.1 us
    all_to_all x12, starting transfers between devices, sent_to_all(): lax.all_to_all(jnp.broadcast_to(value[None], (count, *value.shape)), axis...  47.4 us
    ppermute x24, starting transfers between devices, from_behind(): return lax.ppermute(value, axis, pairs)  45.9 us
    ppermute x24, waiting for transfers between devices, from_behind(): return lax.ppermute(value, axis, pairs)  34.2 us
    rev x12, local copies, waits for them, and re-layouts, fold_ghost(): turned = whole_row[:, ::-1]  33.4 us
    ppermute x24, starting transfers between devices, shifted(): return lax.ppermute(value, axis, pairs)  14.7 us
    mul x12, other arithmetic, stress_update(): 0.5 * along_scale  9.4 us
  transfers between devices with their start and end apart: 61, of which 36 were waited for; matrix products, arithmetic and copies ran while one was open for 23% of the time, Pallas kernels for 0%

commit v1 on v0

v1 whole, which is shorter than its diff:
```python
import jax
import jax.numpy as jnp
from jax import lax
from jax.experimental import pallas as pl
from jax.experimental.pallas import tpu as pltpu
from jax.sharding import PartitionSpec as P


SUB = 12
ROWS = 64
LANES = 128
HALO = 16
PAD = 8
TALL = PAD + HALO + ROWS + HALO + PAD
TOP = PAD + HALO + ROWS

U, V, S1, S2, S12, STR, HW, HH, INE, AA, KU, KV = range(12)
SENT = 12
BB, HWV, HHV, DU, SU, DV, SV, DP, DS, AS, AM = range(12, 23)
HELD = 23
MOVING = (U, V, INE, AA, KU, KV)
NEGATED = (U, V, KU, KV)
MESSAGE = SENT * HALO + SENT // 2 * 8


def lane_index():
    return lax.broadcasted_iota(jnp.int32, (8, LANES), 1)


def row_index():
    return lax.broadcasted_iota(jnp.int32, (8, LANES), 0)


def turned(value, steps):
    steps = steps % LANES
    return value if steps == 0 else pltpu.roll(value, steps, 1)


def west(main, side, first):
    a, b = turned(main, 1), turned(side, 1)
    return jnp.where(first, b, a), jnp.where(first, a, b)


def east(main, side, last):
    a, b = turned(main, -1), turned(side, -1)
    return jnp.where(last, b, a), jnp.where(last, a, b)


def expanded(blocks_t):
    rows = lax.broadcasted_iota(jnp.int32, (ROWS, 16), 0) // 4
    pick_rows = (rows == lax.broadcasted_iota(jnp.int32, (ROWS, 16), 1)).astype(jnp.float32)
    lanes = lax.broadcasted_iota(jnp.int32, (4, LANES), 1) // 32
    pick_lanes = (lanes == lax.broadcasted_iota(jnp.int32, (4, LANES), 0)).astype(jnp.float32)
    half = lax.dot_general(
        pick_rows, blocks_t, (((1,), (1,)), ((), ())), preferred_element_type=jnp.float32
    )
    return lax.dot_general(
        half, pick_lanes, (((1,), (0,)), ((), ())), preferred_element_type=jnp.float32
    )


def prepare_kernel(
    vel_hbm,
    stress_hbm,
    wind_hbm,
    ocean_hbm,
    area_hbm,
    volume_hbm,
    wide_hbm,
    high_hbm,
    land_hbm,
    ice_hbm,
    fields,
    to_west,
    to_east,
    snap,
    vel,
    stress,
    wind,
    ocean,
    wide,
    high,
    land_t,
    ice_t,
    sems,
):
    area, volume = snap.at[0:5], snap.at[5:10]
    moves = (
        (area_hbm, area),
        (volume_hbm, volume),
        (land_hbm, land_t),
        (ice_hbm, ice_t),
        (ocean_hbm, ocean),
        (wind_hbm, wind),
        (stress_hbm, stress),
        (vel_hbm, vel),
        (wide_hbm, wide),
        (high_hbm, high),
    )
    copies = [pltpu.make_async_copy(a, b, sems.at[n]) for n, (a, b) in enumerate(moves)]
    for copy in copies:
        copy.start()
    for copy in copies:
        copy.wait()
    land = expanded(land_t[...].astype(jnp.float32))
    ice = expanded(ice_t[...].astype(jnp.float32))
    area_total = area[0] + area[1] + area[2] + area[3] + area[4]
    volume_total = volume[0] + volume[1] + volume[2] + volume[3] + volume[4]
    fields[U] = vel[0]
    fields[V] = vel[1]
    fields[S1] = 0.5 * stress[0]
    fields[S2] = 0.5 * stress[1]
    fields[S12] = stress[2]
    fields[STR] = (4.0 / 6.0) * volume_total * jnp.exp(-20.0 * (1.0 - area_total)) * land
    fields[HW] = 0.5 * wide[...]
    fields[HH] = 0.5 * high[...]
    inertia = 16.0 * (1.0 + volume_total)
    turning = 0.5 * (1.0 + volume_total)
    damped = inertia + 1.0
    scale = land * ice / (damped * damped + turning * turning)
    still = land * (1.0 - ice)
    fx = wind[0] + ocean[0]
    fy = wind[1] + ocean[1]
    fields[INE] = inertia
    fields[AA] = scale
    fields[KU] = scale * (damped * fx + turning * fy) + still * ocean[0]
    fields[KV] = scale * (damped * fy - turning * fx) + still * ocean[1]
    lane = lane_index()
    for f in range(SENT):
        left = right = None
        for g in range(8):
            part = fields[f, 8 * g : 8 * g + 8]
            inside = (lane >= 16 * g) & (lane < 16 * g + 16)
            a = turned(part, 16 * g)
            b = turned(part, 16 * g - 112)
            left = a if g == 0 else jnp.where(inside, a, left)
            right = b if g == 0 else jnp.where(inside, b, right)
        to_west[8 * f : 8 * f + 8] = left
        to_east[8 * f : 8 * f + 8] = right


def rows_kernel(fields, from_west, from_east, to_north, to_south):
    lane = lane_index()
    for f in range(SENT):
        to_north[HALO * f : HALO * f + HALO] = fields[f, ROWS - HALO : ROWS]
        to_south[HALO * f : HALO * f + HALO] = fields[f, 0:HALO]
    for pair in range(SENT // 2):
        north = south = None
        for member in range(2):
            f = 2 * pair + member
            base = 64 * member
            a = from_west[8 * f : 8 * f + 8]
            b = from_east[8 * f : 8 * f + 8]
            here = lane >= base
            there = lane >= base + 32
            n = jnp.where(there, turned(b, base + 32 - 96), turned(a, base - 96))
            s = jnp.where(there, turned(b, base + 32), turned(a, base))
            north = n if member == 0 else jnp.where(here, n, north)
            south = s if member == 0 else jnp.where(here, s, south)
        at = SENT * HALO + 8 * pair
        to_north[at : at + 8] = north
        to_south[at : at + 8] = south


def stencil_kernel(fields, from_west, from_east, from_south, from_north, from_fold, vel, stress, held):
    is_top = lax.axis_index("row") == 7
    lane = lane_index()
    row = row_index()
    first = lane == 0
    last = lane == LANES - 1
    low = lane < 64
    top_rows = jnp.where(is_top, 1, 0) + jnp.zeros((8, LANES), jnp.int32)

    def side_rows(message, f, a):
        at = SENT * HALO + 8 * (f // 2)
        base = 64 * (f % 2)
        corner = message[at : at + 8]
        return jnp.where(low, turned(corner, -(base + 32 + 16 * a)), turned(corner, 112 - base - 16 * a))

    for f in range(SENT):
        a, b = from_west[8 * f : 8 * f + 8], from_east[8 * f : 8 * f + 8]
        for g in range(8):
            at = PAD + HALO + 8 * g
            held[f, 0, at : at + 8] = fields[f, 8 * g : 8 * g + 8]
            held[f, 1, at : at + 8] = jnp.where(low, turned(b, -16 * g), turned(a, 112 - 16 * g))
        for g in range(2):
            at = PAD + 8 * g
            held[f, 0, at : at + 8] = from_south[HALO * f + 8 * g : HALO * f + 8 * g + 8]
            held[f, 1, at : at + 8] = side_rows(from_south, f, g)

    @pl.when(jnp.logical_not(is_top))
    def _():
        for f in range(SENT):
            for g in range(2):
                at = TOP + 8 * g
                held[f, 0, at : at + 8] = from_north[HALO * f + 8 * g : HALO * f + 8 * g + 8]
                held[f, 1, at : at + 8] = side_rows(from_north, f, g)

    @pl.when(is_top)
    def _():
        def rotated(value):
            value = jnp.take_along_axis(value, LANES - 1 - lane, axis=1)
            return jnp.take_along_axis(value, 7 - row, axis=0)

        for f in range(SENT):
            for g in range(2):
                source = 1 - g
                main = rotated(from_fold[HALO * f + 8 * source : HALO * f + 8 * source + 8])
                side = rotated(side_rows(from_fold, f, source))
                if f in MOVING:
                    main, side = east(main, side, last)
                    if f in NEGATED:
                        main, side = -main, -side
                    at = TOP + 8 * g
                else:
                    at = TOP + 1 + 8 * g
                held[f, 0, at : at + 8] = main
                held[f, 1, at : at + 8] = side
                if f in (HW, HH):
                    main, side = east(main, side, last)
                    own = HWV if f == HW else HHV
                    held[own, 0, TOP + 8 * g : TOP + 8 * g + 8] = main
                    held[own, 1, TOP + 8 * g : TOP + 8 * g + 8] = side

    def velocity_sums(at, um, us, vm, vs):
        wum, wus = west(um, us, first)
        wvm, wvs = west(vm, vs, first)
        for t, (x, wx, y, wy) in enumerate(((um, wum, vm, wvm), (us, wus, vs, wvs))):
            held[DU, t, at : at + 8] = x - wx
            held[SU, t, at : at + 8] = x + wx
            held[DV, t, at : at + 8] = y - wy
            held[SV, t, at : at + 8] = y + wy

    for g in range(12):
        at = PAD + 8 * g
        for t in range(2):
            scale = held[AA, t, at : at + 8]
            inertia = held[INE, t, at : at + 8]
            held[AA, t, at : at + 8] = (inertia + 1.0) * scale
            held[BB, t, at : at + 8] = (inertia * (1.0 / 32.0)) * scale
            if g < 10:
                held[HWV, t, at : at + 8] = held[HW, t, at : at + 8]
                held[HHV, t, at : at + 8] = held[HH, t, at : at + 8]
        velocity_sums(
            at,
            held[U, 0, at : at + 8],
            held[U, 1, at : at + 8],
            held[V, 0, at : at + 8],
            held[V, 1, at : at + 8],
        )

    @pl.when(jnp.logical_not(is_top))
    def _():
        for t in range(2):
            held[HWV, t, TOP : TOP + HALO] = held[HW, t, TOP : TOP + HALO]
            held[HHV, t, TOP : TOP + HALO] = held[HH, t, TOP : TOP + HALO]

    def stress_rows(at):
        fresh = []
        for t in range(2):
            here = lambda f: held[f, t, at : at + 8]
            below = lambda f: held[f, t, at - 1 : at + 7]
            hw, hh = here(HW), here(HH)
            gux = hw * (here(DU) + below(DU))
            guy = hh * (here(SU) - below(SU))
            gvx = hw * (here(DV) + below(DV))
            gvy = hh * (here(SV) - below(SV))
            divergence = gux + gvy
            tension = gux - gvy
            shearing = guy + gvx
            deform = jnp.sqrt(
                divergence * divergence + 0.25 * (tension * tension + shearing * shearing)
            )
            viscous = here(STR) / (deform + 0.5)
            quarter = 0.25 * viscous
            s1 = here(S1) * (2.0 / 3.0) + viscous * (divergence - deform)
            s2 = here(S2) * (2.0 / 3.0) + quarter * tension
            s12 = here(S12) * (2.0 / 3.0) + quarter * shearing
            held[S1, t, at : at + 8] = s1
            held[S2, t, at : at + 8] = s2
            held[S12, t, at : at + 8] = s12
            fresh.append((s1 + s2, s1 - s2, s12))
        (pm, mm, qm), (ps, ms, qs) = fresh
        epm, eps = east(pm, ps, last)
        emm, ems = east(mm, ms, last)
        eqm, eqs = east(qm, qs, last)
        for t, (p, ep, m, em, q, eq) in enumerate(
            ((pm, epm, mm, emm, qm, eqm), (ps, eps, ms, ems, qs, eqs))
        ):
            held[DP, t, at : at + 8] = ep - p
            held[AM, t, at : at + 8] = em + m
            held[DS, t, at : at + 8] = eq - q
            held[AS, t, at : at + 8] = eq + q

    def velocity_rows(at):
        fresh = []
        for t in range(2):
            here = lambda f: held[f, t, at : at + 8]

            def pair(f):
                own, above = here(f), held[f, t, at + 1 : at + 9]
                if at == TOP - 8:
                    above = jnp.where((row == 7) & (top_rows == 1), held[f, t, at + 2 : at + 10], above)
                if at == TOP:
                    own = jnp.where((row == 0) & (top_rows == 1), held[f, t, at - 1 : at + 7], own)
                return own, above

            hw, hh = here(HWV), here(HHV)
            dp, ndp = pair(DP)
            ds, nds = pair(DS)
            as_, nas = pair(AS)
            am, nam = pair(AM)
            inertia, a, b = here(INE), here(AA), here(BB)
            x = inertia * here(U) + (hw * (dp + ndp) + hh * (nas - as_))
            y = inertia * here(V) + (hw * (ds + nds) + hh * (nam - am))
            u = a * x + b * y + here(KU)
            v = a * y - b * x + here(KV)
            held[U, t, at : at + 8] = u
            held[V, t, at : at + 8] = v
            fresh.append((u, v))
        (um, vm), (us, vs) = fresh
        velocity_sums(at, um, us, vm, vs)

    def subcycle(lo, hi):
        def body(_, carry):
            for g in range(lo, hi):
                stress_rows(PAD + 8 * g)
            for g in range(lo, hi):
                velocity_rows(PAD + 8 * g)
            return carry

        return body

    lax.fori_loop(0, 5, subcycle(0, 12), 0)
    lax.fori_loop(5, SUB, subcycle(1, 11), 0)
    at = PAD + HALO
    vel[0] = held[U, 0, at : at + ROWS]
    vel[1] = held[V, 0, at : at + ROWS]
    stress[0] = 2.0 * held[S1, 0, at : at + ROWS]
    stress[1] = 2.0 * held[S2, 0, at : at + ROWS]
    stress[2] = held[S12, 0, at : at + ROWS]


def restart_kernel(writer, own, other, near, near_other, far, far_other, side, side_other, out, zero, sems):
    me = lax.axis_index("row")
    chip, core = me // 2, me % 2
    step = 1 - 2 * core
    behind = lax.rem(chip - step + 4, 4)
    ahead = lax.rem(chip + step + 4, 4)
    across = lax.rem(chip + 2, 4)
    blocks = (
        (own, me),
        (other, 2 * chip + 1 - core),
        (near, 2 * behind + core),
        (near_other, 2 * behind + 1 - core),
        (side, 2 * ahead + 1 - core),
        (side_other, 2 * ahead + core),
        (far, 2 * across + core),
        (far_other, 2 * across + 1 - core),
    )
    mine = writer[lax.axis_index("col")] == me

    @pl.when(mine)
    def _():
        copies = [
            pltpu.make_async_copy(ref, out.at[0, :, pl.ds(place * ROWS, ROWS), :], sems.at[n])
            for n, (ref, place) in enumerate(blocks)
        ]
        for copy in copies:
            copy.start()
        for copy in copies:
            copy.wait()

    @pl.when(jnp.logical_not(mine))
    def _():
        zero[...] = jnp.zeros_like(zero)
        copies = [
            pltpu.make_async_copy(zero, out.at[0, :, pl.ds(n * ROWS, ROWS), :], sems.at[n])
            for n in range(8)
        ]
        for copy in copies:
            copy.start()
        for copy in copies:
            copy.wait()


def vmem():
    return pl.BlockSpec(memory_space=pltpu.VMEM)


def shape(*dims):
    return jax.ShapeDtypeStruct(dims, jnp.float32)


def grant(mebibytes):
    return pltpu.CompilerParams(vmem_limit_bytes=mebibytes << 20)


def step(
    velocity_start,
    stress_start,
    wind_stress,
    ocean_current,
    ice_area,
    ice_volume,
    inverse_width,
    inverse_height,
    land_block,
    ice_block,
    writer,
):
    fields, to_west, to_east, snap = pl.pallas_call(
        prepare_kernel,
        out_shape=(
            shape(SENT, ROWS, LANES),
            shape(SENT * 8, LANES),
            shape(SENT * 8, LANES),
            shape(10, ROWS, LANES),
        ),
        in_specs=[pl.BlockSpec(memory_space=pltpu.HBM)] * 10,
        out_specs=(vmem(),) * 4,
        scratch_shapes=[
            pltpu.VMEM((2, ROWS, LANES), jnp.float32),
            pltpu.VMEM((3, ROWS, LANES), jnp.float32),
            pltpu.VMEM((2, ROWS, LANES), jnp.float32),
            pltpu.VMEM((2, ROWS, LANES), jnp.float32),
            pltpu.VMEM((ROWS, LANES), jnp.float32),
            pltpu.VMEM((ROWS, LANES), jnp.float32),
            pltpu.VMEM((4, 16), jnp.int32),
            pltpu.VMEM((4, 16), jnp.int32),
            pltpu.SemaphoreType.DMA((10,)),
        ],
        compiler_params=grant(8),
        name="prepare",
    )(
        *(
            pltpu.with_memory_space_constraint(value, pltpu.HBM)
            for value in (
                velocity_start,
                stress_start,
                wind_stress,
                ocean_current,
                ice_area,
                ice_volume,
                inverse_width,
                inverse_height,
                land_block.T,
                ice_block.T,
            )
        )
    )
    along = [(r, (r + 2 - 4 * (r % 2)) % 8) for r in range(8)]
    partner = [(r, r ^ 1) for r in range(8)]
    eastward = [(c, (c + 1) % 32) for c in range(32)]
    westward = [(c, (c - 1) % 32) for c in range(32)]
    folded = [(7 * 32 + c, 7 * 32 + 31 - c) for c in range(32)]

    from_west = lax.ppermute(to_east, "col", eastward)
    from_east = lax.ppermute(to_west, "col", westward)
    near = lax.ppermute(snap, "row", along)
    other = lax.ppermute(snap, "row", partner)
    near_other = lax.ppermute(other, "row", along)

    to_north, to_south = pl.pallas_call(
        rows_kernel,
        out_shape=(shape(MESSAGE, LANES),) * 2,
        in_specs=[vmem()] * 3,
        out_specs=(vmem(),) * 2,
        compiler_params=grant(8),
        cost_estimate=pl.CostEstimate(flops=1000000, bytes_accessed=1000000, transcendentals=0),
        name="rows",
    )(fields, from_west, from_east)
    from_south = lax.ppermute(to_north, "row", [(r, r + 1) for r in range(7)])
    from_north = lax.ppermute(to_south, "row", [(r + 1, r) for r in range(7)])
    from_fold = lax.ppermute(to_north, ("row", "col"), folded)
    far = lax.ppermute(near, "row", along)
    side = lax.ppermute(near, "row", partner)
    side_other = lax.ppermute(near_other, "row", partner)
    far_other = lax.ppermute(far, "row", partner)

    velocity, stress = pl.pallas_call(
        stencil_kernel,
        out_shape=(shape(2, ROWS, LANES), shape(3, ROWS, LANES)),
        in_specs=[vmem()] * 6,
        out_specs=(vmem(),) * 2,
        scratch_shapes=[pltpu.VMEM((HELD, 2, TALL, LANES), jnp.float32)],
        compiler_params=grant(16),
        cost_estimate=pl.CostEstimate(flops=40000000, bytes_accessed=2000000, transcendentals=0),
        name="stencil",
    )(fields, from_west, from_east, from_south, from_north, from_fold)

    restart = pl.pallas_call(
        restart_kernel,
        out_shape=shape(1, 10, 8 * ROWS, LANES),
        in_specs=[pl.BlockSpec(memory_space=pltpu.SMEM)] + [pl.BlockSpec(memory_space=pl.ANY)] * 8,
        out_specs=pl.BlockSpec(memory_space=pl.ANY),
        scratch_shapes=[pltpu.VMEM((10, ROWS, LANES), jnp.float32), pltpu.SemaphoreType.DMA((8,))],
        compiler_params=grant(4),
        name="restart",
    )(writer, snap, other, near, near_other, far, far_other, side, side_other)
    return (velocity, stress, restart)


def solution(mesh):
    return jax.shard_map(
        step,
        mesh=mesh,
        in_specs=(
            P(None, "row", "col"),
            P(None, "row", "col"),
            P(None, "row", "col"),
            P(None, "row", "col"),
            P(None, "row", "col"),
            P(None, "row", "col"),
            P("row", "col"),
            P("row", "col"),
            P("row", "col"),
            P("row", "col"),
            P(),
        ),
        out_specs=(P(None, "row", "col"), P(None, "row", "col"), P("row", None, None, "col")),
        check_vma=False,
    )
```

time: 417 us -> 52.3 us (0.13)
  the two profiles are of different devices: /device:TPU:6 before, /device:TPU:1 now
where the time goes in v1:
time: 52.3 us; the launch traced here: 52.2 us
  starting transfers between devices  27.9 us (53%)
  waiting for transfers between devices  13.9 us (27%)
  Pallas kernels  9.08 us (17%)
  between operations  0.7 us (1%)
  local copies, waits for them, and re-layouts  0.65 us (1%)
    ppermute x1, starting transfers between devices, step(): from_east = lax.ppermute(to_west, 'col', westward)  6.32 us
    ppermute x1, starting transfers between devices, step(): far_other = lax.ppermute(far, 'row', partner)  5.32 us
    pallas_call x1, Pallas kernels, step(): pl.pallas_call(stencil_kernel, out_shape=(shape(2, ROWS, LANES), shape(3,...  5.12 us
    ppermute x1, waiting for transfers between devices, step(): near = lax.ppermute(snap, 'row', along)  4.01 us
    ppermute x1, starting transfers between devices, step(): side_other = lax.ppermute(near_other, 'row', partner)  3.51 us
    ppermute x1, starting transfers between devices, step(): near = lax.ppermute(snap, 'row', along)  3.37 us
    ppermute x1, starting transfers between devices, step(): far = lax.ppermute(near, 'row', along)  3.12 us
    ppermute x1, waiting for transfers between devices, step(): from_north = lax.ppermute(to_south, 'row', [(r + 1, r) for r in range(7)])  3.02 us
  transfers between devices with their start and end apart: 12, of which 5 were waited for; matrix products, arithmetic and copies ran while one was open for 0% of the time, Pallas kernels for 10%

profile of v1, /device:TPU:1, one launch (start us, length us, event | category | flops | bytes accessed | tf_op | source)
XLA Modules:
  0.0 52.2 jit_solution(7066817783614145184)
XLA Ops:
  0.6 1.7 %prepare.1 = (f32[12,64,128]{2,1,0:T(8,128)S(1)}, f32[96,128]{1,0:T(8,128)S(1)}, f32[96,128]{1,0:T(8,128)S(1)}, f32[10,64,128]{2,1,0:T(8,128)S(1)}) custom-call(f32[2,64,128]{2,1,0:T(8,128)} %vel_hbm.1, f32[3,64,128]{2,1,0:T(8,128)} %stress_hbm.1, f32[2,64,128]{2,1,0:T(8,128)} %wind_hbm.1, f32[2,64,128]{2,1,0:T(8,128)} %ocean_hbm.1, f32[5,64,128]{2,1,0:T(8,128)} %area_hbm.1, ...), custom_call_target="tpu_custom_call" | custom-call | tf_op jit(solution)/shard_map/prepare/pallas_call | solution.py:412
  2.4 3.4 %collective-permute-start.6 = (f32[10,64,128]{2,1,0:T(8,128)S(1)}, f32[10,64,128]{2,1,0:T(8,128)S(1)}, u32[]{:S(2)}, u32[]{:S(2)}) collective-permute-start(f32[10,64,128]{2,1,0:T(8,128)S(1)} %get-tuple-element.18.own), channel_id=1, source_target_pairs={{0,64},{32,224},{64,128},{96,32},{128,192},{160,96},{192,0},{224,1... | collective-permute-start | bytes 983048 | tf_op jit(solution)/shard_map/ppermute | solution.py:460
  5.7 0.0 collective-permute-start.5
  5.7 4.0 %collective-permute-done.6.near = f32[10,64,128]{2,1,0:T(8,128)S(1)} collective-permute-done((f32[10,64,128]{2,1,0:T(8,128)S(1)}, f32[10,64,128]{2,1,0:T(8,128)S(1)}, u32[]{:S(2)}, u32[]{:S(2)}) %collective-permute-start.6) | collective-permute-done | bytes 327712 | tf_op jit(solution)/shard_map/ppermute | solution.py:460
  9.7 3.1 %collective-permute-start.8 = (f32[10,64,128]{2,1,0:T(8,128)S(1)}, f32[10,64,128]{2,1,0:T(8,128)S(1)}, u32[]{:S(2)}, u32[]{:S(2)}) collective-permute-start(f32[10,64,128]{2,1,0:T(8,128)S(1)} %collective-permute-done.6.near), channel_id=1, source_target_pairs={{0,64},{32,224},{64,128},{96,32},{128,192},{160,96},{192,0},{224,1... | collective-permute-start | bytes 983048 | tf_op jit(solution)/shard_map/ppermute | solution.py:476
  12.9 0.0 collective-permute-done.5.other
  12.9 0.0 collective-permute-start.7
  12.9 1.1 %collective-permute-start.10 = (f32[10,64,128]{2,1,0:T(8,128)S(1)}, f32[10,64,128]{2,1,0:T(8,128)S(1)}, u32[]{:S(2)}, u32[]{:S(2)}) collective-permute-start(f32[10,64,128]{2,1,0:T(8,128)S(1)} %collective-permute-done.6.near), channel_id=1, source_target_pairs={{0,32},{32,0},{64,96},{96,64},{128,160},{160,128},{192,224},{224,1... | collective-permute-start | bytes 983048 | tf_op jit(solution)/shard_map/ppermute | solution.py:477
  14.0 2.9 %collective-permute-done.8.far = f32[10,64,128]{2,1,0:T(8,128)S(1)} collective-permute-done((f32[10,64,128]{2,1,0:T(8,128)S(1)}, f32[10,64,128]{2,1,0:T(8,128)S(1)}, u32[]{:S(2)}, u32[]{:S(2)}) %collective-permute-start.8) | collective-permute-done | bytes 327712 | tf_op jit(solution)/shard_map/ppermute | solution.py:476
  16.9 5.3 %collective-permute-start.9 = (f32[10,64,128]{2,1,0:T(8,128)S(1)}, f32[10,64,128]{2,1,0:T(8,128)S(1)}, u32[]{:S(2)}, u32[]{:S(2)}) collective-permute-start(f32[10,64,128]{2,1,0:T(8,128)S(1)} %collective-permute-done.8.far), channel_id=1, source_target_pairs={{0,32},{32,0},{64,96},{96,64},{128,160},{160,128},{192,224},{224,1... | collective-permute-start | bytes 983048 | tf_op jit(solution)/shard_map/ppermute | solution.py:479
  22.2 0.0 collective-permute-done.7.near_other
  22.2 3.5 %collective-permute-start.11 = (f32[10,64,128]{2,1,0:T(8,128)S(1)}, f32[10,64,128]{2,1,0:T(8,128)S(1)}, u32[]{:S(2)}, u32[]{:S(2)}) collective-permute-start(f32[10,64,128]{2,1,0:T(8,128)S(1)} %collective-permute-done.7.near_other), channel_id=1, source_target_pairs={{0,32},{32,0},{64,96},{96,64},{128,160},{160,128},{192,224},{224,1... | collective-permute-start | bytes 983048 | tf_op jit(solution)/shard_map/ppermute | solution.py:478
  25.7 0.0 collective-permute-start
  25.7 6.3 %collective-permute-start.1 = (f32[96,128]{1,0:T(8,128)S(1)}, f32[96,128]{1,0:T(8,128)S(1)}, u32[]{:S(2)}, u32[]{:S(2)}) collective-permute-start(f32[96,128]{1,0:T(8,128)S(1)} %get-tuple-element.13), channel_id=1, source_target_pairs={{0,31},{1,0},{2,1},{3,2},{4,3},{5,4},{6,5},{7,6},{8,7},{9,8},{10,9... | collective-permute-start | bytes 147464 | tf_op jit(solution)/shard_map/ppermute | solution.py:459
  32.0 2.1 %collective-permute-done.from_west = f32[96,128]{1,0:T(8,128)S(1)} collective-permute-done((f32[96,128]{1,0:T(8,128)S(1)}, f32[96,128]{1,0:T(8,128)S(1)}, u32[]{:S(2)}, u32[]{:S(2)}) %collective-permute-start) | collective-permute-done | bytes 49184 | tf_op jit(solution)/shard_map/ppermute | solution.py:458
  34.1 0.0 collective-permute-done.1.from_east
  34.1 0.1 rows.1
  34.3 2.5 %collective-permute-start.3 = (f32[240,128]{1,0:T(8,128)S(1)}, f32[240,128]{1,0:T(8,128)S(1)}, u32[]{:S(2)}, u32[]{:S(2)}) collective-permute-start(f32[240,128]{1,0:T(8,128)S(1)} %get-tuple-element.15), channel_id=1, source_target_pairs={{32,0},{64,32},{96,64},{128,96},{160,128},{192,160},{224,192},{33,... | collective-permute-start | bytes 368648 | tf_op jit(solution)/shard_map/ppermute | solution.py:474
  36.8 0.7 %collective-permute-start.4 = (f32[240,128]{1,0:T(8,128)S(1)}, f32[240,128]{1,0:T(8,128)S(1)}, u32[]{:S(2)}, u32[]{:S(2)}) collective-permute-start(f32[240,128]{1,0:T(8,128)S(1)} %get-tuple-element.14), channel_id=1, source_target_pairs={{224,255},{225,254},{226,253},{227,252},{228,251},{229,250},{230,2... | collective-permute-start | bytes 368648 | tf_op jit(solution)/shard_map/ppermute | solution.py:475
  37.4 3.0 %collective-permute-done.3.from_north = f32[240,128]{1,0:T(8,128)S(1)} collective-permute-done((f32[240,128]{1,0:T(8,128)S(1)}, f32[240,128]{1,0:T(8,128)S(1)}, u32[]{:S(2)}, u32[]{:S(2)}) %collective-permute-start.3) | collective-permute-done | bytes 122912 | tf_op jit(solution)/shard_map/ppermute | solution.py:474
  40.5 1.9 %collective-permute-start.2 = (f32[240,128]{1,0:T(8,128)S(1)}, f32[240,128]{1,0:T(8,128)S(1)}, u32[]{:S(2)}, u32[]{:S(2)}) collective-permute-start(f32[240,128]{1,0:T(8,128)S(1)} %get-tuple-element.14), channel_id=1, source_target_pairs={{0,32},{32,64},{64,96},{96,128},{128,160},{160,192},{192,224},{1,3... | collective-permute-start | bytes 368648 | tf_op jit(solution)/shard_map/ppermute | solution.py:473
  42.4 0.0 collective-permute-done.4.from_fold
  42.4 1.8 %collective-permute-done.2.from_south = f32[240,128]{1,0:T(8,128)S(1)} collective-permute-done((f32[240,128]{1,0:T(8,128)S(1)}, f32[240,128]{1,0:T(8,128)S(1)}, u32[]{:S(2)}, u32[]{:S(2)}) %collective-permute-start.2) | collective-permute-done | bytes 122912 | tf_op jit(solution)/shard_map/ppermute | solution.py:473
  44.2 5.1 %stencil.1 = (f32[2,64,128]{2,1,0:T(8,128)}, f32[3,64,128]{2,1,0:T(8,128)}) custom-call(f32[12,64,128]{2,1,0:T(8,128)S(1)} %get-tuple-element.11.fields, f32[96,128]{1,0:T(8,128)S(1)} %collective-permute-done.from_west, f32[96,128]{1,0:T(8,128)S(1)} %collective-permute-done.1.from_east, f32[240,128]{1,0:T(8,128)S(1)} %collective-permute-done.2.from_south, ...), custom_call_target="tpu_custom_call" | custom-call | flops 40000000 | bytes 2000000 | tf_op jit(solution)/shard_map/stencil/pallas_call | solution.py:481
  49.3 0.0 collective-permute-done.10.side
  49.3 0.0 collective-permute-done.9.far_other
  49.3 0.0 collective-permute-done.11.side_other
  49.4 0.0 copy-start
  49.4 0.6 %copy-done = s32[32]{0:T(128)S(1)} copy-done((s32[32]{0:T(128)S(1)}, s32[32]{0:T(128)}, u32[]{:S(2)}) %copy-start) | copy-done | bytes 152
  50.0 2.2 %restart.1 = f32[1,10,512,128]{3,2,1,0:T(8,128)} custom-call(s32[32]{0:T(128)S(1)} %copy-done, f32[10,64,128]{2,1,0:T(8,128)S(1)} %get-tuple-element.18.own, f32[10,64,128]{2,1,0:T(8,128)S(1)} %collective-permute-done.5.other, f32[10,64,128]{2,1,0:T(8,128)S(1)} %collective-permute-done.6.near, f32[10,64,128]{2,1,0:T(8,128)S(1)} %collective-permute-done.7.near_other, ...), custom_call_target="tpu_custom_call" | custom-call | tf_op jit(solution)/shard_map/restart/pallas_call | solution.py:492
Async XLA Ops:
  2.4 7.4 %collective-permute-start.6 = (f32[10,64,128]{2,1,0:T(8,128)S(1)}, f32[10,64,128]{2,1,0:T(8,128)S(1)}, u32[]{:S(2)}, u32[]{:S(2)}) collective-permute-start(f32[10,64,128]{2,1,0:T(8,128)S(1)} %get-tuple-element.18.own), channel_id=1, source_target_pairs={{0,64},{32,224},{64,128},{96,32},{128,192},{160,96},{192,0},{224,1... | collective-permute-start | bytes 983048 | tf_op jit(solution)/shard_map/ppermute | solution.py:460
  5.7 7.1 %collective-permute-start.5 = (f32[10,64,128]{2,1,0:T(8,128)S(1)}, f32[10,64,128]{2,1,0:T(8,128)S(1)}, u32[]{:S(2)}, u32[]{:S(2)}) collective-permute-start(f32[10,64,128]{2,1,0:T(8,128)S(1)} %get-tuple-element.18.own), channel_id=1, source_target_pairs={{0,32},{32,0},{64,96},{96,64},{128,160},{160,128},{192,224},{224,1... | collective-permute-start | bytes 983048 | tf_op jit(solution)/shard_map/ppermute | solution.py:461
  9.7 7.1 %collective-permute-start.8 = (f32[10,64,128]{2,1,0:T(8,128)S(1)}, f32[10,64,128]{2,1,0:T(8,128)S(1)}, u32[]{:S(2)}, u32[]{:S(2)}) collective-permute-start(f32[10,64,128]{2,1,0:T(8,128)S(1)} %collective-permute-done.6.near), channel_id=1, source_target_pairs={{0,64},{32,224},{64,128},{96,32},{128,192},{160,96},{192,0},{224,1... | collective-permute-start | bytes 983048 | tf_op jit(solution)/shard_map/ppermute | solution.py:476
  12.9 9.3 %collective-permute-start.7 = (f32[10,64,128]{2,1,0:T(8,128)S(1)}, f32[10,64,128]{2,1,0:T(8,128)S(1)}, u32[]{:S(2)}, u32[]{:S(2)}) collective-permute-start(f32[10,64,128]{2,1,0:T(8,128)S(1)} %collective-permute-done.5.other), channel_id=1, source_target_pairs={{0,64},{32,224},{64,128},{96,32},{128,192},{160,96},{192,0},{224,1... | collective-permute-start | bytes 983048 | tf_op jit(solution)/shard_map/ppermute | solution.py:462
  12.9 36.5 %collective-permute-start.10 = (f32[10,64,128]{2,1,0:T(8,128)S(1)}, f32[10,64,128]{2,1,0:T(8,128)S(1)}, u32[]{:S(2)}, u32[]{:S(2)}) collective-permute-start(f32[10,64,128]{2,1,0:T(8,128)S(1)} %collective-permute-done.6.near), channel_id=1, source_target_pairs={{0,32},{32,0},{64,96},{96,64},{128,160},{160,128},{192,224},{224,1... | collective-permute-start | bytes 983048 | tf_op jit(solution)/shard_map/ppermute | solution.py:477
  16.9 32.5 %collective-permute-start.9 = (f32[10,64,128]{2,1,0:T(8,128)S(1)}, f32[10,64,128]{2,1,0:T(8,128)S(1)}, u32[]{:S(2)}, u32[]{:S(2)}) collective-permute-start(f32[10,64,128]{2,1,0:T(8,128)S(1)} %collective-permute-done.8.far), channel_id=1, source_target_pairs={{0,32},{32,0},{64,96},{96,64},{128,160},{160,128},{192,224},{224,1... | collective-permute-start | bytes 983048 | tf_op jit(solution)/shard_map/ppermute | solution.py:479
  22.2 27.1 %collective-permute-start.11 = (f32[10,64,128]{2,1,0:T(8,128)S(1)}, f32[10,64,128]{2,1,0:T(8,128)S(1)}, u32[]{:S(2)}, u32[]{:S(2)}) collective-permute-start(f32[10,64,128]{2,1,0:T(8,128)S(1)} %collective-permute-done.7.near_other), channel_id=1, source_target_pairs={{0,32},{32,0},{64,96},{96,64},{128,160},{160,128},{192,224},{224,1... | collective-permute-start | bytes 983048 | tf_op jit(solution)/shard_map/ppermute | solution.py:478
  25.7 8.4 %collective-permute-start = (f32[96,128]{1,0:T(8,128)S(1)}, f32[96,128]{1,0:T(8,128)S(1)}, u32[]{:S(2)}, u32[]{:S(2)}) collective-permute-start(f32[96,128]{1,0:T(8,128)S(1)} %get-tuple-element.12), channel_id=1, source_target_pairs={{0,1},{1,2},{2,3},{3,4},{4,5},{5,6},{6,7},{7,8},{8,9},{9,10},{10,1... | collective-permute-start | bytes 147464 | tf_op jit(solution)/shard_map/ppermute | solution.py:458
  25.7 8.4 %collective-permute-start.1 = (f32[96,128]{1,0:T(8,128)S(1)}, f32[96,128]{1,0:T(8,128)S(1)}, u32[]{:S(2)}, u32[]{:S(2)}) collective-permute-start(f32[96,128]{1,0:T(8,128)S(1)} %get-tuple-element.13), channel_id=1, source_target_pairs={{0,31},{1,0},{2,1},{3,2},{4,3},{5,4},{6,5},{7,6},{8,7},{9,8},{10,9... | collective-permute-start | bytes 147464 | tf_op jit(solution)/shard_map/ppermute | solution.py:459
  34.3 6.2 %collective-permute-start.3 = (f32[240,128]{1,0:T(8,128)S(1)}, f32[240,128]{1,0:T(8,128)S(1)}, u32[]{:S(2)}, u32[]{:S(2)}) collective-permute-start(f32[240,128]{1,0:T(8,128)S(1)} %get-tuple-element.15), channel_id=1, source_target_pairs={{32,0},{64,32},{96,64},{128,96},{160,128},{192,160},{224,192},{33,... | collective-permute-start | bytes 368648 | tf_op jit(solution)/shard_map/ppermute | solution.py:474
  36.8 5.6 %collective-permute-start.4 = (f32[240,128]{1,0:T(8,128)S(1)}, f32[240,128]{1,0:T(8,128)S(1)}, u32[]{:S(2)}, u32[]{:S(2)}) collective-permute-start(f32[240,128]{1,0:T(8,128)S(1)} %get-tuple-element.14), channel_id=1, source_target_pairs={{224,255},{225,254},{226,253},{227,252},{228,251},{229,250},{230,2... | collective-permute-start | bytes 368648 | tf_op jit(solution)/shard_map/ppermute | solution.py:475
  40.5 3.8 %collective-permute-start.2 = (f32[240,128]{1,0:T(8,128)S(1)}, f32[240,128]{1,0:T(8,128)S(1)}, u32[]{:S(2)}, u32[]{:S(2)}) collective-permute-start(f32[240,128]{1,0:T(8,128)S(1)} %get-tuple-element.14), channel_id=1, source_target_pairs={{0,32},{32,64},{64,96},{96,128},{128,160},{160,192},{192,224},{1,3... | collective-permute-start | bytes 368648 | tf_op jit(solution)/shard_map/ppermute | solution.py:473
  49.4 0.7 %copy-start = (s32[32]{0:T(128)S(1)}, s32[32]{0:T(128)}, u32[]{:S(2)}) copy-start(s32[32]{0:T(128)} %writer.1) | copy-start | bytes 388

commit v2 on v1

v2 whole, which is shorter than its diff:
```python
import jax
import jax.numpy as jnp
from jax import lax
from jax.experimental import pallas as pl
from jax.experimental.pallas import tpu as pltpu
from jax.sharding import PartitionSpec as P


SUB = 12
ROWS = 64
LANES = 128
HALO = 16
PAD = 8
TALL = PAD + HALO + ROWS + HALO + PAD
TOP = PAD + HALO + ROWS

U, V, S1, S2, S12, STR, HW, HH, INE, AA, KU, KV = range(12)
SENT = 12
BB, HWV, HHV, DU, SU, DV, SV, DP, DS, AS, AM = range(12, 23)
HELD = 23
MOVING = (U, V, INE, AA, KU, KV)
NEGATED = (U, V, KU, KV)
MESSAGE = SENT * HALO + SENT // 2 * 8


def lane_index():
    return lax.broadcasted_iota(jnp.int32, (8, LANES), 1)


def row_index():
    return lax.broadcasted_iota(jnp.int32, (8, LANES), 0)


def turned(value, steps):
    steps = steps % LANES
    return value if steps == 0 else pltpu.roll(value, steps, 1)


def west(main, side, first):
    a, b = turned(main, 1), turned(side, 1)
    return jnp.where(first, b, a), jnp.where(first, a, b)


def east(main, side, last):
    a, b = turned(main, -1), turned(side, -1)
    return jnp.where(last, b, a), jnp.where(last, a, b)


def expanded(blocks_t):
    rows = lax.broadcasted_iota(jnp.int32, (ROWS, 16), 0) // 4
    pick_rows = (rows == lax.broadcasted_iota(jnp.int32, (ROWS, 16), 1)).astype(jnp.float32)
    lanes = lax.broadcasted_iota(jnp.int32, (4, LANES), 1) // 32
    pick_lanes = (lanes == lax.broadcasted_iota(jnp.int32, (4, LANES), 0)).astype(jnp.float32)
    half = lax.dot_general(
        pick_rows, blocks_t, (((1,), (1,)), ((), ())), preferred_element_type=jnp.float32
    )
    return lax.dot_general(
        half, pick_lanes, (((1,), (0,)), ((), ())), preferred_element_type=jnp.float32
    )


def prepare_kernel(
    vel_hbm,
    stress_hbm,
    wind_hbm,
    ocean_hbm,
    area_hbm,
    volume_hbm,
    wide_hbm,
    high_hbm,
    land_hbm,
    ice_hbm,
    fields,
    to_west,
    to_east,
    snap,
    vel,
    stress,
    wind,
    ocean,
    wide,
    high,
    land_t,
    ice_t,
    sems,
):
    area, volume = snap.at[0:5], snap.at[5:10]
    moves = (
        (area_hbm, area),
        (volume_hbm, volume),
        (land_hbm, land_t),
        (ice_hbm, ice_t),
        (ocean_hbm, ocean),
        (wind_hbm, wind),
        (stress_hbm, stress),
        (vel_hbm, vel),
        (wide_hbm, wide),
        (high_hbm, high),
    )
    copies = [pltpu.make_async_copy(a, b, sems.at[n]) for n, (a, b) in enumerate(moves)]
    for copy in copies:
        copy.start()
    for copy in copies:
        copy.wait()
    land = expanded(land_t[...].astype(jnp.float32))
    ice = expanded(ice_t[...].astype(jnp.float32))
    area_total = area[0] + area[1] + area[2] + area[3] + area[4]
    volume_total = volume[0] + volume[1] + volume[2] + volume[3] + volume[4]
    fields[U] = vel[0]
    fields[V] = vel[1]
    fields[S1] = 0.5 * stress[0]
    fields[S2] = 0.5 * stress[1]
    fields[S12] = stress[2]
    fields[STR] = (4.0 / 6.0) * volume_total * jnp.exp(-20.0 * (1.0 - area_total)) * land
    fields[HW] = 0.5 * wide[...]
    fields[HH] = 0.5 * high[...]
    inertia = 16.0 * (1.0 + volume_total)
    turning = 0.5 * (1.0 + volume_total)
    damped = inertia + 1.0
    scale = land * ice / (damped * damped + turning * turning)
    still = land * (1.0 - ice)
    fx = wind[0] + ocean[0]
    fy = wind[1] + ocean[1]
    fields[INE] = inertia
    fields[AA] = scale
    fields[KU] = scale * (damped * fx + turning * fy) + still * ocean[0]
    fields[KV] = scale * (damped * fy - turning * fx) + still * ocean[1]
    lane = lane_index()
    for f in range(SENT):
        left = right = None
        for g in range(8):
            part = fields[f, 8 * g : 8 * g + 8]
            inside = (lane >= 16 * g) & (lane < 16 * g + 16)
            a = turned(part, 16 * g)
            b = turned(part, 16 * g - 112)
            left = a if g == 0 else jnp.where(inside, a, left)
            right = b if g == 0 else jnp.where(inside, b, right)
        to_west[8 * f : 8 * f + 8] = left
        to_east[8 * f : 8 * f + 8] = right


def rows_kernel(fields, from_west, from_east, upward, downward):
    lane = lane_index()
    flipped = lax.axis_index("col") >= 16

    def fill(to_north, to_south):
        for f in range(SENT):
            to_north[HALO * f : HALO * f + HALO] = fields[f, ROWS - HALO : ROWS]
            to_south[HALO * f : HALO * f + HALO] = fields[f, 0:HALO]
        for pair in range(SENT // 2):
            north = south = None
            for member in range(2):
                f = 2 * pair + member
                base = 64 * member
                a = from_west[8 * f : 8 * f + 8]
                b = from_east[8 * f : 8 * f + 8]
                here = lane >= base
                there = lane >= base + 32
                n = jnp.where(there, turned(b, base + 32 - 96), turned(a, base - 96))
                s = jnp.where(there, turned(b, base + 32), turned(a, base))
                north = n if member == 0 else jnp.where(here, n, north)
                south = s if member == 0 else jnp.where(here, s, south)
            at = SENT * HALO + 8 * pair
            to_north[at : at + 8] = north
            to_south[at : at + 8] = south

    @pl.when(flipped)
    def _():
        fill(downward, upward)

    @pl.when(jnp.logical_not(flipped))
    def _():
        fill(upward, downward)


def stencil_masks():
    lane, row = lane_index(), row_index()
    is_top = lax.axis_index("row") == 7
    top_rows = (jnp.where(is_top, 1, 0) + jnp.zeros((8, LANES), jnp.int32)) == 1
    return lane == 0, lane == LANES - 1, row, top_rows


def assemble(fields, from_west, from_east, from_below, from_above, held):
    is_top = lax.axis_index("row") == 7
    flipped = jnp.where(lax.axis_index("col") >= 16, 1, 0) + jnp.zeros((8, LANES), jnp.int32) == 1
    lane = lane_index()
    row = row_index()
    first, last, low = lane == 0, lane == LANES - 1, lane < 64

    def south(at):
        return jnp.where(flipped, from_above[at : at + 8], from_below[at : at + 8])

    def north(at):
        return jnp.where(flipped, from_below[at : at + 8], from_above[at : at + 8])

    def side_rows(message, f, a):
        base = 64 * (f % 2)
        corner = message(SENT * HALO + 8 * (f // 2))
        return jnp.where(low, turned(corner, -(base + 32 + 16 * a)), turned(corner, 112 - base - 16 * a))

    for f in range(SENT):
        a, b = from_west[8 * f : 8 * f + 8], from_east[8 * f : 8 * f + 8]
        for g in range(8):
            at = PAD + HALO + 8 * g
            held[f, 0, at : at + 8] = fields[f, 8 * g : 8 * g + 8]
            held[f, 1, at : at + 8] = jnp.where(low, turned(b, -16 * g), turned(a, 112 - 16 * g))
        for g in range(2):
            at = PAD + 8 * g
            held[f, 0, at : at + 8] = south(HALO * f + 8 * g)
            held[f, 1, at : at + 8] = side_rows(south, f, g)

    @pl.when(jnp.logical_not(is_top))
    def _():
        for f in range(SENT):
            for g in range(2):
                at = TOP + 8 * g
                held[f, 0, at : at + 8] = north(HALO * f + 8 * g)
                held[f, 1, at : at + 8] = side_rows(north, f, g)

    @pl.when(is_top)
    def _():
        def rotated(value):
            value = jnp.take_along_axis(value, LANES - 1 - lane, axis=1)
            return jnp.take_along_axis(value, 7 - row, axis=0)

        for f in range(SENT):
            for g in range(2):
                source = 1 - g
                main = rotated(north(HALO * f + 8 * source))
                side = rotated(side_rows(north, f, source))
                if f in MOVING:
                    main, side = east(main, side, last)
                    if f in NEGATED:
                        main, side = -main, -side
                    at = TOP + 8 * g
                else:
                    at = TOP + 1 + 8 * g
                held[f, 0, at : at + 8] = main
                held[f, 1, at : at + 8] = side
                if f in (HW, HH):
                    main, side = east(main, side, last)
                    own = HWV if f == HW else HHV
                    held[own, 0, TOP + 8 * g : TOP + 8 * g + 8] = main
                    held[own, 1, TOP + 8 * g : TOP + 8 * g + 8] = side

    for g in range(12):
        at = PAD + 8 * g
        for t in range(2):
            scale = held[AA, t, at : at + 8]
            inertia = held[INE, t, at : at + 8]
            held[AA, t, at : at + 8] = (inertia + 1.0) * scale
            held[BB, t, at : at + 8] = (inertia * (1.0 / 32.0)) * scale
            if g < 10:
                held[HWV, t, at : at + 8] = held[HW, t, at : at + 8]
                held[HHV, t, at : at + 8] = held[HH, t, at : at + 8]
        velocity_sums(
            held,
            at,
            held[U, 0, at : at + 8],
            held[U, 1, at : at + 8],
            held[V, 0, at : at + 8],
            held[V, 1, at : at + 8],
            first,
        )

    @pl.when(jnp.logical_not(is_top))
    def _():
        for t in range(2):
            held[HWV, t, TOP : TOP + HALO] = held[HW, t, TOP : TOP + HALO]
            held[HHV, t, TOP : TOP + HALO] = held[HH, t, TOP : TOP + HALO]


def velocity_sums(held, at, um, us, vm, vs, first):
    wum, wus = west(um, us, first)
    wvm, wvs = west(vm, vs, first)
    for t, (x, wx, y, wy) in enumerate(((um, wum, vm, wvm), (us, wus, vs, wvs))):
        held[DU, t, at : at + 8] = x - wx
        held[SU, t, at : at + 8] = x + wx
        held[DV, t, at : at + 8] = y - wy
        held[SV, t, at : at + 8] = y + wy


def stress_rows(held, at, last):
    fresh = []
    for t in range(2):
        here = lambda f: held[f, t, at : at + 8]
        below = lambda f: held[f, t, at - 1 : at + 7]
        hw, hh = here(HW), here(HH)
        gux = hw * (here(DU) + below(DU))
        guy = hh * (here(SU) - below(SU))
        gvx = hw * (here(DV) + below(DV))
        gvy = hh * (here(SV) - below(SV))
        divergence = gux + gvy
        tension = gux - gvy
        shearing = guy + gvx
        deform = jnp.sqrt(
            divergence * divergence + 0.25 * (tension * tension + shearing * shearing)
        )
        viscous = here(STR) / (deform + 0.5)
        quarter = 0.25 * viscous
        s1 = here(S1) * (2.0 / 3.0) + viscous * (divergence - deform)
        s2 = here(S2) * (2.0 / 3.0) + quarter * tension
        s12 = here(S12) * (2.0 / 3.0) + quarter * shearing
        held[S1, t, at : at + 8] = s1
        held[S2, t, at : at + 8] = s2
        held[S12, t, at : at + 8] = s12
        fresh.append((s1 + s2, s1 - s2, s12))
    (pm, mm, qm), (ps, ms, qs) = fresh
    epm, eps = east(pm, ps, last)
    emm, ems = east(mm, ms, last)
    eqm, eqs = east(qm, qs, last)
    for t, (p, ep, m, em, q, eq) in enumerate(
        ((pm, epm, mm, emm, qm, eqm), (ps, eps, ms, ems, qs, eqs))
    ):
        held[DP, t, at : at + 8] = ep - p
        held[AM, t, at : at + 8] = em + m
        held[DS, t, at : at + 8] = eq - q
        held[AS, t, at : at + 8] = eq + q


def velocity_rows(held, at, first, row, top_rows):
    fresh = []
    for t in range(2):
        here = lambda f: held[f, t, at : at + 8]

        def pair(f):
            own, above = here(f), held[f, t, at + 1 : at + 9]
            if at == TOP - 8:
                above = jnp.where((row == 7) & top_rows, held[f, t, at + 2 : at + 10], above)
            if at == TOP:
                own = jnp.where((row == 0) & top_rows, held[f, t, at - 1 : at + 7], own)
            return own, above

        hw, hh = here(HWV), here(HHV)
        dp, ndp = pair(DP)
        ds, nds = pair(DS)
        as_, nas = pair(AS)
        am, nam = pair(AM)
        inertia, a, b = here(INE), here(AA), here(BB)
        x = inertia * here(U) + (hw * (dp + ndp) + hh * (nas - as_))
        y = inertia * here(V) + (hw * (ds + nds) + hh * (nam - am))
        u = a * x + b * y + here(KU)
        v = a * y - b * x + here(KV)
        held[U, t, at : at + 8] = u
        held[V, t, at : at + 8] = v
        fresh.append((u, v))
    (um, vm), (us, vs) = fresh
    velocity_sums(held, at, um, us, vm, vs, first)


def subcycles(held, start, stop, lo, hi):
    first, last, row, top_rows = stencil_masks()

    def body(_, carry):
        for g in range(lo, hi):
            stress_rows(held, PAD + 8 * g, last)
        for g in range(lo, hi):
            velocity_rows(held, PAD + 8 * g, first, row, top_rows)
        return carry

    lax.fori_loop(start, stop, body, 0)


def place_of(me, which):
    chip, core = me // 2, me % 2
    step = 1 - 2 * core
    if which >= 4:
        core = 1 - core
        which -= 4
        step = -step
    chips = (chip, lax.rem(chip - step + 4, 4), lax.rem(chip + step + 4, 4), lax.rem(chip + 2, 4))
    return (2 * chips[which] + core) * ROWS


def into(out, ref, place, sem):
    return pltpu.make_async_copy(ref, out.at[0, :, pl.ds(place, ROWS), :], sem)


def first_half_kernel(
    fields, from_west, from_east, from_below, from_above, snap, writer_hbm, held, out, flag, writer, zero, sems
):
    me = lax.axis_index("row")
    read = pltpu.make_async_copy(writer_hbm, writer, sems.at[8])
    read.start()
    zero[...] = jnp.zeros_like(zero)
    assemble(fields, from_west, from_east, from_below, from_above, held)
    read.wait()
    mine = writer[lax.axis_index("col")] == me
    flag[...] = jnp.where(mine, 1, 0) + jnp.zeros((8, LANES), jnp.int32)
    zeros = [into(out, zero, n * ROWS, sems.at[n]) for n in range(8)]
    own = into(out, snap, place_of(me, 0), sems.at[0])

    @pl.when(mine)
    def _():
        own.start()

    @pl.when(jnp.logical_not(mine))
    def _():
        for copy in zeros:
            copy.start()

    subcycles(held, 0, 5, 0, 12)

    @pl.when(mine)
    def _():
        own.wait()

    @pl.when(jnp.logical_not(mine))
    def _():
        for copy in zeros:
            copy.wait()


def second_half_kernel(state, out_in, flag, near, near_back, vel, stress, held, out, sems):
    me = lax.axis_index("row")
    mine = jnp.max(flag[...]) == 1
    copies = [
        into(out, near, place_of(me, 1), sems.at[0]),
        into(out, near_back, place_of(me, 2), sems.at[1]),
    ]

    @pl.when(mine)
    def _():
        for copy in copies:
            copy.start()

    subcycles(held, 5, SUB, 1, 11)
    at = PAD + HALO
    vel[0] = held[U, 0, at : at + ROWS]
    vel[1] = held[V, 0, at : at + ROWS]
    stress[0] = 2.0 * held[S1, 0, at : at + ROWS]
    stress[1] = 2.0 * held[S2, 0, at : at + ROWS]
    stress[2] = held[S12, 0, at : at + ROWS]

    @pl.when(mine)
    def _():
        for copy in copies:
            copy.wait()


def last_kernel(out_in, flag, far, partner, partner_far, out, sems):
    me = lax.axis_index("row")
    mine = jnp.max(flag[...]) == 1

    @pl.when(mine)
    def _():
        copies = [
            into(out, far, place_of(me, 3), sems.at[0]),
            into(out, partner.at[0], place_of(me, 4), sems.at[1]),
            into(out, partner.at[1], place_of(me, 5), sems.at[2]),
            into(out, partner.at[2], place_of(me, 6), sems.at[3]),
            into(out, partner_far, place_of(me, 7), sems.at[4]),
        ]
        for copy in copies:
            copy.start()
        for copy in copies:
            copy.wait()


def join_kernel(own, near, near_back, joined):
    joined[0] = own[...]
    joined[1] = near[...]
    joined[2] = near_back[...]


def vmem():
    return pl.BlockSpec(memory_space=pltpu.VMEM)


def shape(*dims):
    return jax.ShapeDtypeStruct(dims, jnp.float32)


def grant(mebibytes):
    return pltpu.CompilerParams(vmem_limit_bytes=mebibytes << 20)


def step(
    velocity_start,
    stress_start,
    wind_stress,
    ocean_current,
    ice_area,
    ice_volume,
    inverse_width,
    inverse_height,
    land_block,
    ice_block,
    writer,
):
    fields, to_west, to_east, snap = pl.pallas_call(
        prepare_kernel,
        out_shape=(
            shape(SENT, ROWS, LANES),
            shape(SENT * 8, LANES),
            shape(SENT * 8, LANES),
            shape(10, ROWS, LANES),
        ),
        in_specs=[pl.BlockSpec(memory_space=pltpu.HBM)] * 10,
        out_specs=(vmem(),) * 4,
        scratch_shapes=[
            pltpu.VMEM((2, ROWS, LANES), jnp.float32),
            pltpu.VMEM((3, ROWS, LANES), jnp.float32),
            pltpu.VMEM((2, ROWS, LANES), jnp.float32),
            pltpu.VMEM((2, ROWS, LANES), jnp.float32),
            pltpu.VMEM((ROWS, LANES), jnp.float32),
            pltpu.VMEM((ROWS, LANES), jnp.float32),
            pltpu.VMEM((4, 16), jnp.int32),
            pltpu.VMEM((4, 16), jnp.int32),
            pltpu.SemaphoreType.DMA((10,)),
        ],
        compiler_params=grant(8),
        name="prepare",
    )(
        *(
            pltpu.with_memory_space_constraint(value, pltpu.HBM)
            for value in (
                velocity_start,
                stress_start,
                wind_stress,
                ocean_current,
                ice_area,
                ice_volume,
                inverse_width,
                inverse_height,
                land_block.T,
                ice_block.T,
            )
        )
    )
    along = [(r, (r + 2 - 4 * (r % 2)) % 8) for r in range(8)]
    against = [(r, (r - 2 + 4 * (r % 2)) % 8) for r in range(8)]
    partner = [(r, r ^ 1) for r in range(8)]
    eastward = [(c, (c + 1) % 32) for c in range(32)]
    westward = [(c, (c - 1) % 32) for c in range(32)]
    upward = []
    for c in range(16):
        line = [32 * r + c for r in range(8)] + [32 * (7 - r) + 31 - c for r in range(8)]
        upward += list(zip(line[:-1], line[1:]))
    downward = [(b, a) for a, b in upward]

    near = lax.ppermute(snap, "row", along)
    from_west = lax.ppermute(to_east, "col", eastward)
    from_east = lax.ppermute(to_west, "col", westward)
    near_back = lax.ppermute(snap, "row", against)

    to_above, to_below = pl.pallas_call(
        rows_kernel,
        out_shape=(shape(MESSAGE, LANES),) * 2,
        in_specs=[vmem()] * 3,
        out_specs=(vmem(),) * 2,
        compiler_params=grant(8),
        cost_estimate=pl.CostEstimate(flops=1000000, bytes_accessed=1000000, transcendentals=0),
        name="rows",
    )(fields, from_west, from_east)
    from_below = lax.ppermute(to_above, ("row", "col"), upward)
    from_above = lax.ppermute(to_below, ("row", "col"), downward)
    far = lax.ppermute(near, "row", along)

    hbm = lambda: pl.BlockSpec(memory_space=pl.ANY)
    state, restart, flag = pl.pallas_call(
        first_half_kernel,
        out_shape=(
            shape(HELD, 2, TALL, LANES),
            shape(1, 10, 8 * ROWS, LANES),
            jax.ShapeDtypeStruct((8, LANES), jnp.int32),
        ),
        in_specs=[vmem()] * 5 + [hbm(), hbm()],
        out_specs=(vmem(), hbm(), vmem()),
        scratch_shapes=[
            pltpu.SMEM((32,), jnp.int32),
            pltpu.VMEM((10, ROWS, LANES), jnp.float32),
            pltpu.SemaphoreType.DMA((9,)),
        ],
        compiler_params=grant(16),
        cost_estimate=pl.CostEstimate(flops=20000000, bytes_accessed=2000000, transcendentals=0),
        name="first_half",
    )(
        fields,
        from_west,
        from_east,
        from_below,
        from_above,
        snap,
        pltpu.with_memory_space_constraint(writer, pltpu.HBM),
    )

    joined = pl.pallas_call(
        join_kernel,
        out_shape=shape(3, 10, ROWS, LANES),
        in_specs=[vmem()] * 3,
        out_specs=vmem(),
        compiler_params=grant(8),
        name="join",
    )(snap, near, near_back)
    partner_blocks = lax.ppermute(joined, "row", partner)

    velocity, stress, _, restart = pl.pallas_call(
        second_half_kernel,
        out_shape=(
            shape(2, ROWS, LANES),
            shape(3, ROWS, LANES),
            shape(HELD, 2, TALL, LANES),
            shape(1, 10, 8 * ROWS, LANES),
        ),
        in_specs=[vmem(), hbm(), vmem(), hbm(), hbm()],
        out_specs=(vmem(), vmem(), vmem(), hbm()),
        input_output_aliases={0: 2, 1: 3},
        scratch_shapes=[pltpu.SemaphoreType.DMA((2,))],
        compiler_params=grant(8),
        cost_estimate=pl.CostEstimate(flops=20000000, bytes_accessed=2000000, transcendentals=0),
        name="second_half",
    )(state, restart, flag, near, near_back)
    partner_far = lax.ppermute(far, "row", partner)

    restart = pl.pallas_call(
        last_kernel,
        out_shape=shape(1, 10, 8 * ROWS, LANES),
        in_specs=[hbm(), vmem(), hbm(), hbm(), hbm()],
        out_specs=hbm(),
        input_output_aliases={0: 0},
        scratch_shapes=[pltpu.SemaphoreType.DMA((5,))],
        compiler_params=grant(4),
        name="last",
    )(restart, flag, far, partner_blocks, partner_far)
    return (velocity, stress, restart)


def solution(mesh):
    return jax.shard_map(
        step,
        mesh=mesh,
        in_specs=(
            P(None, "row", "col"),
            P(None, "row", "col"),
            P(None, "row", "col"),
            P(None, "row", "col"),
            P(None, "row", "col"),
            P(None, "row", "col"),
            P("row", "col"),
            P("row", "col"),
            P("row", "col"),
            P("row", "col"),
            P(),
        ),
        out_specs=(P(None, "row", "col"), P(None, "row", "col"), P("row", None, None, "col")),
        check_vma=False,
    )
```

time: 52.3 us -> 53.9 us (1.031)
  the two profiles are of different devices: /device:TPU:1 before, /device:TPU:7 now
where the time goes in v2:
time: 53.9 us; the launch traced here: 53.7 us
  waiting for transfers between devices  24.1 us (45%)
  starting transfers between devices  21 us (39%)
  Pallas kernels  7.94 us (15%)
  between operations  0.71 us (1%)
    ppermute x1, waiting for transfers between devices, step(): from_above = lax.ppermute(to_below, ('row', 'col'), downward)  8.04 us
    ppermute x1, waiting for transfers between devices, step(): far = lax.ppermute(near, 'row', along)  7.14 us
    ppermute x1, starting transfers between devices, step(): from_below = lax.ppermute(to_above, ('row', 'col'), upward)  6.7 us
    ppermute x1, starting transfers between devices, step(): from_east = lax.ppermute(to_west, 'col', westward)  6.39 us
    ppermute x1, waiting for transfers between devices, step(): near = lax.ppermute(snap, 'row', along)  4.94 us
    pallas_call x1, Pallas kernels, step(): pl.pallas_call(second_half_kernel, out_shape=(shape(2, ROWS, LANES), shap...  3.14 us
    pallas_call x1, Pallas kernels, step(): pl.pallas_call(first_half_kernel, out_shape=(shape(HELD, 2, TALL, LANES),...  2.66 us
    ppermute x1, waiting for transfers between devices, step(): near_back = lax.ppermute(snap, 'row', against)  2.22 us
  transfers between devices with their start and end apart: 9, of which 6 were waited for; matrix products, arithmetic and copies ran while one was open for 0% of the time, Pallas kernels for 11%

profile of v2, /device:TPU:7, one launch (start us, length us, event | category | flops | bytes accessed | tf_op | source)
XLA Modules:
  0.0 53.7 jit_solution(9867734294360362691)
XLA Ops:
  0.6 1.7 %prepare.1 = (f32[12,64,128]{2,1,0:T(8,128)S(1)}, f32[96,128]{1,0:T(8,128)S(1)}, f32[96,128]{1,0:T(8,128)S(1)}, f32[10,64,128]{2,1,0:T(8,128)S(1)}) custom-call(f32[2,64,128]{2,1,0:T(8,128)} %vel_hbm.1, f32[3,64,128]{2,1,0:T(8,128)} %stress_hbm.1, f32[2,64,128]{2,1,0:T(8,128)} %wind_hbm.1, f32[2,64,128]{2,1,0:T(8,128)} %ocean_hbm.1, f32[5,64,128]{2,1,0:T(8,128)} %area_hbm.1, ...), custom_call_target="tpu_custom_call" | custom-call | tf_op jit(solution)/shard_map/prepare/pallas_call | solution.py:491
  2.4 0.6 %collective-permute-start.4 = (f32[10,64,128]{2,1,0:T(8,128)S(1)}, f32[10,64,128]{2,1,0:T(8,128)S(1)}, u32[]{:S(2)}, u32[]{:S(2)}) collective-permute-start(f32[10,64,128]{2,1,0:T(8,128)S(1)} %get-tuple-element.20.snap.own), channel_id=1, source_target_pairs={{0,64},{32,224},{64,128},{96,32},{128,192},{160,96},{192,0},{224,1... | collective-permute-start | bytes 983048 | tf_op jit(solution)/shard_map/ppermute | solution.py:542
  3.0 2.1 %collective-permute-start.5 = (f32[10,64,128]{2,1,0:T(8,128)S(1)}, f32[10,64,128]{2,1,0:T(8,128)S(1)}, u32[]{:S(2)}, u32[]{:S(2)}) collective-permute-start(f32[10,64,128]{2,1,0:T(8,128)S(1)} %get-tuple-element.20.snap.own), channel_id=1, source_target_pairs={{0,192},{32,96},{64,0},{96,160},{128,64},{160,224},{192,128},{224,... | collective-permute-start | bytes 983048 | tf_op jit(solution)/shard_map/ppermute | solution.py:545
  5.1 4.9 %collective-permute-done.4.near = f32[10,64,128]{2,1,0:T(8,128)S(1)} collective-permute-done((f32[10,64,128]{2,1,0:T(8,128)S(1)}, f32[10,64,128]{2,1,0:T(8,128)S(1)}, u32[]{:S(2)}, u32[]{:S(2)}) %collective-permute-start.4) | collective-permute-done | bytes 327712 | tf_op jit(solution)/shard_map/ppermute | solution.py:542
  10.0 2.2 %collective-permute-done.5.near_back = f32[10,64,128]{2,1,0:T(8,128)S(1)} collective-permute-done((f32[10,64,128]{2,1,0:T(8,128)S(1)}, f32[10,64,128]{2,1,0:T(8,128)S(1)}, u32[]{:S(2)}, u32[]{:S(2)}) %collective-permute-start.5) | collective-permute-done | bytes 327712 | tf_op jit(solution)/shard_map/ppermute | solution.py:545
  12.3 0.1 join.1
  12.3 1.6 %collective-permute-start.7 = (f32[3,10,64,128]{3,2,1,0:T(8,128)S(1)}, f32[3,10,64,128]{3,2,1,0:T(8,128)S(1)}, u32[]{:S(2)}, u32[]{:S(2)}) collective-permute-start(f32[3,10,64,128]{3,2,1,0:T(8,128)S(1)} %join.1), channel_id=1, source_target_pairs={{0,32},{32,0},{64,96},{96,64},{128,160},{160,128},{192,224},{224,1... | collective-permute-start | bytes 2949128 | tf_op jit(solution)/shard_map/ppermute | solution.py:596
  13.9 0.0 collective-permute-start.6
  13.9 7.1 %collective-permute-done.6.far = f32[10,64,128]{2,1,0:T(8,128)S(1)} collective-permute-done((f32[10,64,128]{2,1,0:T(8,128)S(1)}, f32[10,64,128]{2,1,0:T(8,128)S(1)}, u32[]{:S(2)}, u32[]{:S(2)}) %collective-permute-start.6) | collective-permute-done | bytes 327712 | tf_op jit(solution)/shard_map/ppermute | solution.py:558
  21.1 0.5 collective-permute-start.8
  21.6 1.2 %collective-permute-start = (f32[96,128]{1,0:T(8,128)S(1)}, f32[96,128]{1,0:T(8,128)S(1)}, u32[]{:S(2)}, u32[]{:S(2)}) collective-permute-start(f32[96,128]{1,0:T(8,128)S(1)} %get-tuple-element.16), channel_id=1, source_target_pairs={{0,1},{1,2},{2,3},{3,4},{4,5},{5,6},{6,7},{7,8},{8,9},{9,10},{10,1... | collective-permute-start | bytes 147464 | tf_op jit(solution)/shard_map/ppermute | solution.py:543
  22.7 6.4 %collective-permute-start.1 = (f32[96,128]{1,0:T(8,128)S(1)}, f32[96,128]{1,0:T(8,128)S(1)}, u32[]{:S(2)}, u32[]{:S(2)}) collective-permute-start(f32[96,128]{1,0:T(8,128)S(1)} %get-tuple-element.17), channel_id=1, source_target_pairs={{0,31},{1,0},{2,1},{3,2},{4,3},{5,4},{6,5},{7,6},{8,7},{9,8},{10,9... | collective-permute-start | bytes 147464 | tf_op jit(solution)/shard_map/ppermute | solution.py:544
  29.1 1.5 %collective-permute-done.from_west = f32[96,128]{1,0:T(8,128)S(1)} collective-permute-done((f32[96,128]{1,0:T(8,128)S(1)}, f32[96,128]{1,0:T(8,128)S(1)}, u32[]{:S(2)}, u32[]{:S(2)}) %collective-permute-start) | collective-permute-done | bytes 49184 | tf_op jit(solution)/shard_map/ppermute | solution.py:543
  30.6 0.0 collective-permute-done.1.from_east
  30.6 0.1 rows.1
  30.7 6.7 %collective-permute-start.2 = (f32[240,128]{1,0:T(8,128)S(1)}, f32[240,128]{1,0:T(8,128)S(1)}, u32[]{:S(2)}, u32[]{:S(2)}) collective-permute-start(f32[240,128]{1,0:T(8,128)S(1)} %get-tuple-element.18), channel_id=1, source_target_pairs={{0,32},{32,64},{64,96},{96,128},{128,160},{160,192},{192,224},{224... | collective-permute-start | bytes 368648 | tf_op jit(solution)/shard_map/ppermute | solution.py:556
  37.4 1.9 %collective-permute-start.3 = (f32[240,128]{1,0:T(8,128)S(1)}, f32[240,128]{1,0:T(8,128)S(1)}, u32[]{:S(2)}, u32[]{:S(2)}) collective-permute-start(f32[240,128]{1,0:T(8,128)S(1)} %get-tuple-element.19), channel_id=1, source_target_pairs={{32,0},{64,32},{96,64},{128,96},{160,128},{192,160},{224,192},{255... | collective-permute-start | bytes 368648 | tf_op jit(solution)/shard_map/ppermute | solution.py:557
  39.3 0.2 collective-permute-done.2.from_below
  39.6 8.0 %collective-permute-done.3.from_above = f32[240,128]{1,0:T(8,128)S(1)} collective-permute-done((f32[240,128]{1,0:T(8,128)S(1)}, f32[240,128]{1,0:T(8,128)S(1)}, u32[]{:S(2)}, u32[]{:S(2)}) %collective-permute-start.3) | collective-permute-done | bytes 122912 | tf_op jit(solution)/shard_map/ppermute | solution.py:557
  47.6 2.7 %first_half.1 = (f32[23,2,112,128]{3,2,1,0:T(8,128)S(1)}, f32[1,10,512,128]{3,2,1,0:T(8,128)}, s32[8,128]{1,0:T(8,128)S(1)}) custom-call(f32[12,64,128]{2,1,0:T(8,128)S(1)} %get-tuple-element.15.fields, f32[96,128]{1,0:T(8,128)S(1)} %collective-permute-done.from_west, f32[96,128]{1,0:T(8,128)S(1)} %collective-permute-done.1.from_east, ...), custom_call_target="tpu_custom_call" | custom-call | flops 20000000 | bytes 2000000 | tf_op jit(solution)/shard_map/first_half/pallas_call | solution.py:561
  50.3 3.1 %second_half.1 = (f32[2,64,128]{2,1,0:T(8,128)}, f32[3,64,128]{2,1,0:T(8,128)}, f32[23,2,112,128]{3,2,1,0:T(8,128)S(1)}, f32[1,10,512,128]{3,2,1,0:T(8,128)}) custom-call(f32[23,2,112,128]{3,2,1,0:T(8,128)S(1)} %get-tuple-element.21.state, f32[1,10,512,128]{3,2,1,0:T(8,128)} %get-tuple-element.22.out_in, ...), custom_call_target="tpu_custom_call", output_to_operand_aliasing={{2}: (0, {}), {3}: (1, {})} | custom-call | flops 20000000 | bytes 2000000 | tf_op jit(solution)/shard_map/second_half/pallas_call | solution.py:598
  53.4 0.0 collective-permute-done.8.partner_far
  53.5 0.0 collective-permute-done.7.partner
  53.5 0.3 last.1
Async XLA Ops:
  2.4 7.7 %collective-permute-start.4 = (f32[10,64,128]{2,1,0:T(8,128)S(1)}, f32[10,64,128]{2,1,0:T(8,128)S(1)}, u32[]{:S(2)}, u32[]{:S(2)}) collective-permute-start(f32[10,64,128]{2,1,0:T(8,128)S(1)} %get-tuple-element.20.snap.own), channel_id=1, source_target_pairs={{0,64},{32,224},{64,128},{96,32},{128,192},{160,96},{192,0},{224,1... | collective-permute-start | bytes 983048 | tf_op jit(solution)/shard_map/ppermute | solution.py:542
  3.0 9.3 %collective-permute-start.5 = (f32[10,64,128]{2,1,0:T(8,128)S(1)}, f32[10,64,128]{2,1,0:T(8,128)S(1)}, u32[]{:S(2)}, u32[]{:S(2)}) collective-permute-start(f32[10,64,128]{2,1,0:T(8,128)S(1)} %get-tuple-element.20.snap.own), channel_id=1, source_target_pairs={{0,192},{32,96},{64,0},{96,160},{128,64},{160,224},{192,128},{224,... | collective-permute-start | bytes 983048 | tf_op jit(solution)/shard_map/ppermute | solution.py:545
  12.3 41.1 %collective-permute-start.7 = (f32[3,10,64,128]{3,2,1,0:T(8,128)S(1)}, f32[3,10,64,128]{3,2,1,0:T(8,128)S(1)}, u32[]{:S(2)}, u32[]{:S(2)}) collective-permute-start(f32[3,10,64,128]{3,2,1,0:T(8,128)S(1)} %join.1), channel_id=1, source_target_pairs={{0,32},{32,0},{64,96},{96,64},{128,160},{160,128},{192,224},{224,1... | collective-permute-start | bytes 2949128 | tf_op jit(solution)/shard_map/ppermute | solution.py:596
  13.9 7.1 %collective-permute-start.6 = (f32[10,64,128]{2,1,0:T(8,128)S(1)}, f32[10,64,128]{2,1,0:T(8,128)S(1)}, u32[]{:S(2)}, u32[]{:S(2)}) collective-permute-start(f32[10,64,128]{2,1,0:T(8,128)S(1)} %collective-permute-done.4.near), channel_id=1, source_target_pairs={{0,64},{32,224},{64,128},{96,32},{128,192},{160,96},{192,0},{224,1... | collective-permute-start | bytes 983048 | tf_op jit(solution)/shard_map/ppermute | solution.py:558
  21.1 32.4 %collective-permute-start.8 = (f32[10,64,128]{2,1,0:T(8,128)S(1)}, f32[10,64,128]{2,1,0:T(8,128)S(1)}, u32[]{:S(2)}, u32[]{:S(2)}) collective-permute-start(f32[10,64,128]{2,1,0:T(8,128)S(1)} %collective-permute-done.6.far), channel_id=1, source_target_pairs={{0,32},{32,0},{64,96},{96,64},{128,160},{160,128},{192,224},{224,1... | collective-permute-start | bytes 983048 | tf_op jit(solution)/shard_map/ppermute | solution.py:614
  21.6 9.0 %collective-permute-start = (f32[96,128]{1,0:T(8,128)S(1)}, f32[96,128]{1,0:T(8,128)S(1)}, u32[]{:S(2)}, u32[]{:S(2)}) collective-permute-start(f32[96,128]{1,0:T(8,128)S(1)} %get-tuple-element.16), channel_id=1, source_target_pairs={{0,1},{1,2},{2,3},{3,4},{4,5},{5,6},{6,7},{7,8},{8,9},{9,10},{10,1... | collective-permute-start | bytes 147464 | tf_op jit(solution)/shard_map/ppermute | solution.py:543
  22.7 7.9 %collective-permute-start.1 = (f32[96,128]{1,0:T(8,128)S(1)}, f32[96,128]{1,0:T(8,128)S(1)}, u32[]{:S(2)}, u32[]{:S(2)}) collective-permute-start(f32[96,128]{1,0:T(8,128)S(1)} %get-tuple-element.17), channel_id=1, source_target_pairs={{0,31},{1,0},{2,1},{3,2},{4,3},{5,4},{6,5},{7,6},{8,7},{9,8},{10,9... | collective-permute-start | bytes 147464 | tf_op jit(solution)/shard_map/ppermute | solution.py:544
  30.7 8.9 %collective-permute-start.2 = (f32[240,128]{1,0:T(8,128)S(1)}, f32[240,128]{1,0:T(8,128)S(1)}, u32[]{:S(2)}, u32[]{:S(2)}) collective-permute-start(f32[240,128]{1,0:T(8,128)S(1)} %get-tuple-element.18), channel_id=1, source_target_pairs={{0,32},{32,64},{64,96},{96,128},{128,160},{160,192},{192,224},{224... | collective-permute-start | bytes 368648 | tf_op jit(solution)/shard_map/ppermute | solution.py:556
  37.4 10.2 %collective-permute-start.3 = (f32[240,128]{1,0:T(8,128)S(1)}, f32[240,128]{1,0:T(8,128)S(1)}, u32[]{:S(2)}, u32[]{:S(2)}) collective-permute-start(f32[240,128]{1,0:T(8,128)S(1)} %get-tuple-element.19), channel_id=1, source_target_pairs={{32,0},{64,32},{96,64},{128,96},{160,128},{192,160},{224,192},{255... | collective-permute-start | bytes 368648 | tf_op jit(solution)/shard_map/ppermute | solution.py:557

commit v3 on v2

--- a/solution.py
+++ b/solution.py
@@ -7,6 +7,7 @@
 
 
 SUB = 12
+SPLIT = 7
 ROWS = 64
 LANES = 128
 HALO = 16
@@ -400,6 +401,7 @@
             copy.start()
 
     subcycles(held, 0, 5, 0, 12)
+    subcycles(held, 5, SPLIT, 1, 11)
 
     @pl.when(mine)
     def _():
@@ -411,12 +413,13 @@
             copy.wait()
 
 
-def second_half_kernel(state, out_in, flag, near, near_back, vel, stress, held, out, sems):
+def second_half_kernel(state, out_in, flag, near, near_back, far, vel, stress, held, out, sems):
     me = lax.axis_index("row")
     mine = jnp.max(flag[...]) == 1
     copies = [
         into(out, near, place_of(me, 1), sems.at[0]),
         into(out, near_back, place_of(me, 2), sems.at[1]),
+        into(out, far, place_of(me, 3), sems.at[2]),
     ]
 
     @pl.when(mine)
@@ -424,7 +427,7 @@
         for copy in copies:
             copy.start()
 
-    subcycles(held, 5, SUB, 1, 11)
+    subcycles(held, SPLIT, SUB, 1, 11)
     at = PAD + HALO
     vel[0] = held[U, 0, at : at + ROWS]
     vel[1] = held[V, 0, at : at + ROWS]
@@ -438,29 +441,22 @@
             copy.wait()
 
 
-def last_kernel(out_in, flag, far, partner, partner_far, out, sems):
+def last_kernel(out_in, flag, partner, out, sems):
     me = lax.axis_index("row")
     mine = jnp.max(flag[...]) == 1
 
     @pl.when(mine)
     def _():
-        copies = [
-            into(out, far, place_of(me, 3), sems.at[0]),
-            into(out, partner.at[0], place_of(me, 4), sems.at[1]),
-            into(out, partner.at[1], place_of(me, 5), sems.at[2]),
-            into(out, partner.at[2], place_of(me, 6), sems.at[3]),
-            into(out, partner_far, place_of(me, 7), sems.at[4]),
-        ]
+        copies = [into(out, partner.at[n], place_of(me, 4 + n), sems.at[n]) for n in range(4)]
         for copy in copies:
             copy.start()
         for copy in copies:
             copy.wait()
 
 
-def join_kernel(own, near, near_back, joined):
-    joined[0] = own[...]
-    joined[1] = near[...]
-    joined[2] = near_back[...]
+def join_kernel(own, near, near_back, far, joined):
+    for n, block in enumerate((own, near, near_back, far)):
+        joined[n] = block[...]
 
 
 def vmem():
@@ -587,12 +583,12 @@
 
     joined = pl.pallas_call(
         join_kernel,
-        out_shape=shape(3, 10, ROWS, LANES),
-        in_specs=[vmem()] * 3,
+        out_shape=shape(4, 10, ROWS, LANES),
+        in_specs=[vmem()] * 4,
         out_specs=vmem(),
         compiler_params=grant(8),
         name="join",
-    )(snap, near, near_back)
+    )(snap, near, near_back, far)
     partner_blocks = lax.ppermute(joined, "row", partner)
 
     velocity, stress, _, restart = pl.pallas_call(
@@ -603,26 +599,25 @@
             shape(HELD, 2, TALL, LANES),
             shape(1, 10, 8 * ROWS, LANES),
         ),
-        in_specs=[vmem(), hbm(), vmem(), hbm(), hbm()],
+        in_specs=[vmem(), hbm(), vmem(), hbm(), hbm(), hbm()],
         out_specs=(vmem(), vmem(), vmem(), hbm()),
         input_output_aliases={0: 2, 1: 3},
-        scratch_shapes=[pltpu.SemaphoreType.DMA((2,))],
+        scratch_shapes=[pltpu.SemaphoreType.DMA((3,))],
         compiler_params=grant(8),
         cost_estimate=pl.CostEstimate(flops=20000000, bytes_accessed=2000000, transcendentals=0),
         name="second_half",
-    )(state, restart, flag, near, near_back)
-    partner_far = lax.ppermute(far, "row", partner)
+    )(state, restart, flag, near, near_back, far)
 
     restart = pl.pallas_call(
         last_kernel,
         out_shape=shape(1, 10, 8 * ROWS, LANES),
-        in_specs=[hbm(), vmem(), hbm(), hbm(), hbm()],
+        in_specs=[hbm(), vmem(), hbm()],
         out_specs=hbm(),
         input_output_aliases={0: 0},
-        scratch_shapes=[pltpu.SemaphoreType.DMA((5,))],
+        scratch_shapes=[pltpu.SemaphoreType.DMA((4,))],
         compiler_params=grant(4),
         name="last",
-    )(restart, flag, far, partner_blocks, partner_far)
+    )(restart, flag, partner_blocks)
     return (velocity, stress, restart)
 
 

time: 53.9 us -> 53 us (0.983)
  waiting for transfers between devices: 24.1 us -> 22 us
  starting transfers between devices: 21 us -> 22.1 us
    ppermute x1, starting transfers between devices: 1.58 us -> 4.22 us  [step(): partner_blocks = lax.ppermute(joined, 'row', partner)]
    ppermute x1, waiting for transfers between devices: 7.14 us -> 4.91 us  [step(): far = lax.ppermute(near, 'row', along)]
    ppermute x1, starting transfers between devices: 1.16 us -> 0.5 us  [step(): from_west = lax.ppermute(to_east, 'col', eastward)]
    pallas_call x1, Pallas kernels: 2.66 us -> 3.31 us  [step(): pl.pallas_call(first_half_kernel, out_shape=(shape(HELD, 2, TALL, LANES),...]
    pallas_call x1, Pallas kernels: 3.14 us -> 2.51 us  [step(): pl.pallas_call(second_half_kernel, out_shape=(shape(2, ROWS, LANES), shap...]
    ppermute x1, waiting for transfers between devices: 1.47 us -> 2.02 us  [step(): from_west = lax.ppermute(to_east, 'col', eastward)]
    ppermute x1, starting transfers between devices: 6.7 us -> 6.15 us  [step(): from_below = lax.ppermute(to_above, ('row', 'col'), upward)]
  transfers between devices with their start and end apart: 9 -> 8, of which waited for: 6 -> 6; matrix products, arithmetic and copies ran while one was open for 0% -> 0% of each run, Pallas kernels for 11% -> 11%
where the time goes in v3:
time: 53 us; the launch traced here: 52.8 us
  starting transfers between devices  22.1 us (42%)
  waiting for transfers between devices  22 us (42%)
  Pallas kernels  7.96 us (15%)
  between operations  0.7 us (1%)
    ppermute x1, waiting for transfers between devices, step(): from_above = lax.ppermute(to_below, ('row', 'col'), downward)  8.04 us
    ppermute x1, starting transfers between devices, step(): from_east = lax.ppermute(to_west, 'col', westward)  6.39 us
    ppermute x1, starting transfers between devices, step(): from_below = lax.ppermute(to_above, ('row', 'col'), upward)  6.15 us
    ppermute x1, waiting for transfers between devices, step(): near = lax.ppermute(snap, 'row', along)  4.94 us
    ppermute x1, waiting for transfers between devices, step(): far = lax.ppermute(near, 'row', along)  4.91 us
    ppermute x1, starting transfers between devices, step(): partner_blocks = lax.ppermute(joined, 'row', partner)  4.22 us
    pallas_call x1, Pallas kernels, step(): pl.pallas_call(first_half_kernel, out_shape=(shape(HELD, 2, TALL, LANES),...  3.31 us
    pallas_call x1, Pallas kernels, step(): pl.pallas_call(second_half_kernel, out_shape=(shape(2, ROWS, LANES), shap...  2.51 us
  transfers between devices with their start and end apart: 8, of which 6 were waited for; matrix products, arithmetic and copies ran while one was open for 0% of the time, Pallas kernels for 11%

profile of v3, /device:TPU:7, one launch (start us, length us, event | category | flops | bytes accessed | tf_op | source)
XLA Modules:
  0.0 52.8 jit_solution(10991143123198053784)
XLA Ops:
  0.6 1.7 %prepare.1 = (f32[12,64,128]{2,1,0:T(8,128)S(1)}, f32[96,128]{1,0:T(8,128)S(1)}, f32[96,128]{1,0:T(8,128)S(1)}, f32[10,64,128]{2,1,0:T(8,128)S(1)}) custom-call(f32[2,64,128]{2,1,0:T(8,128)} %vel_hbm.1, f32[3,64,128]{2,1,0:T(8,128)} %stress_hbm.1, f32[2,64,128]{2,1,0:T(8,128)} %wind_hbm.1, f32[2,64,128]{2,1,0:T(8,128)} %ocean_hbm.1, f32[5,64,128]{2,1,0:T(8,128)} %area_hbm.1, ...), custom_call_target="tpu_custom_call" | custom-call | tf_op jit(solution)/shard_map/prepare/pallas_call | solution.py:487
  2.4 0.6 %collective-permute-start.4 = (f32[10,64,128]{2,1,0:T(8,128)S(1)}, f32[10,64,128]{2,1,0:T(8,128)S(1)}, u32[]{:S(2)}, u32[]{:S(2)}) collective-permute-start(f32[10,64,128]{2,1,0:T(8,128)S(1)} %get-tuple-element.20.snap.own), channel_id=1, source_target_pairs={{0,64},{32,224},{64,128},{96,32},{128,192},{160,96},{192,0},{224,1... | collective-permute-start | bytes 983048 | tf_op jit(solution)/shard_map/ppermute | solution.py:538
  3.0 2.1 %collective-permute-start.5 = (f32[10,64,128]{2,1,0:T(8,128)S(1)}, f32[10,64,128]{2,1,0:T(8,128)S(1)}, u32[]{:S(2)}, u32[]{:S(2)}) collective-permute-start(f32[10,64,128]{2,1,0:T(8,128)S(1)} %get-tuple-element.20.snap.own), channel_id=1, source_target_pairs={{0,192},{32,96},{64,0},{96,160},{128,64},{160,224},{192,128},{224,... | collective-permute-start | bytes 983048 | tf_op jit(solution)/shard_map/ppermute | solution.py:541
  5.1 4.9 %collective-permute-done.4.near = f32[10,64,128]{2,1,0:T(8,128)S(1)} collective-permute-done((f32[10,64,128]{2,1,0:T(8,128)S(1)}, f32[10,64,128]{2,1,0:T(8,128)S(1)}, u32[]{:S(2)}, u32[]{:S(2)}) %collective-permute-start.4) | collective-permute-done | bytes 327712 | tf_op jit(solution)/shard_map/ppermute | solution.py:538
  10.0 0.2 collective-permute-start.6
  10.2 2.1 %collective-permute-done.5.near_back = f32[10,64,128]{2,1,0:T(8,128)S(1)} collective-permute-done((f32[10,64,128]{2,1,0:T(8,128)S(1)}, f32[10,64,128]{2,1,0:T(8,128)S(1)}, u32[]{:S(2)}, u32[]{:S(2)}) %collective-permute-start.5) | collective-permute-done | bytes 327712 | tf_op jit(solution)/shard_map/ppermute | solution.py:541
  12.3 4.9 %collective-permute-done.6.far = f32[10,64,128]{2,1,0:T(8,128)S(1)} collective-permute-done((f32[10,64,128]{2,1,0:T(8,128)S(1)}, f32[10,64,128]{2,1,0:T(8,128)S(1)}, u32[]{:S(2)}, u32[]{:S(2)}) %collective-permute-start.6) | collective-permute-done | bytes 327712 | tf_op jit(solution)/shard_map/ppermute | solution.py:554
  17.2 0.1 join.1
  17.3 4.2 %collective-permute-start.7 = (f32[4,10,64,128]{3,2,1,0:T(8,128)S(1)}, f32[4,10,64,128]{3,2,1,0:T(8,128)S(1)}, u32[]{:S(2)}, u32[]{:S(2)}) collective-permute-start(f32[4,10,64,128]{3,2,1,0:T(8,128)S(1)} %join.1), channel_id=1, source_target_pairs={{0,32},{32,0},{64,96},{96,64},{128,160},{160,128},{192,224},{224,1... | collective-permute-start | bytes 3932168 | tf_op jit(solution)/shard_map/ppermute | solution.py:592
  21.5 0.5 collective-permute-start
  22.0 6.4 %collective-permute-start.1 = (f32[96,128]{1,0:T(8,128)S(1)}, f32[96,128]{1,0:T(8,128)S(1)}, u32[]{:S(2)}, u32[]{:S(2)}) collective-permute-start(f32[96,128]{1,0:T(8,128)S(1)} %get-tuple-element.17), channel_id=1, source_target_pairs={{0,31},{1,0},{2,1},{3,2},{4,3},{5,4},{6,5},{7,6},{8,7},{9,8},{10,9... | collective-permute-start | bytes 147464 | tf_op jit(solution)/shard_map/ppermute | solution.py:540
  28.4 2.0 %collective-permute-done.from_west = f32[96,128]{1,0:T(8,128)S(1)} collective-permute-done((f32[96,128]{1,0:T(8,128)S(1)}, f32[96,128]{1,0:T(8,128)S(1)}, u32[]{:S(2)}, u32[]{:S(2)}) %collective-permute-start) | collective-permute-done | bytes 49184 | tf_op jit(solution)/shard_map/ppermute | solution.py:539
  30.4 0.0 collective-permute-done.1.from_east
  30.4 0.1 rows.1
  30.5 6.1 %collective-permute-start.2 = (f32[240,128]{1,0:T(8,128)S(1)}, f32[240,128]{1,0:T(8,128)S(1)}, u32[]{:S(2)}, u32[]{:S(2)}) collective-permute-start(f32[240,128]{1,0:T(8,128)S(1)} %get-tuple-element.18), channel_id=1, source_target_pairs={{0,32},{32,64},{64,96},{96,128},{128,160},{160,192},{192,224},{224... | collective-permute-start | bytes 368648 | tf_op jit(solution)/shard_map/ppermute | solution.py:552
  36.7 1.9 %collective-permute-start.3 = (f32[240,128]{1,0:T(8,128)S(1)}, f32[240,128]{1,0:T(8,128)S(1)}, u32[]{:S(2)}, u32[]{:S(2)}) collective-permute-start(f32[240,128]{1,0:T(8,128)S(1)} %get-tuple-element.19), channel_id=1, source_target_pairs={{32,0},{64,32},{96,64},{128,96},{160,128},{192,160},{224,192},{255... | collective-permute-start | bytes 368648 | tf_op jit(solution)/shard_map/ppermute | solution.py:553
  38.6 0.1 collective-permute-done.2.from_below
  38.7 8.0 %collective-permute-done.3.from_above = f32[240,128]{1,0:T(8,128)S(1)} collective-permute-done((f32[240,128]{1,0:T(8,128)S(1)}, f32[240,128]{1,0:T(8,128)S(1)}, u32[]{:S(2)}, u32[]{:S(2)}) %collective-permute-start.3) | collective-permute-done | bytes 122912 | tf_op jit(solution)/shard_map/ppermute | solution.py:553
  46.7 3.3 %first_half.1 = (f32[23,2,112,128]{3,2,1,0:T(8,128)S(1)}, f32[1,10,512,128]{3,2,1,0:T(8,128)}, s32[8,128]{1,0:T(8,128)S(1)}) custom-call(f32[12,64,128]{2,1,0:T(8,128)S(1)} %get-tuple-element.15.fields, f32[96,128]{1,0:T(8,128)S(1)} %collective-permute-done.from_west, f32[96,128]{1,0:T(8,128)S(1)} %collective-permute-done.1.from_east, ...), custom_call_target="tpu_custom_call" | custom-call | flops 20000000 | bytes 2000000 | tf_op jit(solution)/shard_map/first_half/pallas_call | solution.py:557
  50.0 2.5 %second_half.1 = (f32[2,64,128]{2,1,0:T(8,128)}, f32[3,64,128]{2,1,0:T(8,128)}, f32[23,2,112,128]{3,2,1,0:T(8,128)S(1)}, f32[1,10,512,128]{3,2,1,0:T(8,128)}) custom-call(f32[23,2,112,128]{3,2,1,0:T(8,128)S(1)} %get-tuple-element.21.state, f32[1,10,512,128]{3,2,1,0:T(8,128)} %get-tuple-element.22.out_in, ...), custom_call_target="tpu_custom_call", output_to_operand_aliasing={{2}: (0, {}), {3}: (1, {})} | custom-call | flops 20000000 | bytes 2000000 | tf_op jit(solution)/shard_map/second_half/pallas_call | solution.py:594
  52.5 0.0 collective-permute-done.7.partner
  52.5 0.2 last.1
Async XLA Ops:
  2.4 7.7 %collective-permute-start.4 = (f32[10,64,128]{2,1,0:T(8,128)S(1)}, f32[10,64,128]{2,1,0:T(8,128)S(1)}, u32[]{:S(2)}, u32[]{:S(2)}) collective-permute-start(f32[10,64,128]{2,1,0:T(8,128)S(1)} %get-tuple-element.20.snap.own), channel_id=1, source_target_pairs={{0,64},{32,224},{64,128},{96,32},{128,192},{160,96},{192,0},{224,1... | collective-permute-start | bytes 983048 | tf_op jit(solution)/shard_map/ppermute | solution.py:538
  3.0 9.3 %collective-permute-start.5 = (f32[10,64,128]{2,1,0:T(8,128)S(1)}, f32[10,64,128]{2,1,0:T(8,128)S(1)}, u32[]{:S(2)}, u32[]{:S(2)}) collective-permute-start(f32[10,64,128]{2,1,0:T(8,128)S(1)} %get-tuple-element.20.snap.own), channel_id=1, source_target_pairs={{0,192},{32,96},{64,0},{96,160},{128,64},{160,224},{192,128},{224,... | collective-permute-start | bytes 983048 | tf_op jit(solution)/shard_map/ppermute | solution.py:541
  10.0 7.1 %collective-permute-start.6 = (f32[10,64,128]{2,1,0:T(8,128)S(1)}, f32[10,64,128]{2,1,0:T(8,128)S(1)}, u32[]{:S(2)}, u32[]{:S(2)}) collective-permute-start(f32[10,64,128]{2,1,0:T(8,128)S(1)} %collective-permute-done.4.near), channel_id=1, source_target_pairs={{0,64},{32,224},{64,128},{96,32},{128,192},{160,96},{192,0},{224,1... | collective-permute-start | bytes 983048 | tf_op jit(solution)/shard_map/ppermute | solution.py:554
  17.3 35.3 %collective-permute-start.7 = (f32[4,10,64,128]{3,2,1,0:T(8,128)S(1)}, f32[4,10,64,128]{3,2,1,0:T(8,128)S(1)}, u32[]{:S(2)}, u32[]{:S(2)}) collective-permute-start(f32[4,10,64,128]{3,2,1,0:T(8,128)S(1)} %join.1), channel_id=1, source_target_pairs={{0,32},{32,0},{64,96},{96,64},{128,160},{160,128},{192,224},{224,1... | collective-permute-start | bytes 3932168 | tf_op jit(solution)/shard_map/ppermute | solution.py:592
  21.5 8.9 %collective-permute-start = (f32[96,128]{1,0:T(8,128)S(1)}, f32[96,128]{1,0:T(8,128)S(1)}, u32[]{:S(2)}, u32[]{:S(2)}) collective-permute-start(f32[96,128]{1,0:T(8,128)S(1)} %get-tuple-element.16), channel_id=1, source_target_pairs={{0,1},{1,2},{2,3},{3,4},{4,5},{5,6},{6,7},{7,8},{8,9},{9,10},{10,1... | collective-permute-start | bytes 147464 | tf_op jit(solution)/shard_map/ppermute | solution.py:539
  22.0 8.4 %collective-permute-start.1 = (f32[96,128]{1,0:T(8,128)S(1)}, f32[96,128]{1,0:T(8,128)S(1)}, u32[]{:S(2)}, u32[]{:S(2)}) collective-permute-start(f32[96,128]{1,0:T(8,128)S(1)} %get-tuple-element.17), channel_id=1, source_target_pairs={{0,31},{1,0},{2,1},{3,2},{4,3},{5,4},{6,5},{7,6},{8,7},{9,8},{10,9... | collective-permute-start | bytes 147464 | tf_op jit(solution)/shard_map/ppermute | solution.py:540
  30.5 8.1 %collective-permute-start.2 = (f32[240,128]{1,0:T(8,128)S(1)}, f32[240,128]{1,0:T(8,128)S(1)}, u32[]{:S(2)}, u32[]{:S(2)}) collective-permute-start(f32[240,128]{1,0:T(8,128)S(1)} %get-tuple-element.18), channel_id=1, source_target_pairs={{0,32},{32,64},{64,96},{96,128},{128,160},{160,192},{192,224},{224... | collective-permute-start | bytes 368648 | tf_op jit(solution)/shard_map/ppermute | solution.py:552
  36.7 10.0 %collective-permute-start.3 = (f32[240,128]{1,0:T(8,128)S(1)}, f32[240,128]{1,0:T(8,128)S(1)}, u32[]{:S(2)}, u32[]{:S(2)}) collective-permute-start(f32[240,128]{1,0:T(8,128)S(1)} %get-tuple-element.19), channel_id=1, source_target_pairs={{32,0},{64,32},{96,64},{128,96},{160,128},{192,160},{224,192},{255... | collective-permute-start | bytes 368648 | tf_op jit(solution)/shard_map/ppermute | solution.py:553

commit v4 on v3

--- a/solution.py
+++ b/solution.py
@@ -140,9 +140,9 @@
         to_east[8 * f : 8 * f + 8] = right
 
 
-def rows_kernel(fields, from_west, from_east, upward, downward):
+def rows_kernel(fields, from_west, from_east, outer, inner):
     lane = lane_index()
-    flipped = lax.axis_index("col") >= 16
+    odd = lax.axis_index("row") % 2 == 1
 
     def fill(to_north, to_south):
         for f in range(SENT):
@@ -165,13 +165,13 @@
             to_north[at : at + 8] = north
             to_south[at : at + 8] = south
 
-    @pl.when(flipped)
-    def _():
-        fill(downward, upward)
-
-    @pl.when(jnp.logical_not(flipped))
-    def _():
-        fill(upward, downward)
+    @pl.when(odd)
+    def _():
+        fill(outer, inner)
+
+    @pl.when(jnp.logical_not(odd))
+    def _():
+        fill(inner, outer)
 
 
 def stencil_masks():
@@ -181,18 +181,18 @@
     return lane == 0, lane == LANES - 1, row, top_rows
 
 
-def assemble(fields, from_west, from_east, from_below, from_above, held):
+def assemble(fields, from_west, from_east, from_outer, from_inner, held):
     is_top = lax.axis_index("row") == 7
-    flipped = jnp.where(lax.axis_index("col") >= 16, 1, 0) + jnp.zeros((8, LANES), jnp.int32) == 1
+    odd = lax.axis_index("row") % 2 + jnp.zeros((8, LANES), jnp.int32) == 1
     lane = lane_index()
     row = row_index()
     first, last, low = lane == 0, lane == LANES - 1, lane < 64
 
     def south(at):
-        return jnp.where(flipped, from_above[at : at + 8], from_below[at : at + 8])
+        return jnp.where(odd, from_inner[at : at + 8], from_outer[at : at + 8])
 
     def north(at):
-        return jnp.where(flipped, from_below[at : at + 8], from_above[at : at + 8])
+        return jnp.where(odd, from_outer[at : at + 8], from_inner[at : at + 8])
 
     def side_rows(message, f, a):
         base = 64 * (f % 2)
@@ -378,13 +378,13 @@
 
 
 def first_half_kernel(
-    fields, from_west, from_east, from_below, from_above, snap, writer_hbm, held, out, flag, writer, zero, sems
+    fields, from_west, from_east, from_outer, from_inner, snap, writer_hbm, held, out, flag, writer, zero, sems
 ):
     me = lax.axis_index("row")
     read = pltpu.make_async_copy(writer_hbm, writer, sems.at[8])
     read.start()
     zero[...] = jnp.zeros_like(zero)
-    assemble(fields, from_west, from_east, from_below, from_above, held)
+    assemble(fields, from_west, from_east, from_outer, from_inner, held)
     read.wait()
     mine = writer[lax.axis_index("col")] == me
     flag[...] = jnp.where(mine, 1, 0) + jnp.zeros((8, LANES), jnp.int32)
@@ -529,18 +529,17 @@
     partner = [(r, r ^ 1) for r in range(8)]
     eastward = [(c, (c + 1) % 32) for c in range(32)]
     westward = [(c, (c - 1) % 32) for c in range(32)]
-    upward = []
-    for c in range(16):
-        line = [32 * r + c for r in range(8)] + [32 * (7 - r) + 31 - c for r in range(8)]
-        upward += list(zip(line[:-1], line[1:]))
-    downward = [(b, a) for a, b in upward]
+    across = [(7 * 32 + c, 7 * 32 + 31 - c) for c in range(32)]
+    for c in range(32):
+        for r in (1, 3, 5):
+            across += [(32 * r + c, 32 * r + 32 + c), (32 * r + 32 + c, 32 * r + c)]
 
     near = lax.ppermute(snap, "row", along)
     from_west = lax.ppermute(to_east, "col", eastward)
     from_east = lax.ppermute(to_west, "col", westward)
     near_back = lax.ppermute(snap, "row", against)
 
-    to_above, to_below = pl.pallas_call(
+    outer, inner = pl.pallas_call(
         rows_kernel,
         out_shape=(shape(MESSAGE, LANES),) * 2,
         in_specs=[vmem()] * 3,
@@ -549,8 +548,8 @@
         cost_estimate=pl.CostEstimate(flops=1000000, bytes_accessed=1000000, transcendentals=0),
         name="rows",
     )(fields, from_west, from_east)
-    from_below = lax.ppermute(to_above, ("row", "col"), upward)
-    from_above = lax.ppermute(to_below, ("row", "col"), downward)
+    from_outer = lax.ppermute(outer, ("row", "col"), across)
+    from_inner = lax.ppermute(inner, "row", partner)
     far = lax.ppermute(near, "row", along)
 
     hbm = lambda: pl.BlockSpec(memory_space=pl.ANY)
@@ -575,8 +574,8 @@
         fields,
         from_west,
         from_east,
-        from_below,
-        from_above,
+        from_outer,
+        from_inner,
         snap,
         pltpu.with_memory_space_constraint(writer, pltpu.HBM),
     )

time: 53 us -> 45.7 us (0.86)
  waiting for transfers between devices: 22 us -> 16.6 us
  starting transfers between devices: 22.1 us -> 20.3 us
    ppermute x2, waiting for transfers between devices: 8.1 us -> 2.7 us  [the longest x1 2.69 us: step(): from_outer = lax.ppermute(outer, ('row', 'col'), across)]
    ppermute x2, starting transfers between devices: 8.07 us -> 6.24 us  [the longest x1 6.14 us: step(): from_outer = lax.ppermute(outer, ('row', 'col'), across)]
  transfers between devices with their start and end apart: 8 -> 8, of which waited for: 6 -> 5; matrix products, arithmetic and copies ran while one was open for 0% -> 0% of each run, Pallas kernels for 11% -> 13%
where the time goes in v4:
time: 45.7 us; the launch traced here: 45.6 us
  starting transfers between devices  20.3 us (44%)
  waiting for transfers between devices  16.6 us (36%)
  Pallas kernels  7.96 us (17%)
  between operations  0.7 us (2%)
    ppermute x1, starting transfers between devices, step(): from_east = lax.ppermute(to_west, 'col', westward)  6.39 us
    ppermute x1, starting transfers between devices, step(): from_outer = lax.ppermute(outer, ('row', 'col'), across)  6.14 us
    ppermute x1, waiting for transfers between devices, step(): near = lax.ppermute(snap, 'row', along)  4.94 us
    ppermute x1, waiting for transfers between devices, step(): far = lax.ppermute(near, 'row', along)  4.91 us
    ppermute x1, starting transfers between devices, step(): partner_blocks = lax.ppermute(joined, 'row', partner)  4.22 us
    pallas_call x1, Pallas kernels, step(): pl.pallas_call(first_half_kernel, out_shape=(shape(HELD, 2, TALL, LANES),...  3.31 us
    ppermute x1, waiting for transfers between devices, step(): from_outer = lax.ppermute(outer, ('row', 'col'), across)  2.69 us
    pallas_call x1, Pallas kernels, step(): pl.pallas_call(second_half_kernel, out_shape=(shape(2, ROWS, LANES), shap...  2.51 us
  transfers between devices with their start and end apart: 8, of which 5 were waited for; matrix products, arithmetic and copies ran while one was open for 0% of the time, Pallas kernels for 13%

profile of v4, /device:TPU:7, one launch (start us, length us, event | category | flops | bytes accessed | tf_op | source)
XLA Modules:
  0.0 45.6 jit_solution(3314620071503283140)
XLA Ops:
  0.6 1.7 %prepare.1 = (f32[12,64,128]{2,1,0:T(8,128)S(1)}, f32[96,128]{1,0:T(8,128)S(1)}, f32[96,128]{1,0:T(8,128)S(1)}, f32[10,64,128]{2,1,0:T(8,128)S(1)}) custom-call(f32[2,64,128]{2,1,0:T(8,128)} %vel_hbm.1, f32[3,64,128]{2,1,0:T(8,128)} %stress_hbm.1, f32[2,64,128]{2,1,0:T(8,128)} %wind_hbm.1, f32[2,64,128]{2,1,0:T(8,128)} %ocean_hbm.1, f32[5,64,128]{2,1,0:T(8,128)} %area_hbm.1, ...), custom_call_target="tpu_custom_call" | custom-call | tf_op jit(solution)/shard_map/prepare/pallas_call | solution.py:487
  2.4 0.6 %collective-permute-start.4 = (f32[10,64,128]{2,1,0:T(8,128)S(1)}, f32[10,64,128]{2,1,0:T(8,128)S(1)}, u32[]{:S(2)}, u32[]{:S(2)}) collective-permute-start(f32[10,64,128]{2,1,0:T(8,128)S(1)} %get-tuple-element.20.snap.own), channel_id=1, source_target_pairs={{0,64},{32,224},{64,128},{96,32},{128,192},{160,96},{192,0},{224,1... | collective-permute-start | bytes 983048 | tf_op jit(solution)/shard_map/ppermute | solution.py:537
  3.0 2.1 %collective-permute-start.5 = (f32[10,64,128]{2,1,0:T(8,128)S(1)}, f32[10,64,128]{2,1,0:T(8,128)S(1)}, u32[]{:S(2)}, u32[]{:S(2)}) collective-permute-start(f32[10,64,128]{2,1,0:T(8,128)S(1)} %get-tuple-element.20.snap.own), channel_id=1, source_target_pairs={{0,192},{32,96},{64,0},{96,160},{128,64},{160,224},{192,128},{224,... | collective-permute-start | bytes 983048 | tf_op jit(solution)/shard_map/ppermute | solution.py:540
  5.1 4.9 %collective-permute-done.4.near = f32[10,64,128]{2,1,0:T(8,128)S(1)} collective-permute-done((f32[10,64,128]{2,1,0:T(8,128)S(1)}, f32[10,64,128]{2,1,0:T(8,128)S(1)}, u32[]{:S(2)}, u32[]{:S(2)}) %collective-permute-start.4) | collective-permute-done | bytes 327712 | tf_op jit(solution)/shard_map/ppermute | solution.py:537
  10.0 0.2 collective-permute-start.6
  10.2 2.1 %collective-permute-done.5.near_back = f32[10,64,128]{2,1,0:T(8,128)S(1)} collective-permute-done((f32[10,64,128]{2,1,0:T(8,128)S(1)}, f32[10,64,128]{2,1,0:T(8,128)S(1)}, u32[]{:S(2)}, u32[]{:S(2)}) %collective-permute-start.5) | collective-permute-done | bytes 327712 | tf_op jit(solution)/shard_map/ppermute | solution.py:540
  12.3 4.9 %collective-permute-done.6.far = f32[10,64,128]{2,1,0:T(8,128)S(1)} collective-permute-done((f32[10,64,128]{2,1,0:T(8,128)S(1)}, f32[10,64,128]{2,1,0:T(8,128)S(1)}, u32[]{:S(2)}, u32[]{:S(2)}) %collective-permute-start.6) | collective-permute-done | bytes 327712 | tf_op jit(solution)/shard_map/ppermute | solution.py:553
  17.2 0.1 join.1
  17.3 4.2 %collective-permute-start.7 = (f32[4,10,64,128]{3,2,1,0:T(8,128)S(1)}, f32[4,10,64,128]{3,2,1,0:T(8,128)S(1)}, u32[]{:S(2)}, u32[]{:S(2)}) collective-permute-start(f32[4,10,64,128]{3,2,1,0:T(8,128)S(1)} %join.1), channel_id=1, source_target_pairs={{0,32},{32,0},{64,96},{96,64},{128,160},{160,128},{192,224},{224,1... | collective-permute-start | bytes 3932168 | tf_op jit(solution)/shard_map/ppermute | solution.py:591
  21.5 0.5 %collective-permute-start = (f32[96,128]{1,0:T(8,128)S(1)}, f32[96,128]{1,0:T(8,128)S(1)}, u32[]{:S(2)}, u32[]{:S(2)}) collective-permute-start(f32[96,128]{1,0:T(8,128)S(1)} %get-tuple-element.16), channel_id=1, source_target_pairs={{0,1},{1,2},{2,3},{3,4},{4,5},{5,6},{6,7},{7,8},{8,9},{9,10},{10,1... | collective-permute-start | bytes 147464 | tf_op jit(solution)/shard_map/ppermute | solution.py:538
  22.0 6.4 %collective-permute-start.1 = (f32[96,128]{1,0:T(8,128)S(1)}, f32[96,128]{1,0:T(8,128)S(1)}, u32[]{:S(2)}, u32[]{:S(2)}) collective-permute-start(f32[96,128]{1,0:T(8,128)S(1)} %get-tuple-element.17), channel_id=1, source_target_pairs={{0,31},{1,0},{2,1},{3,2},{4,3},{5,4},{6,5},{7,6},{8,7},{9,8},{10,9... | collective-permute-start | bytes 147464 | tf_op jit(solution)/shard_map/ppermute | solution.py:539
  28.4 2.0 %collective-permute-done.from_west = f32[96,128]{1,0:T(8,128)S(1)} collective-permute-done((f32[96,128]{1,0:T(8,128)S(1)}, f32[96,128]{1,0:T(8,128)S(1)}, u32[]{:S(2)}, u32[]{:S(2)}) %collective-permute-start) | collective-permute-done | bytes 49184 | tf_op jit(solution)/shard_map/ppermute | solution.py:538
  30.4 0.0 collective-permute-done.1.from_east
  30.4 0.1 rows.1
  30.5 6.1 %collective-permute-start.2 = (f32[240,128]{1,0:T(8,128)S(1)}, f32[240,128]{1,0:T(8,128)S(1)}, u32[]{:S(2)}, u32[]{:S(2)}) collective-permute-start(f32[240,128]{1,0:T(8,128)S(1)} %get-tuple-element.18), channel_id=1, source_target_pairs={{224,255},{225,254},{226,253},{227,252},{228,251},{229,250},{230,2... | collective-permute-start | bytes 368648 | tf_op jit(solution)/shard_map/ppermute | solution.py:551
  36.7 0.1 collective-permute-start.3
  36.8 2.7 %collective-permute-done.2.from_outer = f32[240,128]{1,0:T(8,128)S(1)} collective-permute-done((f32[240,128]{1,0:T(8,128)S(1)}, f32[240,128]{1,0:T(8,128)S(1)}, u32[]{:S(2)}, u32[]{:S(2)}) %collective-permute-start.2) | collective-permute-done | bytes 122912 | tf_op jit(solution)/shard_map/ppermute | solution.py:551
  39.5 0.0 collective-permute-done.3.from_inner
  39.5 3.3 %first_half.1 = (f32[23,2,112,128]{3,2,1,0:T(8,128)S(1)}, f32[1,10,512,128]{3,2,1,0:T(8,128)}, s32[8,128]{1,0:T(8,128)S(1)}) custom-call(f32[12,64,128]{2,1,0:T(8,128)S(1)} %get-tuple-element.15.fields, f32[96,128]{1,0:T(8,128)S(1)} %collective-permute-done.from_west, f32[96,128]{1,0:T(8,128)S(1)} %collective-permute-done.1.from_east, ...), custom_call_target="tpu_custom_call" | custom-call | flops 20000000 | bytes 2000000 | tf_op jit(solution)/shard_map/first_half/pallas_call | solution.py:556
  42.8 2.5 %second_half.1 = (f32[2,64,128]{2,1,0:T(8,128)}, f32[3,64,128]{2,1,0:T(8,128)}, f32[23,2,112,128]{3,2,1,0:T(8,128)S(1)}, f32[1,10,512,128]{3,2,1,0:T(8,128)}) custom-call(f32[23,2,112,128]{3,2,1,0:T(8,128)S(1)} %get-tuple-element.21.state, f32[1,10,512,128]{3,2,1,0:T(8,128)} %get-tuple-element.22.out_in, ...), custom_call_target="tpu_custom_call", output_to_operand_aliasing={{2}: (0, {}), {3}: (1, {})} | custom-call | flops 20000000 | bytes 2000000 | tf_op jit(solution)/shard_map/second_half/pallas_call | solution.py:593
  45.3 0.0 collective-permute-done.7.partner
  45.3 0.2 last.1
Async XLA Ops:
  2.4 7.7 %collective-permute-start.4 = (f32[10,64,128]{2,1,0:T(8,128)S(1)}, f32[10,64,128]{2,1,0:T(8,128)S(1)}, u32[]{:S(2)}, u32[]{:S(2)}) collective-permute-start(f32[10,64,128]{2,1,0:T(8,128)S(1)} %get-tuple-element.20.snap.own), channel_id=1, source_target_pairs={{0,64},{32,224},{64,128},{96,32},{128,192},{160,96},{192,0},{224,1... | collective-permute-start | bytes 983048 | tf_op jit(solution)/shard_map/ppermute | solution.py:537
  3.0 9.3 %collective-permute-start.5 = (f32[10,64,128]{2,1,0:T(8,128)S(1)}, f32[10,64,128]{2,1,0:T(8,128)S(1)}, u32[]{:S(2)}, u32[]{:S(2)}) collective-permute-start(f32[10,64,128]{2,1,0:T(8,128)S(1)} %get-tuple-element.20.snap.own), channel_id=1, source_target_pairs={{0,192},{32,96},{64,0},{96,160},{128,64},{160,224},{192,128},{224,... | collective-permute-start | bytes 983048 | tf_op jit(solution)/shard_map/ppermute | solution.py:540
  10.0 7.1 %collective-permute-start.6 = (f32[10,64,128]{2,1,0:T(8,128)S(1)}, f32[10,64,128]{2,1,0:T(8,128)S(1)}, u32[]{:S(2)}, u32[]{:S(2)}) collective-permute-start(f32[10,64,128]{2,1,0:T(8,128)S(1)} %collective-permute-done.4.near), channel_id=1, source_target_pairs={{0,64},{32,224},{64,128},{96,32},{128,192},{160,96},{192,0},{224,1... | collective-permute-start | bytes 983048 | tf_op jit(solution)/shard_map/ppermute | solution.py:553
  17.3 28.0 %collective-permute-start.7 = (f32[4,10,64,128]{3,2,1,0:T(8,128)S(1)}, f32[4,10,64,128]{3,2,1,0:T(8,128)S(1)}, u32[]{:S(2)}, u32[]{:S(2)}) collective-permute-start(f32[4,10,64,128]{3,2,1,0:T(8,128)S(1)} %join.1), channel_id=1, source_target_pairs={{0,32},{32,0},{64,96},{96,64},{128,160},{160,128},{192,224},{224,1... | collective-permute-start | bytes 3932168 | tf_op jit(solution)/shard_map/ppermute | solution.py:591
  21.5 8.9 %collective-permute-start = (f32[96,128]{1,0:T(8,128)S(1)}, f32[96,128]{1,0:T(8,128)S(1)}, u32[]{:S(2)}, u32[]{:S(2)}) collective-permute-start(f32[96,128]{1,0:T(8,128)S(1)} %get-tuple-element.16), channel_id=1, source_target_pairs={{0,1},{1,2},{2,3},{3,4},{4,5},{5,6},{6,7},{7,8},{8,9},{9,10},{10,1... | collective-permute-start | bytes 147464 | tf_op jit(solution)/shard_map/ppermute | solution.py:538
  22.0 8.4 %collective-permute-start.1 = (f32[96,128]{1,0:T(8,128)S(1)}, f32[96,128]{1,0:T(8,128)S(1)}, u32[]{:S(2)}, u32[]{:S(2)}) collective-permute-start(f32[96,128]{1,0:T(8,128)S(1)} %get-tuple-element.17), channel_id=1, source_target_pairs={{0,31},{1,0},{2,1},{3,2},{4,3},{5,4},{6,5},{7,6},{8,7},{9,8},{10,9... | collective-permute-start | bytes 147464 | tf_op jit(solution)/shard_map/ppermute | solution.py:539
  30.5 8.9 %collective-permute-start.2 = (f32[240,128]{1,0:T(8,128)S(1)}, f32[240,128]{1,0:T(8,128)S(1)}, u32[]{:S(2)}, u32[]{:S(2)}) collective-permute-start(f32[240,128]{1,0:T(8,128)S(1)} %get-tuple-element.18), channel_id=1, source_target_pairs={{224,255},{225,254},{226,253},{227,252},{228,251},{229,250},{230,2... | collective-permute-start | bytes 368648 | tf_op jit(solution)/shard_map/ppermute | solution.py:551
  36.7 2.8 %collective-permute-start.3 = (f32[240,128]{1,0:T(8,128)S(1)}, f32[240,128]{1,0:T(8,128)S(1)}, u32[]{:S(2)}, u32[]{:S(2)}) collective-permute-start(f32[240,128]{1,0:T(8,128)S(1)} %get-tuple-element.19), channel_id=1, source_target_pairs={{0,32},{32,0},{64,96},{96,64},{128,160},{160,128},{192,224},{224,1... | collective-permute-start | bytes 368648 | tf_op jit(solution)/shard_map/ppermute | solution.py:552

commit v5 on v4

--- a/solution.py
+++ b/solution.py
@@ -188,8 +188,11 @@
     row = row_index()
     first, last, low = lane == 0, lane == LANES - 1, lane < 64
 
+    bottom = lax.axis_index("row") + jnp.zeros((8, LANES), jnp.int32) == 0
+
     def south(at):
-        return jnp.where(odd, from_inner[at : at + 8], from_outer[at : at + 8])
+        value = jnp.where(odd, from_inner[at : at + 8], from_outer[at : at + 8])
+        return jnp.where(bottom, 0.0, value)
 
     def north(at):
         return jnp.where(odd, from_outer[at : at + 8], from_inner[at : at + 8])
@@ -530,6 +533,7 @@
     eastward = [(c, (c + 1) % 32) for c in range(32)]
     westward = [(c, (c - 1) % 32) for c in range(32)]
     across = [(7 * 32 + c, 7 * 32 + 31 - c) for c in range(32)]
+    across += [(c, c) for c in range(32)]
     for c in range(32):
         for r in (1, 3, 5):
             across += [(32 * r + c, 32 * r + 32 + c), (32 * r + 32 + c, 32 * r + c)]

time: 45.7 us -> 45.7 us (level)
  no operation moved by 1% of the time
where the time goes in v5:
time: 45.7 us; the launch traced here: 45.6 us
  starting transfers between devices  20.3 us (44%)
  waiting for transfers between devices  16.6 us (36%)
  Pallas kernels  7.96 us (17%)
  between operations  0.7 us (2%)
    ppermute x1, starting transfers between devices, step(): from_east = lax.ppermute(to_west, 'col', westward)  6.39 us
    ppermute x1, starting transfers between devices, step(): from_outer = lax.ppermute(outer, ('row', 'col'), across)  6.14 us
    ppermute x1, waiting for transfers between devices, step(): near = lax.ppermute(snap, 'row', along)  4.94 us
    ppermute x1, waiting for transfers between devices, step(): far = lax.ppermute(near, 'row', along)  4.91 us
    ppermute x1, starting transfers between devices, step(): partner_blocks = lax.ppermute(joined, 'row', partner)  4.22 us
    pallas_call x1, Pallas kernels, step(): pl.pallas_call(first_half_kernel, out_shape=(shape(HELD, 2, TALL, LANES),...  3.31 us
    ppermute x1, waiting for transfers between devices, step(): from_outer = lax.ppermute(outer, ('row', 'col'), across)  2.69 us
    pallas_call x1, Pallas kernels, step(): pl.pallas_call(second_half_kernel, out_shape=(shape(2, ROWS, LANES), shap...  2.51 us
  transfers between devices with their start and end apart: 8, of which 5 were waited for; matrix products, arithmetic and copies ran while one was open for 0% of the time, Pallas kernels for 13%

profile of v5, /device:TPU:7, one launch (start us, length us, event | category | flops | bytes accessed | tf_op | source)
XLA Modules:
  0.0 45.6 jit_solution(11868962124062758503)
XLA Ops:
  0.6 1.7 %prepare.1 = (f32[12,64,128]{2,1,0:T(8,128)S(1)}, f32[96,128]{1,0:T(8,128)S(1)}, f32[96,128]{1,0:T(8,128)S(1)}, f32[10,64,128]{2,1,0:T(8,128)S(1)}) custom-call(f32[2,64,128]{2,1,0:T(8,128)} %vel_hbm.1, f32[3,64,128]{2,1,0:T(8,128)} %stress_hbm.1, f32[2,64,128]{2,1,0:T(8,128)} %wind_hbm.1, f32[2,64,128]{2,1,0:T(8,128)} %ocean_hbm.1, f32[5,64,128]{2,1,0:T(8,128)} %area_hbm.1, ...), custom_call_target="tpu_custom_call" | custom-call | tf_op jit(solution)/shard_map/prepare/pallas_call | solution.py:490
  2.4 0.6 %collective-permute-start.4 = (f32[10,64,128]{2,1,0:T(8,128)S(1)}, f32[10,64,128]{2,1,0:T(8,128)S(1)}, u32[]{:S(2)}, u32[]{:S(2)}) collective-permute-start(f32[10,64,128]{2,1,0:T(8,128)S(1)} %get-tuple-element.20.snap.own), channel_id=1, source_target_pairs={{0,64},{32,224},{64,128},{96,32},{128,192},{160,96},{192,0},{224,1... | collective-permute-start | bytes 983048 | tf_op jit(solution)/shard_map/ppermute | solution.py:541
  3.0 2.1 %collective-permute-start.5 = (f32[10,64,128]{2,1,0:T(8,128)S(1)}, f32[10,64,128]{2,1,0:T(8,128)S(1)}, u32[]{:S(2)}, u32[]{:S(2)}) collective-permute-start(f32[10,64,128]{2,1,0:T(8,128)S(1)} %get-tuple-element.20.snap.own), channel_id=1, source_target_pairs={{0,192},{32,96},{64,0},{96,160},{128,64},{160,224},{192,128},{224,... | collective-permute-start | bytes 983048 | tf_op jit(solution)/shard_map/ppermute | solution.py:544
  5.1 4.9 %collective-permute-done.4.near = f32[10,64,128]{2,1,0:T(8,128)S(1)} collective-permute-done((f32[10,64,128]{2,1,0:T(8,128)S(1)}, f32[10,64,128]{2,1,0:T(8,128)S(1)}, u32[]{:S(2)}, u32[]{:S(2)}) %collective-permute-start.4) | collective-permute-done | bytes 327712 | tf_op jit(solution)/shard_map/ppermute | solution.py:541
  10.0 0.2 collective-permute-start.6
  10.2 2.1 %collective-permute-done.5.near_back = f32[10,64,128]{2,1,0:T(8,128)S(1)} collective-permute-done((f32[10,64,128]{2,1,0:T(8,128)S(1)}, f32[10,64,128]{2,1,0:T(8,128)S(1)}, u32[]{:S(2)}, u32[]{:S(2)}) %collective-permute-start.5) | collective-permute-done | bytes 327712 | tf_op jit(solution)/shard_map/ppermute | solution.py:544
  12.3 4.9 %collective-permute-done.6.far = f32[10,64,128]{2,1,0:T(8,128)S(1)} collective-permute-done((f32[10,64,128]{2,1,0:T(8,128)S(1)}, f32[10,64,128]{2,1,0:T(8,128)S(1)}, u32[]{:S(2)}, u32[]{:S(2)}) %collective-permute-start.6) | collective-permute-done | bytes 327712 | tf_op jit(solution)/shard_map/ppermute | solution.py:557
  17.2 0.1 join.1
  17.3 4.2 %collective-permute-start.7 = (f32[4,10,64,128]{3,2,1,0:T(8,128)S(1)}, f32[4,10,64,128]{3,2,1,0:T(8,128)S(1)}, u32[]{:S(2)}, u32[]{:S(2)}) collective-permute-start(f32[4,10,64,128]{3,2,1,0:T(8,128)S(1)} %join.1), channel_id=1, source_target_pairs={{0,32},{32,0},{64,96},{96,64},{128,160},{160,128},{192,224},{224,1... | collective-permute-start | bytes 3932168 | tf_op jit(solution)/shard_map/ppermute | solution.py:595
  21.5 0.5 %collective-permute-start = (f32[96,128]{1,0:T(8,128)S(1)}, f32[96,128]{1,0:T(8,128)S(1)}, u32[]{:S(2)}, u32[]{:S(2)}) collective-permute-start(f32[96,128]{1,0:T(8,128)S(1)} %get-tuple-element.16), channel_id=1, source_target_pairs={{0,1},{1,2},{2,3},{3,4},{4,5},{5,6},{6,7},{7,8},{8,9},{9,10},{10,1... | collective-permute-start | bytes 147464 | tf_op jit(solution)/shard_map/ppermute | solution.py:542
  22.0 6.4 %collective-permute-start.1 = (f32[96,128]{1,0:T(8,128)S(1)}, f32[96,128]{1,0:T(8,128)S(1)}, u32[]{:S(2)}, u32[]{:S(2)}) collective-permute-start(f32[96,128]{1,0:T(8,128)S(1)} %get-tuple-element.17), channel_id=1, source_target_pairs={{0,31},{1,0},{2,1},{3,2},{4,3},{5,4},{6,5},{7,6},{8,7},{9,8},{10,9... | collective-permute-start | bytes 147464 | tf_op jit(solution)/shard_map/ppermute | solution.py:543
  28.4 2.0 %collective-permute-done.from_west = f32[96,128]{1,0:T(8,128)S(1)} collective-permute-done((f32[96,128]{1,0:T(8,128)S(1)}, f32[96,128]{1,0:T(8,128)S(1)}, u32[]{:S(2)}, u32[]{:S(2)}) %collective-permute-start) | collective-permute-done | bytes 49184 | tf_op jit(solution)/shard_map/ppermute | solution.py:542
  30.4 0.0 collective-permute-done.1.from_east
  30.4 0.1 rows.1
  30.5 6.1 %collective-permute-start.2 = (f32[240,128]{1,0:T(8,128)S(1)}, f32[240,128]{1,0:T(8,128)S(1)}, u32[]{:S(2)}, u32[]{:S(2)}) collective-permute-start(f32[240,128]{1,0:T(8,128)S(1)} %get-tuple-element.18), channel_id=1, source_target_pairs={{224,255},{225,254},{226,253},{227,252},{228,251},{229,250},{230,2... | collective-permute-start | bytes 368648 | tf_op jit(solution)/shard_map/ppermute | solution.py:555
  36.7 0.1 collective-permute-start.3
  36.8 2.7 %collective-permute-done.2.from_outer = f32[240,128]{1,0:T(8,128)S(1)} collective-permute-done((f32[240,128]{1,0:T(8,128)S(1)}, f32[240,128]{1,0:T(8,128)S(1)}, u32[]{:S(2)}, u32[]{:S(2)}) %collective-permute-start.2) | collective-permute-done | bytes 122912 | tf_op jit(solution)/shard_map/ppermute | solution.py:555
  39.5 0.0 collective-permute-done.3.from_inner
  39.5 3.3 %first_half.1 = (f32[23,2,112,128]{3,2,1,0:T(8,128)S(1)}, f32[1,10,512,128]{3,2,1,0:T(8,128)}, s32[8,128]{1,0:T(8,128)S(1)}) custom-call(f32[12,64,128]{2,1,0:T(8,128)S(1)} %get-tuple-element.15.fields, f32[96,128]{1,0:T(8,128)S(1)} %collective-permute-done.from_west, f32[96,128]{1,0:T(8,128)S(1)} %collective-permute-done.1.from_east, ...), custom_call_target="tpu_custom_call" | custom-call | flops 20000000 | bytes 2000000 | tf_op jit(solution)/shard_map/first_half/pallas_call | solution.py:560
  42.8 2.5 %second_half.1 = (f32[2,64,128]{2,1,0:T(8,128)}, f32[3,64,128]{2,1,0:T(8,128)}, f32[23,2,112,128]{3,2,1,0:T(8,128)S(1)}, f32[1,10,512,128]{3,2,1,0:T(8,128)}) custom-call(f32[23,2,112,128]{3,2,1,0:T(8,128)S(1)} %get-tuple-element.21.state, f32[1,10,512,128]{3,2,1,0:T(8,128)} %get-tuple-element.22.out_in, ...), custom_call_target="tpu_custom_call", output_to_operand_aliasing={{2}: (0, {}), {3}: (1, {})} | custom-call | flops 20000000 | bytes 2000000 | tf_op jit(solution)/shard_map/second_half/pallas_call | solution.py:597
  45.3 0.0 collective-permute-done.7.partner
  45.3 0.2 last.1
Async XLA Ops:
  2.4 7.7 %collective-permute-start.4 = (f32[10,64,128]{2,1,0:T(8,128)S(1)}, f32[10,64,128]{2,1,0:T(8,128)S(1)}, u32[]{:S(2)}, u32[]{:S(2)}) collective-permute-start(f32[10,64,128]{2,1,0:T(8,128)S(1)} %get-tuple-element.20.snap.own), channel_id=1, source_target_pairs={{0,64},{32,224},{64,128},{96,32},{128,192},{160,96},{192,0},{224,1... | collective-permute-start | bytes 983048 | tf_op jit(solution)/shard_map/ppermute | solution.py:541
  3.0 9.3 %collective-permute-start.5 = (f32[10,64,128]{2,1,0:T(8,128)S(1)}, f32[10,64,128]{2,1,0:T(8,128)S(1)}, u32[]{:S(2)}, u32[]{:S(2)}) collective-permute-start(f32[10,64,128]{2,1,0:T(8,128)S(1)} %get-tuple-element.20.snap.own), channel_id=1, source_target_pairs={{0,192},{32,96},{64,0},{96,160},{128,64},{160,224},{192,128},{224,... | collective-permute-start | bytes 983048 | tf_op jit(solution)/shard_map/ppermute | solution.py:544
  10.0 7.1 %collective-permute-start.6 = (f32[10,64,128]{2,1,0:T(8,128)S(1)}, f32[10,64,128]{2,1,0:T(8,128)S(1)}, u32[]{:S(2)}, u32[]{:S(2)}) collective-permute-start(f32[10,64,128]{2,1,0:T(8,128)S(1)} %collective-permute-done.4.near), channel_id=1, source_target_pairs={{0,64},{32,224},{64,128},{96,32},{128,192},{160,96},{192,0},{224,1... | collective-permute-start | bytes 983048 | tf_op jit(solution)/shard_map/ppermute | solution.py:557
  17.3 28.0 %collective-permute-start.7 = (f32[4,10,64,128]{3,2,1,0:T(8,128)S(1)}, f32[4,10,64,128]{3,2,1,0:T(8,128)S(1)}, u32[]{:S(2)}, u32[]{:S(2)}) collective-permute-start(f32[4,10,64,128]{3,2,1,0:T(8,128)S(1)} %join.1), channel_id=1, source_target_pairs={{0,32},{32,0},{64,96},{96,64},{128,160},{160,128},{192,224},{224,1... | collective-permute-start | bytes 3932168 | tf_op jit(solution)/shard_map/ppermute | solution.py:595
  21.5 8.9 %collective-permute-start = (f32[96,128]{1,0:T(8,128)S(1)}, f32[96,128]{1,0:T(8,128)S(1)}, u32[]{:S(2)}, u32[]{:S(2)}) collective-permute-start(f32[96,128]{1,0:T(8,128)S(1)} %get-tuple-element.16), channel_id=1, source_target_pairs={{0,1},{1,2},{2,3},{3,4},{4,5},{5,6},{6,7},{7,8},{8,9},{9,10},{10,1... | collective-permute-start | bytes 147464 | tf_op jit(solution)/shard_map/ppermute | solution.py:542
  22.0 8.4 %collective-permute-start.1 = (f32[96,128]{1,0:T(8,128)S(1)}, f32[96,128]{1,0:T(8,128)S(1)}, u32[]{:S(2)}, u32[]{:S(2)}) collective-permute-start(f32[96,128]{1,0:T(8,128)S(1)} %get-tuple-element.17), channel_id=1, source_target_pairs={{0,31},{1,0},{2,1},{3,2},{4,3},{5,4},{6,5},{7,6},{8,7},{9,8},{10,9... | collective-permute-start | bytes 147464 | tf_op jit(solution)/shard_map/ppermute | solution.py:543
  30.5 8.9 %collective-permute-start.2 = (f32[240,128]{1,0:T(8,128)S(1)}, f32[240,128]{1,0:T(8,128)S(1)}, u32[]{:S(2)}, u32[]{:S(2)}) collective-permute-start(f32[240,128]{1,0:T(8,128)S(1)} %get-tuple-element.18), channel_id=1, source_target_pairs={{224,255},{225,254},{226,253},{227,252},{228,251},{229,250},{230,2... | collective-permute-start | bytes 368648 | tf_op jit(solution)/shard_map/ppermute | solution.py:555
  36.7 2.8 %collective-permute-start.3 = (f32[240,128]{1,0:T(8,128)S(1)}, f32[240,128]{1,0:T(8,128)S(1)}, u32[]{:S(2)}, u32[]{:S(2)}) collective-permute-start(f32[240,128]{1,0:T(8,128)S(1)} %get-tuple-element.19), channel_id=1, source_target_pairs={{0,32},{32,0},{64,96},{96,64},{128,160},{160,128},{192,224},{224,1... | collective-permute-start | bytes 368648 | tf_op jit(solution)/shard_map/ppermute | solution.py:556

commit v6 on v5

--- a/solution.py
+++ b/solution.py
@@ -14,6 +14,8 @@
 PAD = 8
 TALL = PAD + HALO + ROWS + HALO + PAD
 TOP = PAD + HALO + ROWS
+BAND = 24
+SHORT = PAD + BAND + PAD
 
 U, V, S1, S2, S12, STR, HW, HH, INE, AA, KU, KV = range(12)
 SENT = 12
@@ -37,14 +39,24 @@
     return value if steps == 0 else pltpu.roll(value, steps, 1)
 
 
-def west(main, side, first):
-    a, b = turned(main, 1), turned(side, 1)
-    return jnp.where(first, b, a), jnp.where(first, a, b)
-
-
-def east(main, side, last):
-    a, b = turned(main, -1), turned(side, -1)
-    return jnp.where(last, b, a), jnp.where(last, a, b)
+def west(values, blocks, lane):
+    side = values[0]
+    out = turned(side, 1)
+    mains = []
+    for main, b in zip(values[1:], blocks):
+        out = jnp.where(lane == 32 * b + 16, turned(main, 32 * b + 17), out)
+        mains.append(jnp.where(lane == 0, turned(side, -(32 * b + 15)), turned(main, 1)))
+    return [out] + mains
+
+
+def east(values, blocks, lane):
+    side = values[0]
+    out = turned(side, -1)
+    mains = []
+    for main, b in zip(values[1:], blocks):
+        out = jnp.where(lane == 32 * b + 15, turned(main, 32 * b + 15), out)
+        mains.append(jnp.where(lane == LANES - 1, turned(side, 111 - 32 * b), turned(main, -1)))
+    return [out] + mains
 
 
 def expanded(blocks_t):
@@ -174,21 +186,11 @@
         fill(inner, outer)
 
 
-def stencil_masks():
-    lane, row = lane_index(), row_index()
-    is_top = lax.axis_index("row") == 7
-    top_rows = (jnp.where(is_top, 1, 0) + jnp.zeros((8, LANES), jnp.int32)) == 1
-    return lane == 0, lane == LANES - 1, row, top_rows
-
-
-def assemble(fields, from_west, from_east, from_outer, from_inner, held):
+def assemble(fields, from_west, from_east, from_outer, from_inner, main, side):
     is_top = lax.axis_index("row") == 7
     odd = lax.axis_index("row") % 2 + jnp.zeros((8, LANES), jnp.int32) == 1
-    lane = lane_index()
-    row = row_index()
-    first, last, low = lane == 0, lane == LANES - 1, lane < 64
-
     bottom = lax.axis_index("row") + jnp.zeros((8, LANES), jnp.int32) == 0
+    lane, row = lane_index(), row_index()
 
     def south(at):
         value = jnp.where(odd, from_inner[at : at + 8], from_outer[at : at + 8])
@@ -197,98 +199,107 @@
     def north(at):
         return jnp.where(odd, from_outer[at : at + 8], from_inner[at : at + 8])
 
-    def side_rows(message, f, a):
+    def rotated(value):
+        value = jnp.take_along_axis(value, LANES - 1 - lane, axis=1)
+        return jnp.take_along_axis(value, 7 - row, axis=0)
+
+    for f in range(SENT):
         base = 64 * (f % 2)
-        corner = message(SENT * HALO + 8 * (f // 2))
-        return jnp.where(low, turned(corner, -(base + 32 + 16 * a)), turned(corner, 112 - base - 16 * a))
-
-    for f in range(SENT):
-        a, b = from_west[8 * f : 8 * f + 8], from_east[8 * f : 8 * f + 8]
+        corner_at = SENT * HALO + 8 * (f // 2)
+        west_side, east_side = from_west[8 * f : 8 * f + 8], from_east[8 * f : 8 * f + 8]
+        south_side, north_side = south(corner_at), north(corner_at)
         for g in range(8):
-            at = PAD + HALO + 8 * g
-            held[f, 0, at : at + 8] = fields[f, 8 * g : 8 * g + 8]
-            held[f, 1, at : at + 8] = jnp.where(low, turned(b, -16 * g), turned(a, 112 - 16 * g))
+            main[f, PAD + HALO + 8 * g : PAD + HALO + 8 * g + 8] = fields[f, 8 * g : 8 * g + 8]
         for g in range(2):
-            at = PAD + 8 * g
-            held[f, 0, at : at + 8] = south(HALO * f + 8 * g)
-            held[f, 1, at : at + 8] = side_rows(south, f, g)
-
-    @pl.when(jnp.logical_not(is_top))
+            main[f, PAD + 8 * g : PAD + 8 * g + 8] = south(HALO * f + 8 * g)
+            main[f, TOP + 8 * g : TOP + 8 * g + 8] = north(HALO * f + 8 * g)
+        for j in range(3):
+            value = None
+            for b in range(4):
+                g = 3 * b + j
+                if g < 2:
+                    parts = (south_side, base + 16 * g), (south_side, base + 32 + 16 * g)
+                elif g < 10:
+                    parts = (west_side, 16 * (g - 2)), (east_side, 16 * (g - 2))
+                else:
+                    parts = (north_side, base + 16 * (g - 10)), (north_side, base + 32 + 16 * (g - 10))
+                for n, (part, origin) in enumerate(parts):
+                    to = 32 * b + 16 * n
+                    part = turned(part, to - origin)
+                    value = part if value is None else jnp.where(lane >= to, part, value)
+            side[f, PAD + 8 * j : PAD + 8 * j + 8] = value
+
+    def ghost(f, g):
+        a = 1 - g
+        base = 64 * (f % 2)
+        corner = north(SENT * HALO + 8 * (f // 2))
+        both = jnp.where(lane < 16, turned(corner, -base - 16 * a), turned(corner, -base - 16 - 16 * a))
+        return rotated(both), rotated(north(HALO * f + 8 * a))
+
+    def put_ghost(f, g, shift, tiles):
+        side_value, main_value = tiles
+        at, low = TOP + shift + 8 * g, PAD + 8 + shift + 8 * g
+        main[f, at : at + 8] = main_value
+        side[f, low : low + 8] = jnp.where(lane >= 96, side_value, side[f, low : low + 8])
+
+    @pl.when(is_top)
     def _():
         for f in range(SENT):
             for g in range(2):
-                at = TOP + 8 * g
-                held[f, 0, at : at + 8] = north(HALO * f + 8 * g)
-                held[f, 1, at : at + 8] = side_rows(north, f, g)
+                tiles = ghost(f, g)
+                if f in MOVING:
+                    tiles = east(tiles, (3,), lane)
+                    if f in NEGATED:
+                        tiles = [-value for value in tiles]
+                put_ghost(f, g, 0 if f in MOVING else 1, tiles)
+
+    for ref, tall in ((main, TALL), (side, SHORT)):
+        for at in range(PAD, tall - PAD, 8):
+            rows = slice(at, at + 8)
+            inertia, scale = ref[INE, rows], ref[AA, rows]
+            ref[AA, rows] = (inertia + 1.0) * scale
+            ref[BB, rows] = (inertia * (1.0 / 32.0)) * scale
+            ref[HWV, rows] = ref[HW, rows]
+            ref[HHV, rows] = ref[HH, rows]
 
     @pl.when(is_top)
     def _():
-        def rotated(value):
-            value = jnp.take_along_axis(value, LANES - 1 - lane, axis=1)
-            return jnp.take_along_axis(value, 7 - row, axis=0)
-
-        for f in range(SENT):
+        for f, own in ((HW, HWV), (HH, HHV)):
             for g in range(2):
-                source = 1 - g
-                main = rotated(north(HALO * f + 8 * source))
-                side = rotated(side_rows(north, f, source))
-                if f in MOVING:
-                    main, side = east(main, side, last)
-                    if f in NEGATED:
-                        main, side = -main, -side
-                    at = TOP + 8 * g
-                else:
-                    at = TOP + 1 + 8 * g
-                held[f, 0, at : at + 8] = main
-                held[f, 1, at : at + 8] = side
-                if f in (HW, HH):
-                    main, side = east(main, side, last)
-                    own = HWV if f == HW else HHV
-                    held[own, 0, TOP + 8 * g : TOP + 8 * g + 8] = main
-                    held[own, 1, TOP + 8 * g : TOP + 8 * g + 8] = side
-
-    for g in range(12):
-        at = PAD + 8 * g
-        for t in range(2):
-            scale = held[AA, t, at : at + 8]
-            inertia = held[INE, t, at : at + 8]
-            held[AA, t, at : at + 8] = (inertia + 1.0) * scale
-            held[BB, t, at : at + 8] = (inertia * (1.0 / 32.0)) * scale
-            if g < 10:
-                held[HWV, t, at : at + 8] = held[HW, t, at : at + 8]
-                held[HHV, t, at : at + 8] = held[HH, t, at : at + 8]
-        velocity_sums(
-            held,
-            at,
-            held[U, 0, at : at + 8],
-            held[U, 1, at : at + 8],
-            held[V, 0, at : at + 8],
-            held[V, 1, at : at + 8],
-            first,
-        )
-
-    @pl.when(jnp.logical_not(is_top))
-    def _():
-        for t in range(2):
-            held[HWV, t, TOP : TOP + HALO] = held[HW, t, TOP : TOP + HALO]
-            held[HHV, t, TOP : TOP + HALO] = held[HH, t, TOP : TOP + HALO]
-
-
-def velocity_sums(held, at, um, us, vm, vs, first):
-    wum, wus = west(um, us, first)
-    wvm, wvs = west(vm, vs, first)
-    for t, (x, wx, y, wy) in enumerate(((um, wum, vm, wvm), (us, wus, vs, wvs))):
-        held[DU, t, at : at + 8] = x - wx
-        held[SU, t, at : at + 8] = x + wx
-        held[DV, t, at : at + 8] = y - wy
-        held[SV, t, at : at + 8] = y + wy
-
-
-def stress_rows(held, at, last):
-    fresh = []
-    for t in range(2):
-        here = lambda f: held[f, t, at : at + 8]
-        below = lambda f: held[f, t, at - 1 : at + 7]
+                put_ghost(own, g, 0, east(ghost(f, g), (3,), lane))
+
+    for j in range(3):
+        tiles = unit(main, side, j, 0, 12)
+        u = [ref[U, at : at + 8] for ref, at in tiles]
+        v = [ref[V, at : at + 8] for ref, at in tiles]
+        velocity_sums(side, tiles, blocks_of(j, 0, 12), j, u, v, lane)
+
+
+def blocks_of(j, lo, hi):
+    return [b for b in range(4) if lo <= 3 * b + j < hi]
+
+
+def unit(main, side, j, lo, hi):
+    return [(side, PAD + 8 * j)] + [(main, PAD + 8 * (3 * b + j)) for b in blocks_of(j, lo, hi)]
+
+
+def velocity_sums(side, tiles, blocks, j, u, v, lane):
+    wu = west(u, blocks, lane)
+    wv = west(v, blocks, lane)
+    for (ref, at), x, wx, y, wy in zip(tiles, u, wu, v, wv):
+        made = ((DU, x - wx), (SU, x + wx), (DV, y - wy), (SV, y + wy))
+        for f, value in made:
+            ref[f, at : at + 8] = value
+            if ref is side and j == 2:
+                side[f, 0:PAD] = turned(value, 32)
+
+
+def stress_rows(main, side, j, lo, hi, lane):
+    tiles, blocks = unit(main, side, j, lo, hi), blocks_of(j, lo, hi)
+    ps, ms, qs = [], [], []
+    for ref, at in tiles:
+        here = lambda f: ref[f, at : at + 8]
+        below = lambda f: ref[f, at - 1 : at + 7]
         hw, hh = here(HW), here(HH)
         gux = hw * (here(DU) + below(DU))
         guy = hh * (here(SU) - below(SU))
@@ -305,34 +316,36 @@
         s1 = here(S1) * (2.0 / 3.0) + viscous * (divergence - deform)
         s2 = here(S2) * (2.0 / 3.0) + quarter * tension
         s12 = here(S12) * (2.0 / 3.0) + quarter * shearing
-        held[S1, t, at : at + 8] = s1
-        held[S2, t, at : at + 8] = s2
-        held[S12, t, at : at + 8] = s12
-        fresh.append((s1 + s2, s1 - s2, s12))
-    (pm, mm, qm), (ps, ms, qs) = fresh
-    epm, eps = east(pm, ps, last)
-    emm, ems = east(mm, ms, last)
-    eqm, eqs = east(qm, qs, last)
-    for t, (p, ep, m, em, q, eq) in enumerate(
-        ((pm, epm, mm, emm, qm, eqm), (ps, eps, ms, ems, qs, eqs))
-    ):
-        held[DP, t, at : at + 8] = ep - p
-        held[AM, t, at : at + 8] = em + m
-        held[DS, t, at : at + 8] = eq - q
-        held[AS, t, at : at + 8] = eq + q
-
-
-def velocity_rows(held, at, first, row, top_rows):
-    fresh = []
-    for t in range(2):
-        here = lambda f: held[f, t, at : at + 8]
+        ref[S1, at : at + 8] = s1
+        ref[S2, at : at + 8] = s2
+        ref[S12, at : at + 8] = s12
+        ps.append(s1 + s2)
+        ms.append(s1 - s2)
+        qs.append(s12)
+    for values, minus, plus in ((ps, DP, None), (ms, None, AM), (qs, DS, AS)):
+        for (ref, at), value, shifted in zip(tiles, values, east(values, blocks, lane)):
+            for f, made in ((minus, shifted - value), (plus, shifted + value)):
+                if f is not None:
+                    ref[f, at : at + 8] = made
+                    if ref is side and j == 0:
+                        side[f, PAD + BAND : SHORT] = turned(made, -32)
+
+
+def velocity_rows(main, side, j, lo, hi, lane, row, top_rows):
+    tiles, blocks = unit(main, side, j, lo, hi), blocks_of(j, lo, hi)
+    us, vs = [], []
+    for ref, at in tiles:
+        here = lambda f: ref[f, at : at + 8]
+        below_fold = at == (PAD if ref is side else TOP - 8)
+        above_fold = at == (PAD + 8 if ref is side else TOP)
+        affected = top_rows & (lane >= 96) if ref is side else top_rows
 
         def pair(f):
-            own, above = here(f), held[f, t, at + 1 : at + 9]
-            if at == TOP - 8:
-                above = jnp.where((row == 7) & top_rows, held[f, t, at + 2 : at + 10], above)
-            if at == TOP:
-                own = jnp.where((row == 0) & top_rows, held[f, t, at - 1 : at + 7], own)
+            own, above = here(f), ref[f, at + 1 : at + 9]
+            if below_fold:
+                above = jnp.where((row == 7) & affected, ref[f, at + 2 : at + 10], above)
+            if above_fold:
+                own = jnp.where((row == 0) & affected, ref[f, at - 1 : at + 7], own)
             return own, above
 
         hw, hh = here(HWV), here(HHV)
@@ -345,21 +358,23 @@
         y = inertia * here(V) + (hw * (ds + nds) + hh * (nam - am))
         u = a * x + b * y + here(KU)
         v = a * y - b * x + here(KV)
-        held[U, t, at : at + 8] = u
-        held[V, t, at : at + 8] = v
-        fresh.append((u, v))
-    (um, vm), (us, vs) = fresh
-    velocity_sums(held, at, um, us, vm, vs, first)
-
-
-def subcycles(held, start, stop, lo, hi):
-    first, last, row, top_rows = stencil_masks()
+        ref[U, at : at + 8] = u
+        ref[V, at : at + 8] = v
+        us.append(u)
+        vs.append(v)
+    velocity_sums(side, tiles, blocks, j, us, vs, lane)
+
+
+def subcycles(main, side, start, stop, lo, hi):
+    lane, row = lane_index(), row_index()
+    is_top = lax.axis_index("row") == 7
+    top_rows = (jnp.where(is_top, 1, 0) + jnp.zeros((8, LANES), jnp.int32)) == 1
 
     def body(_, carry):
-        for g in range(lo, hi):
-            stress_rows(held, PAD + 8 * g, last)
-        for g in range(lo, hi):
-            velocity_rows(held, PAD + 8 * g, first, row, top_rows)
+        for j in range(3):
+            stress_rows(main, side, j, lo, hi, lane)
+        for j in range(3):
+            velocity_rows(main, side, j, lo, hi, lane, row, top_rows)
         return carry
 
     lax.fori_loop(start, stop, body, 0)
@@ -381,13 +396,13 @@
 
 
 def first_half_kernel(
-    fields, from_west, from_east, from_outer, from_inner, snap, writer_hbm, held, out, flag, writer, zero, sems
+    fields, from_west, from_east, from_outer, from_inner, snap, writer_hbm, main, side, out, flag, writer, zero, sems
 ):
     me = lax.axis_index("row")
     read = pltpu.make_async_copy(writer_hbm, writer, sems.at[8])
     read.start()
     zero[...] = jnp.zeros_like(zero)
-    assemble(fields, from_west, from_east, from_outer, from_inner, held)
+    assemble(fields, from_west, from_east, from_outer, from_inner, main, side)
     read.wait()
     mine = writer[lax.axis_index("col")] == me
     flag[...] = jnp.where(mine, 1, 0) + jnp.zeros((8, LANES), jnp.int32)
@@ -403,8 +418,8 @@
         for copy in zeros:
             copy.start()
 
-    subcycles(held, 0, 5, 0, 12)
-    subcycles(held, 5, SPLIT, 1, 11)
+    subcycles(main, side, 0, 5, 0, 12)
+    subcycles(main, side, 5, SPLIT, 1, 11)
 
     @pl.when(mine)
     def _():
@@ -416,7 +431,9 @@
             copy.wait()
 
 
-def second_half_kernel(state, out_in, flag, near, near_back, far, vel, stress, held, out, sems):
+def second_half_kernel(
+    main_in, side_in, out_in, flag, near, near_back, far, vel, stress, main, side, out, sems
+):
     me = lax.axis_index("row")
     mine = jnp.max(flag[...]) == 1
     copies = [
@@ -430,13 +447,13 @@
         for copy in copies:
             copy.start()
 
-    subcycles(held, SPLIT, SUB, 1, 11)
+    subcycles(main, side, SPLIT, SUB, 1, 11)
     at = PAD + HALO
-    vel[0] = held[U, 0, at : at + ROWS]
-    vel[1] = held[V, 0, at : at + ROWS]
-    stress[0] = 2.0 * held[S1, 0, at : at + ROWS]
-    stress[1] = 2.0 * held[S2, 0, at : at + ROWS]
-    stress[2] = held[S12, 0, at : at + ROWS]
+    vel[0] = main[U, at : at + ROWS]
+    vel[1] = main[V, at : at + ROWS]
+    stress[0] = 2.0 * main[S1, at : at + ROWS]
+    stress[1] = 2.0 * main[S2, at : at + ROWS]
+    stress[2] = main[S12, at : at + ROWS]
 
     @pl.when(mine)
     def _():
@@ -557,15 +574,16 @@
     far = lax.ppermute(near, "row", along)
 
     hbm = lambda: pl.BlockSpec(memory_space=pl.ANY)
-    state, restart, flag = pl.pallas_call(
+    main, packed, restart, flag = pl.pallas_call(
         first_half_kernel,
         out_shape=(
-            shape(HELD, 2, TALL, LANES),
+            shape(HELD, TALL, LANES),
+            shape(HELD, SHORT, LANES),
             shape(1, 10, 8 * ROWS, LANES),
             jax.ShapeDtypeStruct((8, LANES), jnp.int32),
         ),
         in_specs=[vmem()] * 5 + [hbm(), hbm()],
-        out_specs=(vmem(), hbm(), vmem()),
+        out_specs=(vmem(), vmem(), hbm(), vmem()),
         scratch_shapes=[
             pltpu.SMEM((32,), jnp.int32),
             pltpu.VMEM((10, ROWS, LANES), jnp.float32),
@@ -594,22 +612,23 @@
     )(snap, near, near_back, far)
     partner_blocks = lax.ppermute(joined, "row", partner)
 
-    velocity, stress, _, restart = pl.pallas_call(
+    velocity, stress, _, _, restart = pl.pallas_call(
         second_half_kernel,
         out_shape=(
             shape(2, ROWS, LANES),
             shape(3, ROWS, LANES),
-            shape(HELD, 2, TALL, LANES),
+            shape(HELD, TALL, LANES),
+            shape(HELD, SHORT, LANES),
             shape(1, 10, 8 * ROWS, LANES),
         ),
-        in_specs=[vmem(), hbm(), vmem(), hbm(), hbm(), hbm()],
-        out_specs=(vmem(), vmem(), vmem(), hbm()),
-        input_output_aliases={0: 2, 1: 3},
+        in_specs=[vmem(), vmem(), hbm(), vmem(), hbm(), hbm(), hbm()],
+        out_specs=(vmem(), vmem(), vmem(), vmem(), hbm()),
+        input_output_aliases={0: 2, 1: 3, 2: 4},
         scratch_shapes=[pltpu.SemaphoreType.DMA((3,))],
         compiler_params=grant(8),
         cost_estimate=pl.CostEstimate(flops=20000000, bytes_accessed=2000000, transcendentals=0),
         name="second_half",
-    )(state, restart, flag, near, near_back, far)
+    )(main, packed, restart, flag, near, near_back, far)
 
     restart = pl.pallas_call(
         last_kernel,

time: 45.7 us -> 47.2 us (1.033)
  Pallas kernels: 7.96 us -> 9.45 us
    pallas_call x1, Pallas kernels: 3.31 us -> 4.33 us  [step(): pl.pallas_call(first_half_kernel, out_shape=(shape(HELD, TALL, LANES), sh...]
    pallas_call x1, Pallas kernels: 2.51 us -> 2.98 us  [step(): pl.pallas_call(second_half_kernel, out_shape=(shape(2, ROWS, LANES), shap...]
  transfers between devices with their start and end apart: 8 -> 8, of which waited for: 5 -> 5; matrix products, arithmetic and copies ran while one was open for 0% -> 0% of each run, Pallas kernels for 13% -> 16%
where the time goes in v6:
time: 47.2 us; the launch traced here: 47.1 us
  starting transfers between devices  20.3 us (43%)
  waiting for transfers between devices  16.6 us (35%)
  Pallas kernels  9.45 us (20%)
  between operations  0.7 us (1%)
    ppermute x1, starting transfers between devices, step(): from_east = lax.ppermute(to_west, 'col', westward)  6.39 us
    ppermute x1, starting transfers between devices, step(): from_outer = lax.ppermute(outer, ('row', 'col'), across)  6.14 us
    ppermute x1, waiting for transfers between devices, step(): near = lax.ppermute(snap, 'row', along)  4.94 us
    ppermute x1, waiting for transfers between devices, step(): far = lax.ppermute(near, 'row', along)  4.91 us
    pallas_call x1, Pallas kernels, step(): pl.pallas_call(first_half_kernel, out_shape=(shape(HELD, TALL, LANES), sh...  4.33 us
    ppermute x1, starting transfers between devices, step(): partner_blocks = lax.ppermute(joined, 'row', partner)  4.22 us
    pallas_call x1, Pallas kernels, step(): pl.pallas_call(second_half_kernel, out_shape=(shape(2, ROWS, LANES), shap...  2.98 us
    ppermute x1, waiting for transfers between devices, step(): from_outer = lax.ppermute(outer, ('row', 'col'), across)  2.69 us
  transfers between devices with their start and end apart: 8, of which 5 were waited for; matrix products, arithmetic and copies ran while one was open for 0% of the time, Pallas kernels for 16%

profile of v6, /device:TPU:7, one launch (start us, length us, event | category | flops | bytes accessed | tf_op | source)
XLA Modules:
  0.0 47.1 jit_solution(6290845994192949946)
XLA Ops:
  0.6 1.7 %prepare.1 = (f32[12,64,128]{2,1,0:T(8,128)S(1)}, f32[96,128]{1,0:T(8,128)S(1)}, f32[96,128]{1,0:T(8,128)S(1)}, f32[10,64,128]{2,1,0:T(8,128)S(1)}) custom-call(f32[2,64,128]{2,1,0:T(8,128)} %vel_hbm.1, f32[3,64,128]{2,1,0:T(8,128)} %stress_hbm.1, f32[2,64,128]{2,1,0:T(8,128)} %wind_hbm.1, f32[2,64,128]{2,1,0:T(8,128)} %ocean_hbm.1, f32[5,64,128]{2,1,0:T(8,128)} %area_hbm.1, ...), custom_call_target="tpu_custom_call" | custom-call | tf_op jit(solution)/shard_map/prepare/pallas_call | solution.py:507
  2.4 0.6 %collective-permute-start.4 = (f32[10,64,128]{2,1,0:T(8,128)S(1)}, f32[10,64,128]{2,1,0:T(8,128)S(1)}, u32[]{:S(2)}, u32[]{:S(2)}) collective-permute-start(f32[10,64,128]{2,1,0:T(8,128)S(1)} %get-tuple-element.21.snap.own), channel_id=1, source_target_pairs={{0,64},{32,224},{64,128},{96,32},{128,192},{160,96},{192,0},{224,1... | collective-permute-start | bytes 983048 | tf_op jit(solution)/shard_map/ppermute | solution.py:558
  3.0 2.1 %collective-permute-start.5 = (f32[10,64,128]{2,1,0:T(8,128)S(1)}, f32[10,64,128]{2,1,0:T(8,128)S(1)}, u32[]{:S(2)}, u32[]{:S(2)}) collective-permute-start(f32[10,64,128]{2,1,0:T(8,128)S(1)} %get-tuple-element.21.snap.own), channel_id=1, source_target_pairs={{0,192},{32,96},{64,0},{96,160},{128,64},{160,224},{192,128},{224,... | collective-permute-start | bytes 983048 | tf_op jit(solution)/shard_map/ppermute | solution.py:561
  5.1 4.9 %collective-permute-done.4.near = f32[10,64,128]{2,1,0:T(8,128)S(1)} collective-permute-done((f32[10,64,128]{2,1,0:T(8,128)S(1)}, f32[10,64,128]{2,1,0:T(8,128)S(1)}, u32[]{:S(2)}, u32[]{:S(2)}) %collective-permute-start.4) | collective-permute-done | bytes 327712 | tf_op jit(solution)/shard_map/ppermute | solution.py:558
  10.0 0.2 collective-permute-start.6
  10.2 2.1 %collective-permute-done.5.near_back = f32[10,64,128]{2,1,0:T(8,128)S(1)} collective-permute-done((f32[10,64,128]{2,1,0:T(8,128)S(1)}, f32[10,64,128]{2,1,0:T(8,128)S(1)}, u32[]{:S(2)}, u32[]{:S(2)}) %collective-permute-start.5) | collective-permute-done | bytes 327712 | tf_op jit(solution)/shard_map/ppermute | solution.py:561
  12.3 4.9 %collective-permute-done.6.far = f32[10,64,128]{2,1,0:T(8,128)S(1)} collective-permute-done((f32[10,64,128]{2,1,0:T(8,128)S(1)}, f32[10,64,128]{2,1,0:T(8,128)S(1)}, u32[]{:S(2)}, u32[]{:S(2)}) %collective-permute-start.6) | collective-permute-done | bytes 327712 | tf_op jit(solution)/shard_map/ppermute | solution.py:574
  17.2 0.1 join.1
  17.3 4.2 %collective-permute-start.7 = (f32[4,10,64,128]{3,2,1,0:T(8,128)S(1)}, f32[4,10,64,128]{3,2,1,0:T(8,128)S(1)}, u32[]{:S(2)}, u32[]{:S(2)}) collective-permute-start(f32[4,10,64,128]{3,2,1,0:T(8,128)S(1)} %join.1), channel_id=1, source_target_pairs={{0,32},{32,0},{64,96},{96,64},{128,160},{160,128},{192,224},{224,1... | collective-permute-start | bytes 3932168 | tf_op jit(solution)/shard_map/ppermute | solution.py:613
  21.5 0.5 %collective-permute-start = (f32[96,128]{1,0:T(8,128)S(1)}, f32[96,128]{1,0:T(8,128)S(1)}, u32[]{:S(2)}, u32[]{:S(2)}) collective-permute-start(f32[96,128]{1,0:T(8,128)S(1)} %get-tuple-element.17), channel_id=1, source_target_pairs={{0,1},{1,2},{2,3},{3,4},{4,5},{5,6},{6,7},{7,8},{8,9},{9,10},{10,1... | collective-permute-start | bytes 147464 | tf_op jit(solution)/shard_map/ppermute | solution.py:559
  22.0 6.4 %collective-permute-start.1 = (f32[96,128]{1,0:T(8,128)S(1)}, f32[96,128]{1,0:T(8,128)S(1)}, u32[]{:S(2)}, u32[]{:S(2)}) collective-permute-start(f32[96,128]{1,0:T(8,128)S(1)} %get-tuple-element.18), channel_id=1, source_target_pairs={{0,31},{1,0},{2,1},{3,2},{4,3},{5,4},{6,5},{7,6},{8,7},{9,8},{10,9... | collective-permute-start | bytes 147464 | tf_op jit(solution)/shard_map/ppermute | solution.py:560
  28.4 2.0 %collective-permute-done.from_west = f32[96,128]{1,0:T(8,128)S(1)} collective-permute-done((f32[96,128]{1,0:T(8,128)S(1)}, f32[96,128]{1,0:T(8,128)S(1)}, u32[]{:S(2)}, u32[]{:S(2)}) %collective-permute-start) | collective-permute-done | bytes 49184 | tf_op jit(solution)/shard_map/ppermute | solution.py:559
  30.4 0.0 collective-permute-done.1.from_east
  30.4 0.1 rows.1
  30.5 6.1 %collective-permute-start.2 = (f32[240,128]{1,0:T(8,128)S(1)}, f32[240,128]{1,0:T(8,128)S(1)}, u32[]{:S(2)}, u32[]{:S(2)}) collective-permute-start(f32[240,128]{1,0:T(8,128)S(1)} %get-tuple-element.19), channel_id=1, source_target_pairs={{224,255},{225,254},{226,253},{227,252},{228,251},{229,250},{230,2... | collective-permute-start | bytes 368648 | tf_op jit(solution)/shard_map/ppermute | solution.py:572
  36.7 0.1 collective-permute-start.3
  36.8 2.7 %collective-permute-done.2.from_outer = f32[240,128]{1,0:T(8,128)S(1)} collective-permute-done((f32[240,128]{1,0:T(8,128)S(1)}, f32[240,128]{1,0:T(8,128)S(1)}, u32[]{:S(2)}, u32[]{:S(2)}) %collective-permute-start.2) | collective-permute-done | bytes 122912 | tf_op jit(solution)/shard_map/ppermute | solution.py:572
  39.5 0.0 collective-permute-done.3.from_inner
  39.5 4.3 %first_half.1 = (f32[23,112,128]{2,1,0:T(8,128)S(1)}, f32[23,40,128]{2,1,0:T(8,128)S(1)}, f32[1,10,512,128]{3,2,1,0:T(8,128)}, s32[8,128]{1,0:T(8,128)S(1)}) custom-call(f32[12,64,128]{2,1,0:T(8,128)S(1)} %get-tuple-element.16.fields, f32[96,128]{1,0:T(8,128)S(1)} %collective-permute-done.from_west, f32[96,128]{1,0:T(8,128)S(1)} %collective-permute-done.1.from_east, ...), custom_call_target="tpu_custom_call" | custom-call | flops 20000000 | bytes 2000000 | tf_op jit(solution)/shard_map/first_half/pallas_call | solution.py:577
  43.8 3.0 %second_half.1 = (f32[2,64,128]{2,1,0:T(8,128)}, f32[3,64,128]{2,1,0:T(8,128)}, f32[23,112,128]{2,1,0:T(8,128)S(1)}, f32[23,40,128]{2,1,0:T(8,128)S(1)}, f32[1,10,512,128]{3,2,1,0:T(8,128)}) custom-call(f32[23,112,128]{2,1,0:T(8,128)S(1)} %get-tuple-element.22.main_in, ...), custom_call_target="tpu_custom_call", output_to_operand_aliasing={{2}: (0, {}), {3}: (1, {}), {4}: (2, {})} | custom-call | flops 20000000 | bytes 2000000 | tf_op jit(solution)/shard_map/second_half/pallas_call | solution.py:615
  46.8 0.0 collective-permute-done.7.partner
  46.8 0.2 last.1
Async XLA Ops:
  2.4 7.7 %collective-permute-start.4 = (f32[10,64,128]{2,1,0:T(8,128)S(1)}, f32[10,64,128]{2,1,0:T(8,128)S(1)}, u32[]{:S(2)}, u32[]{:S(2)}) collective-permute-start(f32[10,64,128]{2,1,0:T(8,128)S(1)} %get-tuple-element.21.snap.own), channel_id=1, source_target_pairs={{0,64},{32,224},{64,128},{96,32},{128,192},{160,96},{192,0},{224,1... | collective-permute-start | bytes 983048 | tf_op jit(solution)/shard_map/ppermute | solution.py:558
  3.0 9.3 %collective-permute-start.5 = (f32[10,64,128]{2,1,0:T(8,128)S(1)}, f32[10,64,128]{2,1,0:T(8,128)S(1)}, u32[]{:S(2)}, u32[]{:S(2)}) collective-permute-start(f32[10,64,128]{2,1,0:T(8,128)S(1)} %get-tuple-element.21.snap.own), channel_id=1, source_target_pairs={{0,192},{32,96},{64,0},{96,160},{128,64},{160,224},{192,128},{224,... | collective-permute-start | bytes 983048 | tf_op jit(solution)/shard_map/ppermute | solution.py:561
  10.0 7.1 %collective-permute-start.6 = (f32[10,64,128]{2,1,0:T(8,128)S(1)}, f32[10,64,128]{2,1,0:T(8,128)S(1)}, u32[]{:S(2)}, u32[]{:S(2)}) collective-permute-start(f32[10,64,128]{2,1,0:T(8,128)S(1)} %collective-permute-done.4.near), channel_id=1, source_target_pairs={{0,64},{32,224},{64,128},{96,32},{128,192},{160,96},{192,0},{224,1... | collective-permute-start | bytes 983048 | tf_op jit(solution)/shard_map/ppermute | solution.py:574
  17.3 29.5 %collective-permute-start.7 = (f32[4,10,64,128]{3,2,1,0:T(8,128)S(1)}, f32[4,10,64,128]{3,2,1,0:T(8,128)S(1)}, u32[]{:S(2)}, u32[]{:S(2)}) collective-permute-start(f32[4,10,64,128]{3,2,1,0:T(8,128)S(1)} %join.1), channel_id=1, source_target_pairs={{0,32},{32,0},{64,96},{96,64},{128,160},{160,128},{192,224},{224,1... | collective-permute-start | bytes 3932168 | tf_op jit(solution)/shard_map/ppermute | solution.py:613
  21.5 8.9 %collective-permute-start = (f32[96,128]{1,0:T(8,128)S(1)}, f32[96,128]{1,0:T(8,128)S(1)}, u32[]{:S(2)}, u32[]{:S(2)}) collective-permute-start(f32[96,128]{1,0:T(8,128)S(1)} %get-tuple-element.17), channel_id=1, source_target_pairs={{0,1},{1,2},{2,3},{3,4},{4,5},{5,6},{6,7},{7,8},{8,9},{9,10},{10,1... | collective-permute-start | bytes 147464 | tf_op jit(solution)/shard_map/ppermute | solution.py:559
  22.0 8.4 %collective-permute-start.1 = (f32[96,128]{1,0:T(8,128)S(1)}, f32[96,128]{1,0:T(8,128)S(1)}, u32[]{:S(2)}, u32[]{:S(2)}) collective-permute-start(f32[96,128]{1,0:T(8,128)S(1)} %get-tuple-element.18), channel_id=1, source_target_pairs={{0,31},{1,0},{2,1},{3,2},{4,3},{5,4},{6,5},{7,6},{8,7},{9,8},{10,9... | collective-permute-start | bytes 147464 | tf_op jit(solution)/shard_map/ppermute | solution.py:560
  30.5 8.9 %collective-permute-start.2 = (f32[240,128]{1,0:T(8,128)S(1)}, f32[240,128]{1,0:T(8,128)S(1)}, u32[]{:S(2)}, u32[]{:S(2)}) collective-permute-start(f32[240,128]{1,0:T(8,128)S(1)} %get-tuple-element.19), channel_id=1, source_target_pairs={{224,255},{225,254},{226,253},{227,252},{228,251},{229,250},{230,2... | collective-permute-start | bytes 368648 | tf_op jit(solution)/shard_map/ppermute | solution.py:572
  36.7 2.8 %collective-permute-start.3 = (f32[240,128]{1,0:T(8,128)S(1)}, f32[240,128]{1,0:T(8,128)S(1)}, u32[]{:S(2)}, u32[]{:S(2)}) collective-permute-start(f32[240,128]{1,0:T(8,128)S(1)} %get-tuple-element.20), channel_id=1, source_target_pairs={{0,32},{32,0},{64,96},{96,64},{128,160},{160,128},{192,224},{224,1... | collective-permute-start | bytes 368648 | tf_op jit(solution)/shard_map/ppermute | solution.py:573

commit v7 on v5

--- a/solution.py
+++ b/solution.py
@@ -71,10 +71,13 @@
     high_hbm,
     land_hbm,
     ice_hbm,
+    writer_hbm,
     fields,
     to_west,
     to_east,
     snap,
+    flag,
+    blank,
     vel,
     stress,
     wind,
@@ -83,6 +86,7 @@
     high,
     land_t,
     ice_t,
+    writer,
     sems,
 ):
     area, volume = snap.at[0:5], snap.at[5:10]
@@ -97,12 +101,16 @@
         (vel_hbm, vel),
         (wide_hbm, wide),
         (high_hbm, high),
+        (writer_hbm, writer),
     )
     copies = [pltpu.make_async_copy(a, b, sems.at[n]) for n, (a, b) in enumerate(moves)]
     for copy in copies:
         copy.start()
+    blank[...] = jnp.zeros_like(blank)
     for copy in copies:
         copy.wait()
+    mine = writer[lax.axis_index("col")] == lax.axis_index("row")
+    flag[...] = jnp.where(mine, 1, 0) + jnp.zeros((8, LANES), jnp.int32)
     land = expanded(land_t[...].astype(jnp.float32))
     ice = expanded(ice_t[...].astype(jnp.float32))
     area_total = area[0] + area[1] + area[2] + area[3] + area[4]
@@ -381,16 +389,10 @@
 
 
 def first_half_kernel(
-    fields, from_west, from_east, from_outer, from_inner, snap, writer_hbm, held, out, flag, writer, zero, sems
+    fields, from_west, from_east, from_outer, from_inner, snap, flag, zero, held, out, sems
 ):
     me = lax.axis_index("row")
-    read = pltpu.make_async_copy(writer_hbm, writer, sems.at[8])
-    read.start()
-    zero[...] = jnp.zeros_like(zero)
-    assemble(fields, from_west, from_east, from_outer, from_inner, held)
-    read.wait()
-    mine = writer[lax.axis_index("col")] == me
-    flag[...] = jnp.where(mine, 1, 0) + jnp.zeros((8, LANES), jnp.int32)
+    mine = jnp.max(flag[...]) == 1
     zeros = [into(out, zero, n * ROWS, sems.at[n]) for n in range(8)]
     own = into(out, snap, place_of(me, 0), sems.at[0])
 
@@ -403,6 +405,7 @@
         for copy in zeros:
             copy.start()
 
+    assemble(fields, from_west, from_east, from_outer, from_inner, held)
     subcycles(held, 0, 5, 0, 12)
     subcycles(held, 5, SPLIT, 1, 11)
 
@@ -416,13 +419,12 @@
             copy.wait()
 
 
-def second_half_kernel(state, out_in, flag, near, near_back, far, vel, stress, held, out, sems):
+def second_half_kernel(state, out_in, flag, near, near_back, vel, stress, held, out, sems):
     me = lax.axis_index("row")
     mine = jnp.max(flag[...]) == 1
     copies = [
         into(out, near, place_of(me, 1), sems.at[0]),
         into(out, near_back, place_of(me, 2), sems.at[1]),
-        into(out, far, place_of(me, 3), sems.at[2]),
     ]
 
     @pl.when(mine)
@@ -444,21 +446,34 @@
             copy.wait()
 
 
-def last_kernel(out_in, flag, partner, out, sems):
+def last_kernel(
+    out_in, flag, vel, stress, far, partner, partner_far, out, vel_out, stress_out, sems
+):
     me = lax.axis_index("row")
+    fields_out = [
+        pltpu.make_async_copy(vel, vel_out, sems.at[5]),
+        pltpu.make_async_copy(stress, stress_out, sems.at[6]),
+    ]
+    for copy in fields_out:
+        copy.start()
     mine = jnp.max(flag[...]) == 1
 
     @pl.when(mine)
     def _():
-        copies = [into(out, partner.at[n], place_of(me, 4 + n), sems.at[n]) for n in range(4)]
+        copies = [into(out, partner.at[n], place_of(me, 4 + n), sems.at[n]) for n in range(3)]
+        copies.append(into(out, partner_far, place_of(me, 7), sems.at[3]))
+        copies.append(into(out, far, place_of(me, 3), sems.at[4]))
         for copy in copies:
             copy.start()
         for copy in copies:
             copy.wait()
 
-
-def join_kernel(own, near, near_back, far, joined):
-    for n, block in enumerate((own, near, near_back, far)):
+    for copy in fields_out:
+        copy.wait()
+
+
+def join_kernel(own, near, near_back, joined):
+    for n, block in enumerate((own, near, near_back)):
         joined[n] = block[...]
 
 
@@ -487,16 +502,18 @@
     ice_block,
     writer,
 ):
-    fields, to_west, to_east, snap = pl.pallas_call(
+    fields, to_west, to_east, snap, flag, blank = pl.pallas_call(
         prepare_kernel,
         out_shape=(
             shape(SENT, ROWS, LANES),
             shape(SENT * 8, LANES),
             shape(SENT * 8, LANES),
             shape(10, ROWS, LANES),
+            jax.ShapeDtypeStruct((8, LANES), jnp.int32),
+            shape(10, ROWS, LANES),
         ),
-        in_specs=[pl.BlockSpec(memory_space=pltpu.HBM)] * 10,
-        out_specs=(vmem(),) * 4,
+        in_specs=[pl.BlockSpec(memory_space=pltpu.HBM)] * 11,
+        out_specs=(vmem(),) * 6,
         scratch_shapes=[
             pltpu.VMEM((2, ROWS, LANES), jnp.float32),
             pltpu.VMEM((3, ROWS, LANES), jnp.float32),
@@ -506,7 +523,8 @@
             pltpu.VMEM((ROWS, LANES), jnp.float32),
             pltpu.VMEM((4, 16), jnp.int32),
             pltpu.VMEM((4, 16), jnp.int32),
-            pltpu.SemaphoreType.DMA((10,)),
+            pltpu.SMEM((32,), jnp.int32),
+            pltpu.SemaphoreType.DMA((11,)),
         ],
         compiler_params=grant(8),
         name="prepare",
@@ -524,6 +542,7 @@
                 inverse_height,
                 land_block.T,
                 ice_block.T,
+                writer,
             )
         )
     )
@@ -533,7 +552,7 @@
     eastward = [(c, (c + 1) % 32) for c in range(32)]
     westward = [(c, (c - 1) % 32) for c in range(32)]
     across = [(7 * 32 + c, 7 * 32 + 31 - c) for c in range(32)]
-    across += [(c, c) for c in range(32)]
+    across += [(c, c ^ 1) for c in range(32)]
     for c in range(32):
         for r in (1, 3, 5):
             across += [(32 * r + c, 32 * r + 32 + c), (32 * r + 32 + c, 32 * r + c)]
@@ -557,41 +576,25 @@
     far = lax.ppermute(near, "row", along)
 
     hbm = lambda: pl.BlockSpec(memory_space=pl.ANY)
-    state, restart, flag = pl.pallas_call(
+    state, restart = pl.pallas_call(
         first_half_kernel,
-        out_shape=(
-            shape(HELD, 2, TALL, LANES),
-            shape(1, 10, 8 * ROWS, LANES),
-            jax.ShapeDtypeStruct((8, LANES), jnp.int32),
-        ),
-        in_specs=[vmem()] * 5 + [hbm(), hbm()],
-        out_specs=(vmem(), hbm(), vmem()),
-        scratch_shapes=[
-            pltpu.SMEM((32,), jnp.int32),
-            pltpu.VMEM((10, ROWS, LANES), jnp.float32),
-            pltpu.SemaphoreType.DMA((9,)),
-        ],
+        out_shape=(shape(HELD, 2, TALL, LANES), shape(1, 10, 8 * ROWS, LANES)),
+        in_specs=[vmem()] * 5 + [hbm(), vmem(), hbm()],
+        out_specs=(vmem(), hbm()),
+        scratch_shapes=[pltpu.SemaphoreType.DMA((8,))],
         compiler_params=grant(16),
         cost_estimate=pl.CostEstimate(flops=20000000, bytes_accessed=2000000, transcendentals=0),
         name="first_half",
-    )(
-        fields,
-        from_west,
-        from_east,
-        from_outer,
-        from_inner,
-        snap,
-        pltpu.with_memory_space_constraint(writer, pltpu.HBM),
-    )
+    )(fields, from_west, from_east, from_outer, from_inner, snap, flag, blank)
 
     joined = pl.pallas_call(
         join_kernel,
-        out_shape=shape(4, 10, ROWS, LANES),
-        in_specs=[vmem()] * 4,
+        out_shape=shape(3, 10, ROWS, LANES),
+        in_specs=[vmem()] * 3,
         out_specs=vmem(),
         compiler_params=grant(8),
         name="join",
-    )(snap, near, near_back, far)
+    )(snap, near, near_back)
     partner_blocks = lax.ppermute(joined, "row", partner)
 
     velocity, stress, _, restart = pl.pallas_call(
@@ -602,25 +605,30 @@
             shape(HELD, 2, TALL, LANES),
             shape(1, 10, 8 * ROWS, LANES),
         ),
-        in_specs=[vmem(), hbm(), vmem(), hbm(), hbm(), hbm()],
+        in_specs=[vmem(), hbm(), vmem(), hbm(), hbm()],
         out_specs=(vmem(), vmem(), vmem(), hbm()),
         input_output_aliases={0: 2, 1: 3},
-        scratch_shapes=[pltpu.SemaphoreType.DMA((3,))],
+        scratch_shapes=[pltpu.SemaphoreType.DMA((2,))],
         compiler_params=grant(8),
         cost_estimate=pl.CostEstimate(flops=20000000, bytes_accessed=2000000, transcendentals=0),
         name="second_half",
-    )(state, restart, flag, near, near_back, far)
-
-    restart = pl.pallas_call(
+    )(state, restart, flag, near, near_back)
+    partner_far = lax.ppermute(far, "row", partner)
+
+    restart, velocity, stress = pl.pallas_call(
         last_kernel,
-        out_shape=shape(1, 10, 8 * ROWS, LANES),
-        in_specs=[hbm(), vmem(), hbm()],
-        out_specs=hbm(),
+        out_shape=(
+            shape(1, 10, 8 * ROWS, LANES),
+            shape(2, ROWS, LANES),
+            shape(3, ROWS, LANES),
+        ),
+        in_specs=[hbm(), vmem()] + [hbm()] * 5,
+        out_specs=(hbm(), hbm(), hbm()),
         input_output_aliases={0: 0},
-        scratch_shapes=[pltpu.SemaphoreType.DMA((4,))],
+        scratch_shapes=[pltpu.SemaphoreType.DMA((7,))],
         compiler_params=grant(4),
         name="last",
-    )(restart, flag, partner_blocks)
+    )(restart, flag, velocity, stress, far, partner_blocks, partner_far)
     return (velocity, stress, restart)
 
 

time: 45.7 us -> 44.7 us (0.978)
  the two profiles are of different devices: /device:TPU:7 before, /device:TPU:1 now
where the time goes in v7:
time: 44.7 us; the launch traced here: 44.6 us
  waiting for transfers between devices  22.8 us (51%)
  starting transfers between devices  13.6 us (30%)
  Pallas kernels  7.54 us (17%)
  between operations  0.7 us (2%)
    ppermute x1, waiting for transfers between devices, step(): near_back = lax.ppermute(snap, 'row', against)  6.55 us
    ppermute x1, starting transfers between devices, step(): from_east = lax.ppermute(to_west, 'col', westward)  6.39 us
    ppermute x1, waiting for transfers between devices, step(): far = lax.ppermute(near, 'row', along)  6.22 us
    ppermute x1, waiting for transfers between devices, step(): near = lax.ppermute(snap, 'row', along)  4.02 us
    ppermute x1, waiting for transfers between devices, step(): from_outer = lax.ppermute(outer, ('row', 'col'), across)  3.92 us
    ppermute x1, starting transfers between devices, step(): near = lax.ppermute(snap, 'row', along)  3.37 us
    pallas_call x1, Pallas kernels, step(): pl.pallas_call(first_half_kernel, out_shape=(shape(HELD, 2, TALL, LANES),...  3.04 us
    ppermute x1, starting transfers between devices, step(): partner_far = lax.ppermute(far, 'row', partner)  2.16 us
  transfers between devices with their start and end apart: 9, of which 5 were waited for; matrix products, arithmetic and copies ran while one was open for 0% of the time, Pallas kernels for 11%

profile of v7, /device:TPU:1, one launch (start us, length us, event | category | flops | bytes accessed | tf_op | source)
XLA Modules:
  0.0 44.6 jit_solution(5036224505789805294)
XLA Ops:
  0.6 1.7 %prepare.1 = (f32[12,64,128]{2,1,0:T(8,128)S(1)}, f32[96,128]{1,0:T(8,128)S(1)}, f32[96,128]{1,0:T(8,128)S(1)}, f32[10,64,128]{2,1,0:T(8,128)S(1)}, s32[8,128]{1,0:T(8,128)S(1)}, /*index=5*/f32[10,64,128]{2,1,0:T(8,128)S(1)}) custom-call(f32[2,64,128]{2,1,0:T(8,128)} %vel_hbm.1, f32[3,64,128]{2,1,0:T(8,128)} %stress_hbm.1, f32[2,64,128]{2,1,0:T(8,128)} %wind_hbm.1, ...), custom_call_target="tpu_custom_call" | custom-call | tf_op jit(solution)/shard_map/prepare/pallas_call | solution.py:505
  2.4 3.4 %collective-permute-start.4 = (f32[10,64,128]{2,1,0:T(8,128)S(1)}, f32[10,64,128]{2,1,0:T(8,128)S(1)}, u32[]{:S(2)}, u32[]{:S(2)}) collective-permute-start(f32[10,64,128]{2,1,0:T(8,128)S(1)} %get-tuple-element.24.snap.own), channel_id=1, source_target_pairs={{0,64},{32,224},{64,128},{96,32},{128,192},{160,96},{192,0},{224,1... | collective-permute-start | bytes 983048 | tf_op jit(solution)/shard_map/ppermute | solution.py:560
  5.8 0.0 collective-permute-start.5
  5.8 4.0 %collective-permute-done.4.near = f32[10,64,128]{2,1,0:T(8,128)S(1)} collective-permute-done((f32[10,64,128]{2,1,0:T(8,128)S(1)}, f32[10,64,128]{2,1,0:T(8,128)S(1)}, u32[]{:S(2)}, u32[]{:S(2)}) %collective-permute-start.4) | collective-permute-done | bytes 327712 | tf_op jit(solution)/shard_map/ppermute | solution.py:560
  9.8 6.6 %collective-permute-done.5.near_back = f32[10,64,128]{2,1,0:T(8,128)S(1)} collective-permute-done((f32[10,64,128]{2,1,0:T(8,128)S(1)}, f32[10,64,128]{2,1,0:T(8,128)S(1)}, u32[]{:S(2)}, u32[]{:S(2)}) %collective-permute-start.5) | collective-permute-done | bytes 327712 | tf_op jit(solution)/shard_map/ppermute | solution.py:563
  16.3 0.1 join.1
  16.4 0.9 %collective-permute-start.7 = (f32[3,10,64,128]{3,2,1,0:T(8,128)S(1)}, f32[3,10,64,128]{3,2,1,0:T(8,128)S(1)}, u32[]{:S(2)}, u32[]{:S(2)}) collective-permute-start(f32[3,10,64,128]{3,2,1,0:T(8,128)S(1)} %join.1), channel_id=1, source_target_pairs={{0,32},{32,0},{64,96},{96,64},{128,160},{160,128},{192,224},{224,1... | collective-permute-start | bytes 2949128 | tf_op jit(solution)/shard_map/ppermute | solution.py:598
  17.2 0.0 collective-permute-start.6
  17.3 6.2 %collective-permute-done.6.far = f32[10,64,128]{2,1,0:T(8,128)S(1)} collective-permute-done((f32[10,64,128]{2,1,0:T(8,128)S(1)}, f32[10,64,128]{2,1,0:T(8,128)S(1)}, u32[]{:S(2)}, u32[]{:S(2)}) %collective-permute-start.6) | collective-permute-done | bytes 327712 | tf_op jit(solution)/shard_map/ppermute | solution.py:576
  23.5 2.2 %collective-permute-start.8 = (f32[10,64,128]{2,1,0:T(8,128)S(1)}, f32[10,64,128]{2,1,0:T(8,128)S(1)}, u32[]{:S(2)}, u32[]{:S(2)}) collective-permute-start(f32[10,64,128]{2,1,0:T(8,128)S(1)} %collective-permute-done.6.far), channel_id=1, source_target_pairs={{0,32},{32,0},{64,96},{96,64},{128,160},{160,128},{192,224},{224,1... | collective-permute-start | bytes 983048 | tf_op jit(solution)/shard_map/ppermute | solution.py:616
  25.6 0.0 collective-permute-start
  25.6 6.4 %collective-permute-start.1 = (f32[96,128]{1,0:T(8,128)S(1)}, f32[96,128]{1,0:T(8,128)S(1)}, u32[]{:S(2)}, u32[]{:S(2)}) collective-permute-start(f32[96,128]{1,0:T(8,128)S(1)} %get-tuple-element.21), channel_id=1, source_target_pairs={{0,31},{1,0},{2,1},{3,2},{4,3},{5,4},{6,5},{7,6},{8,7},{9,8},{10,9... | collective-permute-start | bytes 147464 | tf_op jit(solution)/shard_map/ppermute | solution.py:562
  32.0 2.1 %collective-permute-done.from_west = f32[96,128]{1,0:T(8,128)S(1)} collective-permute-done((f32[96,128]{1,0:T(8,128)S(1)}, f32[96,128]{1,0:T(8,128)S(1)}, u32[]{:S(2)}, u32[]{:S(2)}) %collective-permute-start) | collective-permute-done | bytes 49184 | tf_op jit(solution)/shard_map/ppermute | solution.py:561
  34.1 0.0 collective-permute-done.1.from_east
  34.1 0.1 rows.1
  34.3 0.1 collective-permute-start.2
  34.4 0.7 %collective-permute-start.3 = (f32[240,128]{1,0:T(8,128)S(1)}, f32[240,128]{1,0:T(8,128)S(1)}, u32[]{:S(2)}, u32[]{:S(2)}) collective-permute-start(f32[240,128]{1,0:T(8,128)S(1)} %get-tuple-element.23), channel_id=1, source_target_pairs={{0,32},{32,0},{64,96},{96,64},{128,160},{160,128},{192,224},{224,1... | collective-permute-start | bytes 368648 | tf_op jit(solution)/shard_map/ppermute | solution.py:575
  35.0 3.9 %collective-permute-done.2.from_outer = f32[240,128]{1,0:T(8,128)S(1)} collective-permute-done((f32[240,128]{1,0:T(8,128)S(1)}, f32[240,128]{1,0:T(8,128)S(1)}, u32[]{:S(2)}, u32[]{:S(2)}) %collective-permute-start.2) | collective-permute-done | bytes 122912 | tf_op jit(solution)/shard_map/ppermute | solution.py:574
  39.0 0.0 collective-permute-done.3.from_inner
  39.0 3.0 %first_half.1 = (f32[23,2,112,128]{3,2,1,0:T(8,128)S(1)}, f32[1,10,512,128]{3,2,1,0:T(8,128)}) custom-call(f32[12,64,128]{2,1,0:T(8,128)S(1)} %get-tuple-element.19.fields, f32[96,128]{1,0:T(8,128)S(1)} %collective-permute-done.from_west, f32[96,128]{1,0:T(8,128)S(1)} %collective-permute-done.1.from_east, f32[240,128]{1,0:T(8,128)S(1)} %collective-permute-done.2.from_outer, ...), custom_call_target="tpu_custom_call" | custom-call | flops 20000000 | bytes 2000000 | tf_op jit(solution)/shard_map/first_half/pallas_call | solution.py:579
  42.0 1.9 %second_half.1 = (f32[2,64,128]{2,1,0:T(8,128)S(1)}, f32[3,64,128]{2,1,0:T(8,128)S(1)}, f32[23,2,112,128]{3,2,1,0:T(8,128)S(1)}, f32[1,10,512,128]{3,2,1,0:T(8,128)}) custom-call(f32[23,2,112,128]{3,2,1,0:T(8,128)S(1)} %get-tuple-element.27.state, f32[1,10,512,128]{3,2,1,0:T(8,128)} %get-tuple-element.28.out_in, ...), custom_call_target="tpu_custom_call", output_to_operand_aliasing={{2}: (0, {}), {3}: (1, {})} | custom-call | flops 20000000 | bytes 2000000 | tf_op jit(solution)/shard_map/second_half/pallas_call | solution.py:600
  43.9 0.0 collective-permute-done.8.partner_far
  43.9 0.0 collective-permute-done.7.partner
  43.9 0.7 %last.1 = (f32[1,10,512,128]{3,2,1,0:T(8,128)}, f32[2,64,128]{2,1,0:T(8,128)}, f32[3,64,128]{2,1,0:T(8,128)}) custom-call(f32[1,10,512,128]{3,2,1,0:T(8,128)} %get-tuple-element.29.out_in, s32[8,128]{1,0:T(8,128)S(1)} %get-tuple-element.25.flag, f32[2,64,128]{2,1,0:T(8,128)S(1)} %get-tuple-element.30.vel, ...), custom_call_target="tpu_custom_call", output_to_operand_aliasing={{0}: (0, {})} | custom-call | tf_op jit(solution)/shard_map/last/pallas_call | solution.py:618
Async XLA Ops:
  2.4 7.4 %collective-permute-start.4 = (f32[10,64,128]{2,1,0:T(8,128)S(1)}, f32[10,64,128]{2,1,0:T(8,128)S(1)}, u32[]{:S(2)}, u32[]{:S(2)}) collective-permute-start(f32[10,64,128]{2,1,0:T(8,128)S(1)} %get-tuple-element.24.snap.own), channel_id=1, source_target_pairs={{0,64},{32,224},{64,128},{96,32},{128,192},{160,96},{192,0},{224,1... | collective-permute-start | bytes 983048 | tf_op jit(solution)/shard_map/ppermute | solution.py:560
  5.8 10.6 %collective-permute-start.5 = (f32[10,64,128]{2,1,0:T(8,128)S(1)}, f32[10,64,128]{2,1,0:T(8,128)S(1)}, u32[]{:S(2)}, u32[]{:S(2)}) collective-permute-start(f32[10,64,128]{2,1,0:T(8,128)S(1)} %get-tuple-element.24.snap.own), channel_id=1, source_target_pairs={{0,192},{32,96},{64,0},{96,160},{128,64},{160,224},{192,128},{224,... | collective-permute-start | bytes 983048 | tf_op jit(solution)/shard_map/ppermute | solution.py:563
  16.4 27.5 %collective-permute-start.7 = (f32[3,10,64,128]{3,2,1,0:T(8,128)S(1)}, f32[3,10,64,128]{3,2,1,0:T(8,128)S(1)}, u32[]{:S(2)}, u32[]{:S(2)}) collective-permute-start(f32[3,10,64,128]{3,2,1,0:T(8,128)S(1)} %join.1), channel_id=1, source_target_pairs={{0,32},{32,0},{64,96},{96,64},{128,160},{160,128},{192,224},{224,1... | collective-permute-start | bytes 2949128 | tf_op jit(solution)/shard_map/ppermute | solution.py:598
  17.2 6.2 %collective-permute-start.6 = (f32[10,64,128]{2,1,0:T(8,128)S(1)}, f32[10,64,128]{2,1,0:T(8,128)S(1)}, u32[]{:S(2)}, u32[]{:S(2)}) collective-permute-start(f32[10,64,128]{2,1,0:T(8,128)S(1)} %collective-permute-done.4.near), channel_id=1, source_target_pairs={{0,64},{32,224},{64,128},{96,32},{128,192},{160,96},{192,0},{224,1... | collective-permute-start | bytes 983048 | tf_op jit(solution)/shard_map/ppermute | solution.py:576
  23.5 20.4 %collective-permute-start.8 = (f32[10,64,128]{2,1,0:T(8,128)S(1)}, f32[10,64,128]{2,1,0:T(8,128)S(1)}, u32[]{:S(2)}, u32[]{:S(2)}) collective-permute-start(f32[10,64,128]{2,1,0:T(8,128)S(1)} %collective-permute-done.6.far), channel_id=1, source_target_pairs={{0,32},{32,0},{64,96},{96,64},{128,160},{160,128},{192,224},{224,1... | collective-permute-start | bytes 983048 | tf_op jit(solution)/shard_map/ppermute | solution.py:616
  25.6 8.5 %collective-permute-start = (f32[96,128]{1,0:T(8,128)S(1)}, f32[96,128]{1,0:T(8,128)S(1)}, u32[]{:S(2)}, u32[]{:S(2)}) collective-permute-start(f32[96,128]{1,0:T(8,128)S(1)} %get-tuple-element.20), channel_id=1, source_target_pairs={{0,1},{1,2},{2,3},{3,4},{4,5},{5,6},{6,7},{7,8},{8,9},{9,10},{10,1... | collective-permute-start | bytes 147464 | tf_op jit(solution)/shard_map/ppermute | solution.py:561
  25.6 8.5 %collective-permute-start.1 = (f32[96,128]{1,0:T(8,128)S(1)}, f32[96,128]{1,0:T(8,128)S(1)}, u32[]{:S(2)}, u32[]{:S(2)}) collective-permute-start(f32[96,128]{1,0:T(8,128)S(1)} %get-tuple-element.21), channel_id=1, source_target_pairs={{0,31},{1,0},{2,1},{3,2},{4,3},{5,4},{6,5},{7,6},{8,7},{9,8},{10,9... | collective-permute-start | bytes 147464 | tf_op jit(solution)/shard_map/ppermute | solution.py:562
  34.3 4.7 %collective-permute-start.2 = (f32[240,128]{1,0:T(8,128)S(1)}, f32[240,128]{1,0:T(8,128)S(1)}, u32[]{:S(2)}, u32[]{:S(2)}) collective-permute-start(f32[240,128]{1,0:T(8,128)S(1)} %get-tuple-element.22), channel_id=1, source_target_pairs={{224,255},{225,254},{226,253},{227,252},{228,251},{229,250},{230,2... | collective-permute-start | bytes 368648 | tf_op jit(solution)/shard_map/ppermute | solution.py:574
  34.4 4.6 %collective-permute-start.3 = (f32[240,128]{1,0:T(8,128)S(1)}, f32[240,128]{1,0:T(8,128)S(1)}, u32[]{:S(2)}, u32[]{:S(2)}) collective-permute-start(f32[240,128]{1,0:T(8,128)S(1)} %get-tuple-element.23), channel_id=1, source_target_pairs={{0,32},{32,0},{64,96},{96,64},{128,160},{160,128},{192,224},{224,1... | collective-permute-start | bytes 368648 | tf_op jit(solution)/shard_map/ppermute | solution.py:575

commit v8 on v7

--- a/solution.py
+++ b/solution.py
@@ -375,7 +375,7 @@
 
 def place_of(me, which):
     chip, core = me // 2, me % 2
-    step = 1 - 2 * core
+    step = 2 * core - 1
     if which >= 4:
         core = 1 - core
         which -= 4
@@ -546,8 +546,8 @@
             )
         )
     )
-    along = [(r, (r + 2 - 4 * (r % 2)) % 8) for r in range(8)]
-    against = [(r, (r - 2 + 4 * (r % 2)) % 8) for r in range(8)]
+    along = [(r, (r - 2 + 4 * (r % 2)) % 8) for r in range(8)]
+    against = [(r, (r + 2 - 4 * (r % 2)) % 8) for r in range(8)]
     partner = [(r, r ^ 1) for r in range(8)]
     eastward = [(c, (c + 1) % 32) for c in range(32)]
     westward = [(c, (c - 1) % 32) for c in range(32)]

time: 44.7 us -> 46 us (1.029)
  the two profiles are of different devices: /device:TPU:1 before, /device:TPU:7 now
where the time goes in v8:
time: 46 us; the launch traced here: 45.8 us
  waiting for transfers between devices  18.9 us (41%)
  starting transfers between devices  18.4 us (40%)
  Pallas kernels  7.79 us (17%)
  between operations  0.7 us (2%)
    ppermute x1, starting transfers between devices, step(): from_east = lax.ppermute(to_west, 'col', westward)  6.39 us
    ppermute x1, waiting for transfers between devices, step(): near = lax.ppermute(snap, 'row', along)  6.29 us
    ppermute x1, waiting for transfers between devices, step(): far = lax.ppermute(near, 'row', along)  5.73 us
    ppermute x1, starting transfers between devices, step(): from_outer = lax.ppermute(outer, ('row', 'col'), across)  4.59 us
    pallas_call x1, Pallas kernels, step(): pl.pallas_call(first_half_kernel, out_shape=(shape(HELD, 2, TALL, LANES),...  3.29 us
    ppermute x1, waiting for transfers between devices, step(): from_outer = lax.ppermute(outer, ('row', 'col'), across)  2.54 us
    ppermute x1, waiting for transfers between devices, step(): near_back = lax.ppermute(snap, 'row', against)  2.22 us
    ppermute x1, starting transfers between devices, step(): partner_far = lax.ppermute(far, 'row', partner)  2.16 us
  transfers between devices with their start and end apart: 9, of which 5 were waited for; matrix products, arithmetic and copies ran while one was open for 0% of the time, Pallas kernels for 11%

profile of v8, /device:TPU:7, one launch (start us, length us, event | category | flops | bytes accessed | tf_op | source)
XLA Modules:
  0.0 45.8 jit_solution(17221915927664508472)
XLA Ops:
  0.6 1.7 %prepare.1 = (f32[12,64,128]{2,1,0:T(8,128)S(1)}, f32[96,128]{1,0:T(8,128)S(1)}, f32[96,128]{1,0:T(8,128)S(1)}, f32[10,64,128]{2,1,0:T(8,128)S(1)}, s32[8,128]{1,0:T(8,128)S(1)}, /*index=5*/f32[10,64,128]{2,1,0:T(8,128)S(1)}) custom-call(f32[2,64,128]{2,1,0:T(8,128)} %vel_hbm.1, f32[3,64,128]{2,1,0:T(8,128)} %stress_hbm.1, f32[2,64,128]{2,1,0:T(8,128)} %wind_hbm.1, ...), custom_call_target="tpu_custom_call" | custom-call | tf_op jit(solution)/shard_map/prepare/pallas_call | solution.py:505
  2.4 0.1 collective-permute-start.4
  2.5 1.5 %collective-permute-start.5 = (f32[10,64,128]{2,1,0:T(8,128)S(1)}, f32[10,64,128]{2,1,0:T(8,128)S(1)}, u32[]{:S(2)}, u32[]{:S(2)}) collective-permute-start(f32[10,64,128]{2,1,0:T(8,128)S(1)} %get-tuple-element.24.snap.own), channel_id=1, source_target_pairs={{0,64},{32,224},{64,128},{96,32},{128,192},{160,96},{192,0},{224,1... | collective-permute-start | bytes 983048 | tf_op jit(solution)/shard_map/ppermute | solution.py:563
  3.9 6.3 %collective-permute-done.4.near = f32[10,64,128]{2,1,0:T(8,128)S(1)} collective-permute-done((f32[10,64,128]{2,1,0:T(8,128)S(1)}, f32[10,64,128]{2,1,0:T(8,128)S(1)}, u32[]{:S(2)}, u32[]{:S(2)}) %collective-permute-start.4) | collective-permute-done | bytes 327712 | tf_op jit(solution)/shard_map/ppermute | solution.py:560
  10.2 2.2 %collective-permute-done.5.near_back = f32[10,64,128]{2,1,0:T(8,128)S(1)} collective-permute-done((f32[10,64,128]{2,1,0:T(8,128)S(1)}, f32[10,64,128]{2,1,0:T(8,128)S(1)}, u32[]{:S(2)}, u32[]{:S(2)}) %collective-permute-start.5) | collective-permute-done | bytes 327712 | tf_op jit(solution)/shard_map/ppermute | solution.py:563
  12.4 0.1 join.1
  12.5 1.5 %collective-permute-start.7 = (f32[3,10,64,128]{3,2,1,0:T(8,128)S(1)}, f32[3,10,64,128]{3,2,1,0:T(8,128)S(1)}, u32[]{:S(2)}, u32[]{:S(2)}) collective-permute-start(f32[3,10,64,128]{3,2,1,0:T(8,128)S(1)} %join.1), channel_id=1, source_target_pairs={{0,32},{32,0},{64,96},{96,64},{128,160},{160,128},{192,224},{224,1... | collective-permute-start | bytes 2949128 | tf_op jit(solution)/shard_map/ppermute | solution.py:598
  14.0 0.5 %collective-permute-start.6 = (f32[10,64,128]{2,1,0:T(8,128)S(1)}, f32[10,64,128]{2,1,0:T(8,128)S(1)}, u32[]{:S(2)}, u32[]{:S(2)}) collective-permute-start(f32[10,64,128]{2,1,0:T(8,128)S(1)} %collective-permute-done.4.near), channel_id=1, source_target_pairs={{0,192},{32,96},{64,0},{96,160},{128,64},{160,224},{192,128},{224,... | collective-permute-start | bytes 983048 | tf_op jit(solution)/shard_map/ppermute | solution.py:576
  14.5 5.7 %collective-permute-done.6.far = f32[10,64,128]{2,1,0:T(8,128)S(1)} collective-permute-done((f32[10,64,128]{2,1,0:T(8,128)S(1)}, f32[10,64,128]{2,1,0:T(8,128)S(1)}, u32[]{:S(2)}, u32[]{:S(2)}) %collective-permute-start.6) | collective-permute-done | bytes 327712 | tf_op jit(solution)/shard_map/ppermute | solution.py:576
  20.3 2.2 %collective-permute-start.8 = (f32[10,64,128]{2,1,0:T(8,128)S(1)}, f32[10,64,128]{2,1,0:T(8,128)S(1)}, u32[]{:S(2)}, u32[]{:S(2)}) collective-permute-start(f32[10,64,128]{2,1,0:T(8,128)S(1)} %collective-permute-done.6.far), channel_id=1, source_target_pairs={{0,32},{32,0},{64,96},{96,64},{128,160},{160,128},{192,224},{224,1... | collective-permute-start | bytes 983048 | tf_op jit(solution)/shard_map/ppermute | solution.py:616
  22.4 1.7 %collective-permute-start = (f32[96,128]{1,0:T(8,128)S(1)}, f32[96,128]{1,0:T(8,128)S(1)}, u32[]{:S(2)}, u32[]{:S(2)}) collective-permute-start(f32[96,128]{1,0:T(8,128)S(1)} %get-tuple-element.20), channel_id=1, source_target_pairs={{0,1},{1,2},{2,3},{3,4},{4,5},{5,6},{6,7},{7,8},{8,9},{9,10},{10,1... | collective-permute-start | bytes 147464 | tf_op jit(solution)/shard_map/ppermute | solution.py:561
  24.2 6.4 %collective-permute-start.1 = (f32[96,128]{1,0:T(8,128)S(1)}, f32[96,128]{1,0:T(8,128)S(1)}, u32[]{:S(2)}, u32[]{:S(2)}) collective-permute-start(f32[96,128]{1,0:T(8,128)S(1)} %get-tuple-element.21), channel_id=1, source_target_pairs={{0,31},{1,0},{2,1},{3,2},{4,3},{5,4},{6,5},{7,6},{8,7},{9,8},{10,9... | collective-permute-start | bytes 147464 | tf_op jit(solution)/shard_map/ppermute | solution.py:562
  30.6 2.1 %collective-permute-done.from_west = f32[96,128]{1,0:T(8,128)S(1)} collective-permute-done((f32[96,128]{1,0:T(8,128)S(1)}, f32[96,128]{1,0:T(8,128)S(1)}, u32[]{:S(2)}, u32[]{:S(2)}) %collective-permute-start) | collective-permute-done | bytes 49184 | tf_op jit(solution)/shard_map/ppermute | solution.py:561
  32.7 0.0 collective-permute-done.1.from_east
  32.7 0.1 rows.1
  32.8 4.6 %collective-permute-start.2 = (f32[240,128]{1,0:T(8,128)S(1)}, f32[240,128]{1,0:T(8,128)S(1)}, u32[]{:S(2)}, u32[]{:S(2)}) collective-permute-start(f32[240,128]{1,0:T(8,128)S(1)} %get-tuple-element.22), channel_id=1, source_target_pairs={{224,255},{225,254},{226,253},{227,252},{228,251},{229,250},{230,2... | collective-permute-start | bytes 368648 | tf_op jit(solution)/shard_map/ppermute | solution.py:574
  37.4 0.0 collective-permute-start.3
  37.4 2.5 %collective-permute-done.2.from_outer = f32[240,128]{1,0:T(8,128)S(1)} collective-permute-done((f32[240,128]{1,0:T(8,128)S(1)}, f32[240,128]{1,0:T(8,128)S(1)}, u32[]{:S(2)}, u32[]{:S(2)}) %collective-permute-start.2) | collective-permute-done | bytes 122912 | tf_op jit(solution)/shard_map/ppermute | solution.py:574
  39.9 0.0 collective-permute-done.3.from_inner
  39.9 3.3 %first_half.1 = (f32[23,2,112,128]{3,2,1,0:T(8,128)S(1)}, f32[1,10,512,128]{3,2,1,0:T(8,128)}) custom-call(f32[12,64,128]{2,1,0:T(8,128)S(1)} %get-tuple-element.19.fields, f32[96,128]{1,0:T(8,128)S(1)} %collective-permute-done.from_west, f32[96,128]{1,0:T(8,128)S(1)} %collective-permute-done.1.from_east, f32[240,128]{1,0:T(8,128)S(1)} %collective-permute-done.2.from_outer, ...), custom_call_target="tpu_custom_call" | custom-call | flops 20000000 | bytes 2000000 | tf_op jit(solution)/shard_map/first_half/pallas_call | solution.py:579
  43.2 1.9 %second_half.1 = (f32[2,64,128]{2,1,0:T(8,128)S(1)}, f32[3,64,128]{2,1,0:T(8,128)S(1)}, f32[23,2,112,128]{3,2,1,0:T(8,128)S(1)}, f32[1,10,512,128]{3,2,1,0:T(8,128)}) custom-call(f32[23,2,112,128]{3,2,1,0:T(8,128)S(1)} %get-tuple-element.27.state, f32[1,10,512,128]{3,2,1,0:T(8,128)} %get-tuple-element.28.out_in, ...), custom_call_target="tpu_custom_call", output_to_operand_aliasing={{2}: (0, {}), {3}: (1, {})} | custom-call | flops 20000000 | bytes 2000000 | tf_op jit(solution)/shard_map/second_half/pallas_call | solution.py:600
  45.1 0.0 collective-permute-done.8.partner_far
  45.1 0.0 collective-permute-done.7.partner
  45.1 0.7 %last.1 = (f32[1,10,512,128]{3,2,1,0:T(8,128)}, f32[2,64,128]{2,1,0:T(8,128)}, f32[3,64,128]{2,1,0:T(8,128)}) custom-call(f32[1,10,512,128]{3,2,1,0:T(8,128)} %get-tuple-element.29.out_in, s32[8,128]{1,0:T(8,128)S(1)} %get-tuple-element.25.flag, f32[2,64,128]{2,1,0:T(8,128)S(1)} %get-tuple-element.30.vel, ...), custom_call_target="tpu_custom_call", output_to_operand_aliasing={{0}: (0, {})} | custom-call | tf_op jit(solution)/shard_map/last/pallas_call | solution.py:618
Async XLA Ops:
  2.4 7.8 %collective-permute-start.4 = (f32[10,64,128]{2,1,0:T(8,128)S(1)}, f32[10,64,128]{2,1,0:T(8,128)S(1)}, u32[]{:S(2)}, u32[]{:S(2)}) collective-permute-start(f32[10,64,128]{2,1,0:T(8,128)S(1)} %get-tuple-element.24.snap.own), channel_id=1, source_target_pairs={{0,192},{32,96},{64,0},{96,160},{128,64},{160,224},{192,128},{224,... | collective-permute-start | bytes 983048 | tf_op jit(solution)/shard_map/ppermute | solution.py:560
  2.5 10.0 %collective-permute-start.5 = (f32[10,64,128]{2,1,0:T(8,128)S(1)}, f32[10,64,128]{2,1,0:T(8,128)S(1)}, u32[]{:S(2)}, u32[]{:S(2)}) collective-permute-start(f32[10,64,128]{2,1,0:T(8,128)S(1)} %get-tuple-element.24.snap.own), channel_id=1, source_target_pairs={{0,64},{32,224},{64,128},{96,32},{128,192},{160,96},{192,0},{224,1... | collective-permute-start | bytes 983048 | tf_op jit(solution)/shard_map/ppermute | solution.py:563
  12.5 32.6 %collective-permute-start.7 = (f32[3,10,64,128]{3,2,1,0:T(8,128)S(1)}, f32[3,10,64,128]{3,2,1,0:T(8,128)S(1)}, u32[]{:S(2)}, u32[]{:S(2)}) collective-permute-start(f32[3,10,64,128]{3,2,1,0:T(8,128)S(1)} %join.1), channel_id=1, source_target_pairs={{0,32},{32,0},{64,96},{96,64},{128,160},{160,128},{192,224},{224,1... | collective-permute-start | bytes 2949128 | tf_op jit(solution)/shard_map/ppermute | solution.py:598
  14.0 6.2 %collective-permute-start.6 = (f32[10,64,128]{2,1,0:T(8,128)S(1)}, f32[10,64,128]{2,1,0:T(8,128)S(1)}, u32[]{:S(2)}, u32[]{:S(2)}) collective-permute-start(f32[10,64,128]{2,1,0:T(8,128)S(1)} %collective-permute-done.4.near), channel_id=1, source_target_pairs={{0,192},{32,96},{64,0},{96,160},{128,64},{160,224},{192,128},{224,... | collective-permute-start | bytes 983048 | tf_op jit(solution)/shard_map/ppermute | solution.py:576
  20.3 24.8 %collective-permute-start.8 = (f32[10,64,128]{2,1,0:T(8,128)S(1)}, f32[10,64,128]{2,1,0:T(8,128)S(1)}, u32[]{:S(2)}, u32[]{:S(2)}) collective-permute-start(f32[10,64,128]{2,1,0:T(8,128)S(1)} %collective-permute-done.6.far), channel_id=1, source_target_pairs={{0,32},{32,0},{64,96},{96,64},{128,160},{160,128},{192,224},{224,1... | collective-permute-start | bytes 983048 | tf_op jit(solution)/shard_map/ppermute | solution.py:616
  22.4 10.2 %collective-permute-start = (f32[96,128]{1,0:T(8,128)S(1)}, f32[96,128]{1,0:T(8,128)S(1)}, u32[]{:S(2)}, u32[]{:S(2)}) collective-permute-start(f32[96,128]{1,0:T(8,128)S(1)} %get-tuple-element.20), channel_id=1, source_target_pairs={{0,1},{1,2},{2,3},{3,4},{4,5},{5,6},{6,7},{7,8},{8,9},{9,10},{10,1... | collective-permute-start | bytes 147464 | tf_op jit(solution)/shard_map/ppermute | solution.py:561
  24.2 8.5 %collective-permute-start.1 = (f32[96,128]{1,0:T(8,128)S(1)}, f32[96,128]{1,0:T(8,128)S(1)}, u32[]{:S(2)}, u32[]{:S(2)}) collective-permute-start(f32[96,128]{1,0:T(8,128)S(1)} %get-tuple-element.21), channel_id=1, source_target_pairs={{0,31},{1,0},{2,1},{3,2},{4,3},{5,4},{6,5},{7,6},{8,7},{9,8},{10,9... | collective-permute-start | bytes 147464 | tf_op jit(solution)/shard_map/ppermute | solution.py:562
  32.8 7.1 %collective-permute-start.2 = (f32[240,128]{1,0:T(8,128)S(1)}, f32[240,128]{1,0:T(8,128)S(1)}, u32[]{:S(2)}, u32[]{:S(2)}) collective-permute-start(f32[240,128]{1,0:T(8,128)S(1)} %get-tuple-element.22), channel_id=1, source_target_pairs={{224,255},{225,254},{226,253},{227,252},{228,251},{229,250},{230,2... | collective-permute-start | bytes 368648 | tf_op jit(solution)/shard_map/ppermute | solution.py:574
  37.4 2.6 %collective-permute-start.3 = (f32[240,128]{1,0:T(8,128)S(1)}, f32[240,128]{1,0:T(8,128)S(1)}, u32[]{:S(2)}, u32[]{:S(2)}) collective-permute-start(f32[240,128]{1,0:T(8,128)S(1)} %get-tuple-element.23), channel_id=1, source_target_pairs={{0,32},{32,0},{64,96},{96,64},{128,160},{160,128},{192,224},{224,1... | collective-permute-start | bytes 368648 | tf_op jit(solution)/shard_map/ppermute | solution.py:575

commit v9 on v8

--- a/solution.py
+++ b/solution.py
@@ -189,7 +189,40 @@
     return lane == 0, lane == LANES - 1, row, top_rows
 
 
-def assemble(fields, from_west, from_east, from_outer, from_inner, held):
+def own_kernel(fields, from_west, from_east, held):
+    lane = lane_index()
+    for f in range(SENT):
+        a, b = from_west[8 * f : 8 * f + 8], from_east[8 * f : 8 * f + 8]
+        for g in range(8):
+            at = PAD + HALO + 8 * g
+            held[f, 0, at : at + 8] = fields[f, 8 * g : 8 * g + 8]
+            held[f, 1, at : at + 8] = jnp.where(lane < 64, turned(b, -16 * g), turned(a, 112 - 16 * g))
+    for g in range(2, 10):
+        derive(held, g, lane == 0)
+        same_sizes(held, g)
+
+
+def same_sizes(held, g):
+    rows = slice(PAD + 8 * g, PAD + 8 * g + 8)
+    for t in range(2):
+        held[HWV, t, rows] = held[HW, t, rows]
+        held[HHV, t, rows] = held[HH, t, rows]
+
+
+def derive(held, g, first):
+    at = PAD + 8 * g
+    rows = slice(at, at + 8)
+    for t in range(2):
+        scale = held[AA, t, rows]
+        inertia = held[INE, t, rows]
+        held[AA, t, rows] = (inertia + 1.0) * scale
+        held[BB, t, rows] = (inertia * (1.0 / 32.0)) * scale
+    velocity_sums(
+        held, at, held[U, 0, rows], held[U, 1, rows], held[V, 0, rows], held[V, 1, rows], first
+    )
+
+
+def assemble(from_outer, from_inner, held):
     is_top = lax.axis_index("row") == 7
     odd = lax.axis_index("row") % 2 + jnp.zeros((8, LANES), jnp.int32) == 1
     lane = lane_index()
@@ -211,11 +244,6 @@
         return jnp.where(low, turned(corner, -(base + 32 + 16 * a)), turned(corner, 112 - base - 16 * a))
 
     for f in range(SENT):
-        a, b = from_west[8 * f : 8 * f + 8], from_east[8 * f : 8 * f + 8]
-        for g in range(8):
-            at = PAD + HALO + 8 * g
-            held[f, 0, at : at + 8] = fields[f, 8 * g : 8 * g + 8]
-            held[f, 1, at : at + 8] = jnp.where(low, turned(b, -16 * g), turned(a, 112 - 16 * g))
         for g in range(2):
             at = PAD + 8 * g
             held[f, 0, at : at + 8] = south(HALO * f + 8 * g)
@@ -255,31 +283,16 @@
                     held[own, 0, TOP + 8 * g : TOP + 8 * g + 8] = main
                     held[own, 1, TOP + 8 * g : TOP + 8 * g + 8] = side
 
-    for g in range(12):
-        at = PAD + 8 * g
-        for t in range(2):
-            scale = held[AA, t, at : at + 8]
-            inertia = held[INE, t, at : at + 8]
-            held[AA, t, at : at + 8] = (inertia + 1.0) * scale
-            held[BB, t, at : at + 8] = (inertia * (1.0 / 32.0)) * scale
-            if g < 10:
-                held[HWV, t, at : at + 8] = held[HW, t, at : at + 8]
-                held[HHV, t, at : at + 8] = held[HH, t, at : at + 8]
-        velocity_sums(
-            held,
-            at,
-            held[U, 0, at : at + 8],
-            held[U, 1, at : at + 8],
-            held[V, 0, at : at + 8],
-            held[V, 1, at : at + 8],
-            first,
-        )
+    for g in (0, 1):
+        derive(held, g, first)
+        same_sizes(held, g)
+    for g in (10, 11):
+        derive(held, g, first)
 
     @pl.when(jnp.logical_not(is_top))
     def _():
-        for t in range(2):
-            held[HWV, t, TOP : TOP + HALO] = held[HW, t, TOP : TOP + HALO]
-            held[HHV, t, TOP : TOP + HALO] = held[HH, t, TOP : TOP + HALO]
+        for g in (10, 11):
+            same_sizes(held, g)
 
 
 def velocity_sums(held, at, um, us, vm, vs, first):
@@ -389,7 +402,7 @@
 
 
 def first_half_kernel(
-    fields, from_west, from_east, from_outer, from_inner, snap, flag, zero, held, out, sems
+    state, from_outer, from_inner, snap, flag, zero, held, out, sems
 ):
     me = lax.axis_index("row")
     mine = jnp.max(flag[...]) == 1
@@ -405,7 +418,7 @@
         for copy in zeros:
             copy.start()
 
-    assemble(fields, from_west, from_east, from_outer, from_inner, held)
+    assemble(from_outer, from_inner, held)
     subcycles(held, 0, 5, 0, 12)
     subcycles(held, 5, SPLIT, 1, 11)
 
@@ -446,13 +459,11 @@
             copy.wait()
 
 
-def last_kernel(
-    out_in, flag, vel, stress, far, partner, partner_far, out, vel_out, stress_out, sems
-):
+def late_kernel(out_in, flag, vel, stress, far, partner, out, vel_out, stress_out, sems):
     me = lax.axis_index("row")
     fields_out = [
-        pltpu.make_async_copy(vel, vel_out, sems.at[5]),
-        pltpu.make_async_copy(stress, stress_out, sems.at[6]),
+        pltpu.make_async_copy(vel, vel_out, sems.at[4]),
+        pltpu.make_async_copy(stress, stress_out, sems.at[5]),
     ]
     for copy in fields_out:
         copy.start()
@@ -461,14 +472,23 @@
     @pl.when(mine)
     def _():
         copies = [into(out, partner.at[n], place_of(me, 4 + n), sems.at[n]) for n in range(3)]
-        copies.append(into(out, partner_far, place_of(me, 7), sems.at[3]))
-        copies.append(into(out, far, place_of(me, 3), sems.at[4]))
+        copies.append(into(out, far, place_of(me, 3), sems.at[3]))
         for copy in copies:
             copy.start()
         for copy in copies:
             copy.wait()
 
     for copy in fields_out:
+        copy.wait()
+
+
+def last_kernel(out_in, flag, partner_far, out, sem):
+    mine = jnp.max(flag[...]) == 1
+
+    @pl.when(mine)
+    def _():
+        copy = into(out, partner_far, place_of(lax.axis_index("row"), 7), sem)
+        copy.start()
         copy.wait()
 
 
@@ -576,16 +596,26 @@
     far = lax.ppermute(near, "row", along)
 
     hbm = lambda: pl.BlockSpec(memory_space=pl.ANY)
+    state = pl.pallas_call(
+        own_kernel,
+        out_shape=shape(HELD, 2, TALL, LANES),
+        in_specs=[vmem()] * 3,
+        out_specs=vmem(),
+        compiler_params=grant(8),
+        cost_estimate=pl.CostEstimate(flops=1000000, bytes_accessed=1000000, transcendentals=0),
+        name="own",
+    )(fields, from_west, from_east)
     state, restart = pl.pallas_call(
         first_half_kernel,
         out_shape=(shape(HELD, 2, TALL, LANES), shape(1, 10, 8 * ROWS, LANES)),
-        in_specs=[vmem()] * 5 + [hbm(), vmem(), hbm()],
+        in_specs=[vmem()] * 3 + [hbm(), vmem(), hbm()],
         out_specs=(vmem(), hbm()),
+        input_output_aliases={0: 0},
         scratch_shapes=[pltpu.SemaphoreType.DMA((8,))],
         compiler_params=grant(16),
         cost_estimate=pl.CostEstimate(flops=20000000, bytes_accessed=2000000, transcendentals=0),
         name="first_half",
-    )(fields, from_west, from_east, from_outer, from_inner, snap, flag, blank)
+    )(state, from_outer, from_inner, snap, flag, blank)
 
     joined = pl.pallas_call(
         join_kernel,
@@ -616,19 +646,30 @@
     partner_far = lax.ppermute(far, "row", partner)
 
     restart, velocity, stress = pl.pallas_call(
-        last_kernel,
+        late_kernel,
         out_shape=(
             shape(1, 10, 8 * ROWS, LANES),
             shape(2, ROWS, LANES),
             shape(3, ROWS, LANES),
         ),
-        in_specs=[hbm(), vmem()] + [hbm()] * 5,
+        in_specs=[hbm(), vmem()] + [hbm()] * 4,
         out_specs=(hbm(), hbm(), hbm()),
         input_output_aliases={0: 0},
-        scratch_shapes=[pltpu.SemaphoreType.DMA((7,))],
+        scratch_shapes=[pltpu.SemaphoreType.DMA((6,))],
+        compiler_params=grant(4),
+        cost_estimate=pl.CostEstimate(flops=1000000, bytes_accessed=1000000, transcendentals=0),
+        name="late",
+    )(restart, flag, velocity, stress, far, partner_blocks)
+    restart = pl.pallas_call(
+        last_kernel,
+        out_shape=shape(1, 10, 8 * ROWS, LANES),
+        in_specs=[hbm(), vmem(), hbm()],
+        out_specs=hbm(),
+        input_output_aliases={0: 0},
+        scratch_shapes=[pltpu.SemaphoreType.DMA],
         compiler_params=grant(4),
         name="last",
-    )(restart, flag, velocity, stress, far, partner_blocks, partner_far)
+    )(restart, flag, partner_far)
     return (velocity, stress, restart)
 
 

time: 46 us -> 46 us (level)
    pallas_call x1 -> x3, Pallas kernels: 0.73 us -> 1.23 us  [the longest x1 0.72 us: step(): pl.pallas_call(late_kernel, out_shape=(shape(1, 10, 8 * ROWS, LANES), sha...]
  transfers between devices with their start and end apart: 9 -> 9, of which waited for: 5 -> 5; matrix products, arithmetic and copies ran while one was open for 0% -> 0% of each run, Pallas kernels for 11% -> 13%
where the time goes in v9:
time: 46 us; the launch traced here: 45.9 us
  waiting for transfers between devices  18.6 us (40%)
  starting transfers between devices  18.4 us (40%)
  Pallas kernels  8.13 us (18%)
  between operations  0.71 us (2%)
    ppermute x1, starting transfers between devices, step(): from_east = lax.ppermute(to_west, 'col', westward)  6.39 us
    ppermute x1, waiting for transfers between devices, step(): near = lax.ppermute(snap, 'row', along)  6.29 us
    ppermute x1, waiting for transfers between devices, step(): far = lax.ppermute(near, 'row', along)  5.73 us
    ppermute x1, starting transfers between devices, step(): from_outer = lax.ppermute(outer, ('row', 'col'), across)  4.59 us
    pallas_call x1, Pallas kernels, step(): pl.pallas_call(first_half_kernel, out_shape=(shape(HELD, 2, TALL, LANES),...  3.12 us
    ppermute x1, waiting for transfers between devices, step(): from_outer = lax.ppermute(outer, ('row', 'col'), across)  2.27 us
    ppermute x1, waiting for transfers between devices, step(): near_back = lax.ppermute(snap, 'row', against)  2.22 us
    ppermute x1, starting transfers between devices, step(): partner_far = lax.ppermute(far, 'row', partner)  2.16 us
  transfers between devices with their start and end apart: 9, of which 5 were waited for; matrix products, arithmetic and copies ran while one was open for 0% of the time, Pallas kernels for 13%

profile of v9, /device:TPU:7, one launch (start us, length us, event | category | flops | bytes accessed | tf_op | source)
XLA Modules:
  0.0 45.9 jit_solution(6896847096363133066)
XLA Ops:
  0.6 1.7 %prepare.1 = (f32[12,64,128]{2,1,0:T(8,128)S(1)}, f32[96,128]{1,0:T(8,128)S(1)}, f32[96,128]{1,0:T(8,128)S(1)}, f32[10,64,128]{2,1,0:T(8,128)S(1)}, s32[8,128]{1,0:T(8,128)S(1)}, /*index=5*/f32[10,64,128]{2,1,0:T(8,128)S(1)}) custom-call(f32[2,64,128]{2,1,0:T(8,128)} %vel_hbm.1, f32[3,64,128]{2,1,0:T(8,128)} %stress_hbm.1, f32[2,64,128]{2,1,0:T(8,128)} %wind_hbm.1, ...), custom_call_target="tpu_custom_call" | custom-call | tf_op jit(solution)/shard_map/prepare/pallas_call | solution.py:525
  2.4 0.1 collective-permute-start.4
  2.5 1.5 %collective-permute-start.5 = (f32[10,64,128]{2,1,0:T(8,128)S(1)}, f32[10,64,128]{2,1,0:T(8,128)S(1)}, u32[]{:S(2)}, u32[]{:S(2)}) collective-permute-start(f32[10,64,128]{2,1,0:T(8,128)S(1)} %get-tuple-element.24.snap.own), channel_id=1, source_target_pairs={{0,64},{32,224},{64,128},{96,32},{128,192},{160,96},{192,0},{224,1... | collective-permute-start | bytes 983048 | tf_op jit(solution)/shard_map/ppermute | solution.py:583
  3.9 6.3 %collective-permute-done.4.near = f32[10,64,128]{2,1,0:T(8,128)S(1)} collective-permute-done((f32[10,64,128]{2,1,0:T(8,128)S(1)}, f32[10,64,128]{2,1,0:T(8,128)S(1)}, u32[]{:S(2)}, u32[]{:S(2)}) %collective-permute-start.4) | collective-permute-done | bytes 327712 | tf_op jit(solution)/shard_map/ppermute | solution.py:580
  10.2 2.2 %collective-permute-done.5.near_back = f32[10,64,128]{2,1,0:T(8,128)S(1)} collective-permute-done((f32[10,64,128]{2,1,0:T(8,128)S(1)}, f32[10,64,128]{2,1,0:T(8,128)S(1)}, u32[]{:S(2)}, u32[]{:S(2)}) %collective-permute-start.5) | collective-permute-done | bytes 327712 | tf_op jit(solution)/shard_map/ppermute | solution.py:583
  12.4 0.1 join.1
  12.5 1.5 %collective-permute-start.7 = (f32[3,10,64,128]{3,2,1,0:T(8,128)S(1)}, f32[3,10,64,128]{3,2,1,0:T(8,128)S(1)}, u32[]{:S(2)}, u32[]{:S(2)}) collective-permute-start(f32[3,10,64,128]{3,2,1,0:T(8,128)S(1)} %join.1), channel_id=1, source_target_pairs={{0,32},{32,0},{64,96},{96,64},{128,160},{160,128},{192,224},{224,1... | collective-permute-start | bytes 2949128 | tf_op jit(solution)/shard_map/ppermute | solution.py:628
  14.0 0.5 %collective-permute-start.6 = (f32[10,64,128]{2,1,0:T(8,128)S(1)}, f32[10,64,128]{2,1,0:T(8,128)S(1)}, u32[]{:S(2)}, u32[]{:S(2)}) collective-permute-start(f32[10,64,128]{2,1,0:T(8,128)S(1)} %collective-permute-done.4.near), channel_id=1, source_target_pairs={{0,192},{32,96},{64,0},{96,160},{128,64},{160,224},{192,128},{224,... | collective-permute-start | bytes 983048 | tf_op jit(solution)/shard_map/ppermute | solution.py:596
  14.5 5.7 %collective-permute-done.6.far = f32[10,64,128]{2,1,0:T(8,128)S(1)} collective-permute-done((f32[10,64,128]{2,1,0:T(8,128)S(1)}, f32[10,64,128]{2,1,0:T(8,128)S(1)}, u32[]{:S(2)}, u32[]{:S(2)}) %collective-permute-start.6) | collective-permute-done | bytes 327712 | tf_op jit(solution)/shard_map/ppermute | solution.py:596
  20.3 2.2 %collective-permute-start.8 = (f32[10,64,128]{2,1,0:T(8,128)S(1)}, f32[10,64,128]{2,1,0:T(8,128)S(1)}, u32[]{:S(2)}, u32[]{:S(2)}) collective-permute-start(f32[10,64,128]{2,1,0:T(8,128)S(1)} %collective-permute-done.6.far), channel_id=1, source_target_pairs={{0,32},{32,0},{64,96},{96,64},{128,160},{160,128},{192,224},{224,1... | collective-permute-start | bytes 983048 | tf_op jit(solution)/shard_map/ppermute | solution.py:646
  22.4 1.7 %collective-permute-start = (f32[96,128]{1,0:T(8,128)S(1)}, f32[96,128]{1,0:T(8,128)S(1)}, u32[]{:S(2)}, u32[]{:S(2)}) collective-permute-start(f32[96,128]{1,0:T(8,128)S(1)} %get-tuple-element.20), channel_id=1, source_target_pairs={{0,1},{1,2},{2,3},{3,4},{4,5},{5,6},{6,7},{7,8},{8,9},{9,10},{10,1... | collective-permute-start | bytes 147464 | tf_op jit(solution)/shard_map/ppermute | solution.py:581
  24.2 6.4 %collective-permute-start.1 = (f32[96,128]{1,0:T(8,128)S(1)}, f32[96,128]{1,0:T(8,128)S(1)}, u32[]{:S(2)}, u32[]{:S(2)}) collective-permute-start(f32[96,128]{1,0:T(8,128)S(1)} %get-tuple-element.21), channel_id=1, source_target_pairs={{0,31},{1,0},{2,1},{3,2},{4,3},{5,4},{6,5},{7,6},{8,7},{9,8},{10,9... | collective-permute-start | bytes 147464 | tf_op jit(solution)/shard_map/ppermute | solution.py:582
  30.6 2.1 %collective-permute-done.from_west = f32[96,128]{1,0:T(8,128)S(1)} collective-permute-done((f32[96,128]{1,0:T(8,128)S(1)}, f32[96,128]{1,0:T(8,128)S(1)}, u32[]{:S(2)}, u32[]{:S(2)}) %collective-permute-start) | collective-permute-done | bytes 49184 | tf_op jit(solution)/shard_map/ppermute | solution.py:581
  32.7 0.0 collective-permute-done.1.from_east
  32.7 0.1 rows.1
  32.8 4.6 %collective-permute-start.2 = (f32[240,128]{1,0:T(8,128)S(1)}, f32[240,128]{1,0:T(8,128)S(1)}, u32[]{:S(2)}, u32[]{:S(2)}) collective-permute-start(f32[240,128]{1,0:T(8,128)S(1)} %get-tuple-element.22), channel_id=1, source_target_pairs={{224,255},{225,254},{226,253},{227,252},{228,251},{229,250},{230,2... | collective-permute-start | bytes 368648 | tf_op jit(solution)/shard_map/ppermute | solution.py:594
  37.4 0.0 collective-permute-start.3
  37.4 0.3 own.1.state
  37.7 2.3 %collective-permute-done.2.from_outer = f32[240,128]{1,0:T(8,128)S(1)} collective-permute-done((f32[240,128]{1,0:T(8,128)S(1)}, f32[240,128]{1,0:T(8,128)S(1)}, u32[]{:S(2)}, u32[]{:S(2)}) %collective-permute-start.2) | collective-permute-done | bytes 122912 | tf_op jit(solution)/shard_map/ppermute | solution.py:594
  39.9 0.0 collective-permute-done.3.from_inner
  39.9 3.1 %first_half.1 = (f32[23,2,112,128]{3,2,1,0:T(8,128)S(1)}, f32[1,10,512,128]{3,2,1,0:T(8,128)}) custom-call(f32[23,2,112,128]{3,2,1,0:T(8,128)S(1)} %own.1.state, f32[240,128]{1,0:T(8,128)S(1)} %collective-permute-done.2.from_outer, f32[240,128]{1,0:T(8,128)S(1)} %collective-permute-done.3.from_inner, ...), custom_call_target="tpu_custom_call", output_to_operand_aliasing={{0}: (0, {})} | custom-call | flops 20000000 | bytes 2000000 | tf_op jit(solution)/shard_map/first_half/pallas_call | solution.py:608
  43.1 1.9 %second_half.1 = (f32[2,64,128]{2,1,0:T(8,128)S(1)}, f32[3,64,128]{2,1,0:T(8,128)S(1)}, f32[23,2,112,128]{3,2,1,0:T(8,128)S(1)}, f32[1,10,512,128]{3,2,1,0:T(8,128)}) custom-call(f32[23,2,112,128]{3,2,1,0:T(8,128)S(1)} %get-tuple-element.27.state, f32[1,10,512,128]{3,2,1,0:T(8,128)} %get-tuple-element.28.out_in, ...), custom_call_target="tpu_custom_call", output_to_operand_aliasing={{2}: (0, {}), {3}: (1, {})} | custom-call | flops 20000000 | bytes 2000000 | tf_op jit(solution)/shard_map/second_half/pallas_call | solution.py:630
  44.9 0.0 collective-permute-done.7.partner
  44.9 0.7 %late.1 = (f32[1,10,512,128]{3,2,1,0:T(8,128)}, f32[2,64,128]{2,1,0:T(8,128)}, f32[3,64,128]{2,1,0:T(8,128)}) custom-call(f32[1,10,512,128]{3,2,1,0:T(8,128)} %get-tuple-element.29.out_in, s32[8,128]{1,0:T(8,128)S(1)} %get-tuple-element.25.flag, f32[2,64,128]{2,1,0:T(8,128)S(1)} %get-tuple-element.30.vel, ...), custom_call_target="tpu_custom_call", output_to_operand_aliasing={{0}: (0, {})} | custom-call | flops 1000000 | bytes 1000000 | tf_op jit(solution)/shard_map/late/pallas_call | solution.py:648
  45.7 0.0 collective-permute-done.8.partner_far
  45.7 0.2 last.1
Async XLA Ops:
  2.4 7.8 %collective-permute-start.4 = (f32[10,64,128]{2,1,0:T(8,128)S(1)}, f32[10,64,128]{2,1,0:T(8,128)S(1)}, u32[]{:S(2)}, u32[]{:S(2)}) collective-permute-start(f32[10,64,128]{2,1,0:T(8,128)S(1)} %get-tuple-element.24.snap.own), channel_id=1, source_target_pairs={{0,192},{32,96},{64,0},{96,160},{128,64},{160,224},{192,128},{224,... | collective-permute-start | bytes 983048 | tf_op jit(solution)/shard_map/ppermute | solution.py:580
  2.5 10.0 %collective-permute-start.5 = (f32[10,64,128]{2,1,0:T(8,128)S(1)}, f32[10,64,128]{2,1,0:T(8,128)S(1)}, u32[]{:S(2)}, u32[]{:S(2)}) collective-permute-start(f32[10,64,128]{2,1,0:T(8,128)S(1)} %get-tuple-element.24.snap.own), channel_id=1, source_target_pairs={{0,64},{32,224},{64,128},{96,32},{128,192},{160,96},{192,0},{224,1... | collective-permute-start | bytes 983048 | tf_op jit(solution)/shard_map/ppermute | solution.py:583
  12.5 32.4 %collective-permute-start.7 = (f32[3,10,64,128]{3,2,1,0:T(8,128)S(1)}, f32[3,10,64,128]{3,2,1,0:T(8,128)S(1)}, u32[]{:S(2)}, u32[]{:S(2)}) collective-permute-start(f32[3,10,64,128]{3,2,1,0:T(8,128)S(1)} %join.1), channel_id=1, source_target_pairs={{0,32},{32,0},{64,96},{96,64},{128,160},{160,128},{192,224},{224,1... | collective-permute-start | bytes 2949128 | tf_op jit(solution)/shard_map/ppermute | solution.py:628
  14.0 6.2 %collective-permute-start.6 = (f32[10,64,128]{2,1,0:T(8,128)S(1)}, f32[10,64,128]{2,1,0:T(8,128)S(1)}, u32[]{:S(2)}, u32[]{:S(2)}) collective-permute-start(f32[10,64,128]{2,1,0:T(8,128)S(1)} %collective-permute-done.4.near), channel_id=1, source_target_pairs={{0,192},{32,96},{64,0},{96,160},{128,64},{160,224},{192,128},{224,... | collective-permute-start | bytes 983048 | tf_op jit(solution)/shard_map/ppermute | solution.py:596
  20.3 25.4 %collective-permute-start.8 = (f32[10,64,128]{2,1,0:T(8,128)S(1)}, f32[10,64,128]{2,1,0:T(8,128)S(1)}, u32[]{:S(2)}, u32[]{:S(2)}) collective-permute-start(f32[10,64,128]{2,1,0:T(8,128)S(1)} %collective-permute-done.6.far), channel_id=1, source_target_pairs={{0,32},{32,0},{64,96},{96,64},{128,160},{160,128},{192,224},{224,1... | collective-permute-start | bytes 983048 | tf_op jit(solution)/shard_map/ppermute | solution.py:646
  22.4 10.2 %collective-permute-start = (f32[96,128]{1,0:T(8,128)S(1)}, f32[96,128]{1,0:T(8,128)S(1)}, u32[]{:S(2)}, u32[]{:S(2)}) collective-permute-start(f32[96,128]{1,0:T(8,128)S(1)} %get-tuple-element.20), channel_id=1, source_target_pairs={{0,1},{1,2},{2,3},{3,4},{4,5},{5,6},{6,7},{7,8},{8,9},{9,10},{10,1... | collective-permute-start | bytes 147464 | tf_op jit(solution)/shard_map/ppermute | solution.py:581
  24.2 8.5 %collective-permute-start.1 = (f32[96,128]{1,0:T(8,128)S(1)}, f32[96,128]{1,0:T(8,128)S(1)}, u32[]{:S(2)}, u32[]{:S(2)}) collective-permute-start(f32[96,128]{1,0:T(8,128)S(1)} %get-tuple-element.21), channel_id=1, source_target_pairs={{0,31},{1,0},{2,1},{3,2},{4,3},{5,4},{6,5},{7,6},{8,7},{9,8},{10,9... | collective-permute-start | bytes 147464 | tf_op jit(solution)/shard_map/ppermute | solution.py:582
  32.8 7.1 %collective-permute-start.2 = (f32[240,128]{1,0:T(8,128)S(1)}, f32[240,128]{1,0:T(8,128)S(1)}, u32[]{:S(2)}, u32[]{:S(2)}) collective-permute-start(f32[240,128]{1,0:T(8,128)S(1)} %get-tuple-element.22), channel_id=1, source_target_pairs={{224,255},{225,254},{226,253},{227,252},{228,251},{229,250},{230,2... | collective-permute-start | bytes 368648 | tf_op jit(solution)/shard_map/ppermute | solution.py:594
  37.4 2.6 %collective-permute-start.3 = (f32[240,128]{1,0:T(8,128)S(1)}, f32[240,128]{1,0:T(8,128)S(1)}, u32[]{:S(2)}, u32[]{:S(2)}) collective-permute-start(f32[240,128]{1,0:T(8,128)S(1)} %get-tuple-element.23), channel_id=1, source_target_pairs={{0,32},{32,0},{64,96},{96,64},{128,160},{160,128},{192,224},{224,1... | collective-permute-start | bytes 368648 | tf_op jit(solution)/shard_map/ppermute | solution.py:595

commit v10 on v9

--- a/solution.py
+++ b/solution.py
@@ -7,7 +7,7 @@
 
 
 SUB = 12
-SPLIT = 7
+SPLIT = 5
 ROWS = 64
 LANES = 128
 HALO = 16
@@ -420,7 +420,6 @@
 
     assemble(from_outer, from_inner, held)
     subcycles(held, 0, 5, 0, 12)
-    subcycles(held, 5, SPLIT, 1, 11)
 
     @pl.when(mine)
     def _():
@@ -432,12 +431,13 @@
             copy.wait()
 
 
-def second_half_kernel(state, out_in, flag, near, near_back, vel, stress, held, out, sems):
+def second_half_kernel(state, out_in, flag, near, near_back, far, vel, stress, held, out, sems):
     me = lax.axis_index("row")
     mine = jnp.max(flag[...]) == 1
     copies = [
         into(out, near, place_of(me, 1), sems.at[0]),
         into(out, near_back, place_of(me, 2), sems.at[1]),
+        into(out, far, place_of(me, 3), sems.at[2]),
     ]
 
     @pl.when(mine)
@@ -459,41 +459,32 @@
             copy.wait()
 
 
-def late_kernel(out_in, flag, vel, stress, far, partner, out, vel_out, stress_out, sems):
+def late_kernel(vel, stress, vel_out, stress_out, sems):
+    copies = [
+        pltpu.make_async_copy(vel, vel_out, sems.at[0]),
+        pltpu.make_async_copy(stress, stress_out, sems.at[1]),
+    ]
+    for copy in copies:
+        copy.start()
+    for copy in copies:
+        copy.wait()
+
+
+def last_kernel(out_in, flag, partner, out, sems):
     me = lax.axis_index("row")
-    fields_out = [
-        pltpu.make_async_copy(vel, vel_out, sems.at[4]),
-        pltpu.make_async_copy(stress, stress_out, sems.at[5]),
-    ]
-    for copy in fields_out:
-        copy.start()
     mine = jnp.max(flag[...]) == 1
 
     @pl.when(mine)
     def _():
-        copies = [into(out, partner.at[n], place_of(me, 4 + n), sems.at[n]) for n in range(3)]
-        copies.append(into(out, far, place_of(me, 3), sems.at[3]))
+        copies = [into(out, partner.at[n], place_of(me, 4 + n), sems.at[n]) for n in range(4)]
         for copy in copies:
             copy.start()
         for copy in copies:
             copy.wait()
 
-    for copy in fields_out:
-        copy.wait()
-
-
-def last_kernel(out_in, flag, partner_far, out, sem):
-    mine = jnp.max(flag[...]) == 1
-
-    @pl.when(mine)
-    def _():
-        copy = into(out, partner_far, place_of(lax.axis_index("row"), 7), sem)
-        copy.start()
-        copy.wait()
-
-
-def join_kernel(own, near, near_back, joined):
-    for n, block in enumerate((own, near, near_back)):
+
+def join_kernel(own, near, near_back, far, joined):
+    for n, block in enumerate((own, near, near_back, far)):
         joined[n] = block[...]
 
 
@@ -619,12 +610,12 @@
 
     joined = pl.pallas_call(
         join_kernel,
-        out_shape=shape(3, 10, ROWS, LANES),
-        in_specs=[vmem()] * 3,
+        out_shape=shape(4, 10, ROWS, LANES),
+        in_specs=[vmem()] * 4,
         out_specs=vmem(),
         compiler_params=grant(8),
         name="join",
-    )(snap, near, near_back)
+    )(snap, near, near_back, far)
     partner_blocks = lax.ppermute(joined, "row", partner)
 
     velocity, stress, _, restart = pl.pallas_call(
@@ -635,41 +626,35 @@
             shape(HELD, 2, TALL, LANES),
             shape(1, 10, 8 * ROWS, LANES),
         ),
-        in_specs=[vmem(), hbm(), vmem(), hbm(), hbm()],
+        in_specs=[vmem(), hbm(), vmem(), hbm(), hbm(), hbm()],
         out_specs=(vmem(), vmem(), vmem(), hbm()),
         input_output_aliases={0: 2, 1: 3},
-        scratch_shapes=[pltpu.SemaphoreType.DMA((2,))],
+        scratch_shapes=[pltpu.SemaphoreType.DMA((3,))],
         compiler_params=grant(8),
         cost_estimate=pl.CostEstimate(flops=20000000, bytes_accessed=2000000, transcendentals=0),
         name="second_half",
-    )(state, restart, flag, near, near_back)
-    partner_far = lax.ppermute(far, "row", partner)
-
-    restart, velocity, stress = pl.pallas_call(
+    )(state, restart, flag, near, near_back, far)
+
+    velocity, stress = pl.pallas_call(
         late_kernel,
-        out_shape=(
-            shape(1, 10, 8 * ROWS, LANES),
-            shape(2, ROWS, LANES),
-            shape(3, ROWS, LANES),
-        ),
-        in_specs=[hbm(), vmem()] + [hbm()] * 4,
-        out_specs=(hbm(), hbm(), hbm()),
-        input_output_aliases={0: 0},
-        scratch_shapes=[pltpu.SemaphoreType.DMA((6,))],
+        out_shape=(shape(2, ROWS, LANES), shape(3, ROWS, LANES)),
+        in_specs=[hbm(), hbm()],
+        out_specs=(hbm(), hbm()),
+        scratch_shapes=[pltpu.SemaphoreType.DMA((2,))],
         compiler_params=grant(4),
         cost_estimate=pl.CostEstimate(flops=1000000, bytes_accessed=1000000, transcendentals=0),
         name="late",
-    )(restart, flag, velocity, stress, far, partner_blocks)
+    )(velocity, stress)
     restart = pl.pallas_call(
         last_kernel,
         out_shape=shape(1, 10, 8 * ROWS, LANES),
         in_specs=[hbm(), vmem(), hbm()],
         out_specs=hbm(),
         input_output_aliases={0: 0},
-        scratch_shapes=[pltpu.SemaphoreType.DMA],
+        scratch_shapes=[pltpu.SemaphoreType.DMA((4,))],
         compiler_params=grant(4),
         name="last",
-    )(restart, flag, partner_far)
+    )(restart, flag, partner_blocks)
     return (velocity, stress, restart)
 
 

time: 46 us -> 45.8 us (level)
  waiting for transfers between devices: 18.6 us -> 16.8 us
  starting transfers between devices: 18.4 us -> 20.1 us
    ppermute x1, starting transfers between devices: 1.53 us -> 6.11 us  [step(): partner_blocks = lax.ppermute(joined, 'row', partner)]
    ppermute x1 -> x0, starting transfers between devices: 2.16 us -> none  [step(): partner_far = lax.ppermute(far, 'row', partner)]
    ppermute x1, waiting for transfers between devices: 5.73 us -> 3.7 us  [step(): far = lax.ppermute(near, 'row', along)]
    pallas_call x1, Pallas kernels: 1.87 us -> 2.53 us  [step(): pl.pallas_call(second_half_kernel, out_shape=(shape(2, ROWS, LANES), shap...]
    pallas_call x1, Pallas kernels: 3.12 us -> 2.48 us  [step(): pl.pallas_call(first_half_kernel, out_shape=(shape(HELD, 2, TALL, LANES),...]
    ppermute x1, starting transfers between devices: 0.49 us -> 0.01 us  [step(): far = lax.ppermute(near, 'row', along)]
  transfers between devices with their start and end apart: 9 -> 8, of which waited for: 5 -> 5; matrix products, arithmetic and copies ran while one was open for 0% -> 0% of each run, Pallas kernels for 13% -> 13%
where the time goes in v10:
time: 45.8 us; the launch traced here: 45.7 us
  starting transfers between devices  20.1 us (44%)
  waiting for transfers between devices  16.8 us (37%)
  Pallas kernels  8.14 us (18%)
  between operations  0.71 us (2%)
    ppermute x1, starting transfers between devices, step(): from_east = lax.ppermute(to_west, 'col', westward)  6.39 us
    ppermute x1, waiting for transfers between devices, step(): near = lax.ppermute(snap, 'row', along)  6.29 us
    ppermute x1, starting transfers between devices, step(): partner_blocks = lax.ppermute(joined, 'row', partner)  6.11 us
    ppermute x1, starting transfers between devices, step(): from_outer = lax.ppermute(outer, ('row', 'col'), across)  4.32 us
    ppermute x1, waiting for transfers between devices, step(): far = lax.ppermute(near, 'row', along)  3.7 us
    ppermute x1, waiting for transfers between devices, step(): from_outer = lax.ppermute(outer, ('row', 'col'), across)  2.53 us
    pallas_call x1, Pallas kernels, step(): pl.pallas_call(second_half_kernel, out_shape=(shape(2, ROWS, LANES), shap...  2.53 us
    pallas_call x1, Pallas kernels, step(): pl.pallas_call(first_half_kernel, out_shape=(shape(HELD, 2, TALL, LANES),...  2.48 us
  transfers between devices with their start and end apart: 8, of which 5 were waited for; matrix products, arithmetic and copies ran while one was open for 0% of the time, Pallas kernels for 13%

profile of v10, /device:TPU:7, one launch (start us, length us, event | category | flops | bytes accessed | tf_op | source)
XLA Modules:
  0.0 45.7 jit_solution(5694578684192177203)
XLA Ops:
  0.6 1.7 %prepare.1 = (f32[12,64,128]{2,1,0:T(8,128)S(1)}, f32[96,128]{1,0:T(8,128)S(1)}, f32[96,128]{1,0:T(8,128)S(1)}, f32[10,64,128]{2,1,0:T(8,128)S(1)}, s32[8,128]{1,0:T(8,128)S(1)}, /*index=5*/f32[10,64,128]{2,1,0:T(8,128)S(1)}) custom-call(f32[2,64,128]{2,1,0:T(8,128)} %vel_hbm.1, f32[3,64,128]{2,1,0:T(8,128)} %stress_hbm.1, f32[2,64,128]{2,1,0:T(8,128)} %wind_hbm.1, ...), custom_call_target="tpu_custom_call" | custom-call | tf_op jit(solution)/shard_map/prepare/pallas_call | solution.py:516
  2.4 0.1 collective-permute-start.4
  2.5 1.5 %collective-permute-start.5 = (f32[10,64,128]{2,1,0:T(8,128)S(1)}, f32[10,64,128]{2,1,0:T(8,128)S(1)}, u32[]{:S(2)}, u32[]{:S(2)}) collective-permute-start(f32[10,64,128]{2,1,0:T(8,128)S(1)} %get-tuple-element.23.snap.own), channel_id=1, source_target_pairs={{0,64},{32,224},{64,128},{96,32},{128,192},{160,96},{192,0},{224,1... | collective-permute-start | bytes 983048 | tf_op jit(solution)/shard_map/ppermute | solution.py:574
  3.9 6.3 %collective-permute-done.4.near = f32[10,64,128]{2,1,0:T(8,128)S(1)} collective-permute-done((f32[10,64,128]{2,1,0:T(8,128)S(1)}, f32[10,64,128]{2,1,0:T(8,128)S(1)}, u32[]{:S(2)}, u32[]{:S(2)}) %collective-permute-start.4) | collective-permute-done | bytes 327712 | tf_op jit(solution)/shard_map/ppermute | solution.py:571
  10.2 0.0 collective-permute-start.6
  10.2 2.2 %collective-permute-done.5.near_back = f32[10,64,128]{2,1,0:T(8,128)S(1)} collective-permute-done((f32[10,64,128]{2,1,0:T(8,128)S(1)}, f32[10,64,128]{2,1,0:T(8,128)S(1)}, u32[]{:S(2)}, u32[]{:S(2)}) %collective-permute-start.5) | collective-permute-done | bytes 327712 | tf_op jit(solution)/shard_map/ppermute | solution.py:574
  12.4 3.7 %collective-permute-done.6.far = f32[10,64,128]{2,1,0:T(8,128)S(1)} collective-permute-done((f32[10,64,128]{2,1,0:T(8,128)S(1)}, f32[10,64,128]{2,1,0:T(8,128)S(1)}, u32[]{:S(2)}, u32[]{:S(2)}) %collective-permute-start.6) | collective-permute-done | bytes 327712 | tf_op jit(solution)/shard_map/ppermute | solution.py:587
  16.1 0.1 join.1
  16.2 6.1 %collective-permute-start.7 = (f32[4,10,64,128]{3,2,1,0:T(8,128)S(1)}, f32[4,10,64,128]{3,2,1,0:T(8,128)S(1)}, u32[]{:S(2)}, u32[]{:S(2)}) collective-permute-start(f32[4,10,64,128]{3,2,1,0:T(8,128)S(1)} %join.1), channel_id=1, source_target_pairs={{0,32},{32,0},{64,96},{96,64},{128,160},{160,128},{192,224},{224,1... | collective-permute-start | bytes 3932168 | tf_op jit(solution)/shard_map/ppermute | solution.py:619
  22.3 1.7 %collective-permute-start = (f32[96,128]{1,0:T(8,128)S(1)}, f32[96,128]{1,0:T(8,128)S(1)}, u32[]{:S(2)}, u32[]{:S(2)}) collective-permute-start(f32[96,128]{1,0:T(8,128)S(1)} %get-tuple-element.19), channel_id=1, source_target_pairs={{0,1},{1,2},{2,3},{3,4},{4,5},{5,6},{6,7},{7,8},{8,9},{9,10},{10,1... | collective-permute-start | bytes 147464 | tf_op jit(solution)/shard_map/ppermute | solution.py:572
  24.1 6.4 %collective-permute-start.1 = (f32[96,128]{1,0:T(8,128)S(1)}, f32[96,128]{1,0:T(8,128)S(1)}, u32[]{:S(2)}, u32[]{:S(2)}) collective-permute-start(f32[96,128]{1,0:T(8,128)S(1)} %get-tuple-element.20), channel_id=1, source_target_pairs={{0,31},{1,0},{2,1},{3,2},{4,3},{5,4},{6,5},{7,6},{8,7},{9,8},{10,9... | collective-permute-start | bytes 147464 | tf_op jit(solution)/shard_map/ppermute | solution.py:573
  30.5 2.0 %collective-permute-done.from_west = f32[96,128]{1,0:T(8,128)S(1)} collective-permute-done((f32[96,128]{1,0:T(8,128)S(1)}, f32[96,128]{1,0:T(8,128)S(1)}, u32[]{:S(2)}, u32[]{:S(2)}) %collective-permute-start) | collective-permute-done | bytes 49184 | tf_op jit(solution)/shard_map/ppermute | solution.py:572
  32.5 0.0 collective-permute-done.1.from_east
  32.5 0.1 rows.1
  32.6 4.3 %collective-permute-start.2 = (f32[240,128]{1,0:T(8,128)S(1)}, f32[240,128]{1,0:T(8,128)S(1)}, u32[]{:S(2)}, u32[]{:S(2)}) collective-permute-start(f32[240,128]{1,0:T(8,128)S(1)} %get-tuple-element.21), channel_id=1, source_target_pairs={{224,255},{225,254},{226,253},{227,252},{228,251},{229,250},{230,2... | collective-permute-start | bytes 368648 | tf_op jit(solution)/shard_map/ppermute | solution.py:585
  36.9 0.0 collective-permute-start.3
  36.9 0.3 own.1.state
  37.2 2.5 %collective-permute-done.2.from_outer = f32[240,128]{1,0:T(8,128)S(1)} collective-permute-done((f32[240,128]{1,0:T(8,128)S(1)}, f32[240,128]{1,0:T(8,128)S(1)}, u32[]{:S(2)}, u32[]{:S(2)}) %collective-permute-start.2) | collective-permute-done | bytes 122912 | tf_op jit(solution)/shard_map/ppermute | solution.py:585
  39.8 0.0 collective-permute-done.3.from_inner
  39.8 2.5 %first_half.1 = (f32[23,2,112,128]{3,2,1,0:T(8,128)S(1)}, f32[1,10,512,128]{3,2,1,0:T(8,128)}) custom-call(f32[23,2,112,128]{3,2,1,0:T(8,128)S(1)} %own.1.state, f32[240,128]{1,0:T(8,128)S(1)} %collective-permute-done.2.from_outer, f32[240,128]{1,0:T(8,128)S(1)} %collective-permute-done.3.from_inner, ...), custom_call_target="tpu_custom_call", output_to_operand_aliasing={{0}: (0, {})} | custom-call | flops 20000000 | bytes 2000000 | tf_op jit(solution)/shard_map/first_half/pallas_call | solution.py:599
  42.2 2.5 %second_half.1 = (f32[2,64,128]{2,1,0:T(8,128)S(1)}, f32[3,64,128]{2,1,0:T(8,128)S(1)}, f32[23,2,112,128]{3,2,1,0:T(8,128)S(1)}, f32[1,10,512,128]{3,2,1,0:T(8,128)}) custom-call(f32[23,2,112,128]{3,2,1,0:T(8,128)S(1)} %get-tuple-element.26.state, f32[1,10,512,128]{3,2,1,0:T(8,128)} %get-tuple-element.27.out_in, ...), custom_call_target="tpu_custom_call", output_to_operand_aliasing={{2}: (0, {}), {3}: (1, {})} | custom-call | flops 20000000 | bytes 2000000 | tf_op jit(solution)/shard_map/second_half/pallas_call | solution.py:621
  44.8 0.7 %late.1 = (f32[2,64,128]{2,1,0:T(8,128)}, f32[3,64,128]{2,1,0:T(8,128)}) custom-call(f32[2,64,128]{2,1,0:T(8,128)S(1)} %get-tuple-element.28.vel, f32[3,64,128]{2,1,0:T(8,128)S(1)} %get-tuple-element.29.stress), custom_call_target="tpu_custom_call" | custom-call | flops 1000000 | bytes 1000000 | tf_op jit(solution)/shard_map/late/pallas_call | solution.py:638
  45.5 0.0 collective-permute-done.7.partner
  45.5 0.2 last.1
Async XLA Ops:
  2.4 7.8 %collective-permute-start.4 = (f32[10,64,128]{2,1,0:T(8,128)S(1)}, f32[10,64,128]{2,1,0:T(8,128)S(1)}, u32[]{:S(2)}, u32[]{:S(2)}) collective-permute-start(f32[10,64,128]{2,1,0:T(8,128)S(1)} %get-tuple-element.23.snap.own), channel_id=1, source_target_pairs={{0,192},{32,96},{64,0},{96,160},{128,64},{160,224},{192,128},{224,... | collective-permute-start | bytes 983048 | tf_op jit(solution)/shard_map/ppermute | solution.py:571
  2.5 10.0 %collective-permute-start.5 = (f32[10,64,128]{2,1,0:T(8,128)S(1)}, f32[10,64,128]{2,1,0:T(8,128)S(1)}, u32[]{:S(2)}, u32[]{:S(2)}) collective-permute-start(f32[10,64,128]{2,1,0:T(8,128)S(1)} %get-tuple-element.23.snap.own), channel_id=1, source_target_pairs={{0,64},{32,224},{64,128},{96,32},{128,192},{160,96},{192,0},{224,1... | collective-permute-start | bytes 983048 | tf_op jit(solution)/shard_map/ppermute | solution.py:574
  10.2 5.9 %collective-permute-start.6 = (f32[10,64,128]{2,1,0:T(8,128)S(1)}, f32[10,64,128]{2,1,0:T(8,128)S(1)}, u32[]{:S(2)}, u32[]{:S(2)}) collective-permute-start(f32[10,64,128]{2,1,0:T(8,128)S(1)} %collective-permute-done.4.near), channel_id=1, source_target_pairs={{0,192},{32,96},{64,0},{96,160},{128,64},{160,224},{192,128},{224,... | collective-permute-start | bytes 983048 | tf_op jit(solution)/shard_map/ppermute | solution.py:587
  16.2 29.2 %collective-permute-start.7 = (f32[4,10,64,128]{3,2,1,0:T(8,128)S(1)}, f32[4,10,64,128]{3,2,1,0:T(8,128)S(1)}, u32[]{:S(2)}, u32[]{:S(2)}) collective-permute-start(f32[4,10,64,128]{3,2,1,0:T(8,128)S(1)} %join.1), channel_id=1, source_target_pairs={{0,32},{32,0},{64,96},{96,64},{128,160},{160,128},{192,224},{224,1... | collective-permute-start | bytes 3932168 | tf_op jit(solution)/shard_map/ppermute | solution.py:619
  22.3 10.2 %collective-permute-start = (f32[96,128]{1,0:T(8,128)S(1)}, f32[96,128]{1,0:T(8,128)S(1)}, u32[]{:S(2)}, u32[]{:S(2)}) collective-permute-start(f32[96,128]{1,0:T(8,128)S(1)} %get-tuple-element.19), channel_id=1, source_target_pairs={{0,1},{1,2},{2,3},{3,4},{4,5},{5,6},{6,7},{7,8},{8,9},{9,10},{10,1... | collective-permute-start | bytes 147464 | tf_op jit(solution)/shard_map/ppermute | solution.py:572
  24.1 8.4 %collective-permute-start.1 = (f32[96,128]{1,0:T(8,128)S(1)}, f32[96,128]{1,0:T(8,128)S(1)}, u32[]{:S(2)}, u32[]{:S(2)}) collective-permute-start(f32[96,128]{1,0:T(8,128)S(1)} %get-tuple-element.20), channel_id=1, source_target_pairs={{0,31},{1,0},{2,1},{3,2},{4,3},{5,4},{6,5},{7,6},{8,7},{9,8},{10,9... | collective-permute-start | bytes 147464 | tf_op jit(solution)/shard_map/ppermute | solution.py:573
  32.6 7.1 %collective-permute-start.2 = (f32[240,128]{1,0:T(8,128)S(1)}, f32[240,128]{1,0:T(8,128)S(1)}, u32[]{:S(2)}, u32[]{:S(2)}) collective-permute-start(f32[240,128]{1,0:T(8,128)S(1)} %get-tuple-element.21), channel_id=1, source_target_pairs={{224,255},{225,254},{226,253},{227,252},{228,251},{229,250},{230,2... | collective-permute-start | bytes 368648 | tf_op jit(solution)/shard_map/ppermute | solution.py:585
  36.9 2.8 %collective-permute-start.3 = (f32[240,128]{1,0:T(8,128)S(1)}, f32[240,128]{1,0:T(8,128)S(1)}, u32[]{:S(2)}, u32[]{:S(2)}) collective-permute-start(f32[240,128]{1,0:T(8,128)S(1)} %get-tuple-element.22), channel_id=1, source_target_pairs={{0,32},{32,0},{64,96},{96,64},{128,160},{160,128},{192,224},{224,1... | collective-permute-start | bytes 368648 | tf_op jit(solution)/shard_map/ppermute | solution.py:586

commit v11 on v9

--- a/solution.py
+++ b/solution.py
@@ -7,7 +7,6 @@
 
 
 SUB = 12
-SPLIT = 7
 ROWS = 64
 LANES = 128
 HALO = 16
@@ -401,17 +400,18 @@
     return pltpu.make_async_copy(ref, out.at[0, :, pl.ds(place, ROWS), :], sem)
 
 
-def first_half_kernel(
-    state, from_outer, from_inner, snap, flag, zero, held, out, sems
+def stencil_kernel(
+    state, from_outer, from_inner, snap, near, near_back, flag, zero, vel, stress, held, out, sems
 ):
     me = lax.axis_index("row")
     mine = jnp.max(flag[...]) == 1
     zeros = [into(out, zero, n * ROWS, sems.at[n]) for n in range(8)]
-    own = into(out, snap, place_of(me, 0), sems.at[0])
+    own = [into(out, ref, place_of(me, n), sems.at[n]) for n, ref in enumerate((snap, near, near_back))]
 
     @pl.when(mine)
     def _():
-        own.start()
+        for copy in own:
+            copy.start()
 
     @pl.when(jnp.logical_not(mine))
     def _():
@@ -420,32 +420,7 @@
 
     assemble(from_outer, from_inner, held)
     subcycles(held, 0, 5, 0, 12)
-    subcycles(held, 5, SPLIT, 1, 11)
-
-    @pl.when(mine)
-    def _():
-        own.wait()
-
-    @pl.when(jnp.logical_not(mine))
-    def _():
-        for copy in zeros:
-            copy.wait()
-
-
-def second_half_kernel(state, out_in, flag, near, near_back, vel, stress, held, out, sems):
-    me = lax.axis_index("row")
-    mine = jnp.max(flag[...]) == 1
-    copies = [
-        into(out, near, place_of(me, 1), sems.at[0]),
-        into(out, near_back, place_of(me, 2), sems.at[1]),
-    ]
-
-    @pl.when(mine)
-    def _():
-        for copy in copies:
-            copy.start()
-
-    subcycles(held, SPLIT, SUB, 1, 11)
+    subcycles(held, 5, SUB, 1, 11)
     at = PAD + HALO
     vel[0] = held[U, 0, at : at + ROWS]
     vel[1] = held[V, 0, at : at + ROWS]
@@ -455,7 +430,12 @@
 
     @pl.when(mine)
     def _():
-        for copy in copies:
+        for copy in own:
+            copy.wait()
+
+    @pl.when(jnp.logical_not(mine))
+    def _():
+        for copy in zeros:
             copy.wait()
 
 
@@ -605,18 +585,6 @@
         cost_estimate=pl.CostEstimate(flops=1000000, bytes_accessed=1000000, transcendentals=0),
         name="own",
     )(fields, from_west, from_east)
-    state, restart = pl.pallas_call(
-        first_half_kernel,
-        out_shape=(shape(HELD, 2, TALL, LANES), shape(1, 10, 8 * ROWS, LANES)),
-        in_specs=[vmem()] * 3 + [hbm(), vmem(), hbm()],
-        out_specs=(vmem(), hbm()),
-        input_output_aliases={0: 0},
-        scratch_shapes=[pltpu.SemaphoreType.DMA((8,))],
-        compiler_params=grant(16),
-        cost_estimate=pl.CostEstimate(flops=20000000, bytes_accessed=2000000, transcendentals=0),
-        name="first_half",
-    )(state, from_outer, from_inner, snap, flag, blank)
-
     joined = pl.pallas_call(
         join_kernel,
         out_shape=shape(3, 10, ROWS, LANES),
@@ -628,21 +596,21 @@
     partner_blocks = lax.ppermute(joined, "row", partner)
 
     velocity, stress, _, restart = pl.pallas_call(
-        second_half_kernel,
+        stencil_kernel,
         out_shape=(
             shape(2, ROWS, LANES),
             shape(3, ROWS, LANES),
             shape(HELD, 2, TALL, LANES),
             shape(1, 10, 8 * ROWS, LANES),
         ),
-        in_specs=[vmem(), hbm(), vmem(), hbm(), hbm()],
+        in_specs=[vmem()] * 3 + [hbm()] * 3 + [vmem(), hbm()],
         out_specs=(vmem(), vmem(), vmem(), hbm()),
-        input_output_aliases={0: 2, 1: 3},
-        scratch_shapes=[pltpu.SemaphoreType.DMA((2,))],
-        compiler_params=grant(8),
-        cost_estimate=pl.CostEstimate(flops=20000000, bytes_accessed=2000000, transcendentals=0),
-        name="second_half",
-    )(state, restart, flag, near, near_back)
+        input_output_aliases={0: 2},
+        scratch_shapes=[pltpu.SemaphoreType.DMA((8,))],
+        compiler_params=grant(16),
+        cost_estimate=pl.CostEstimate(flops=40000000, bytes_accessed=2000000, transcendentals=0),
+        name="stencil",
+    )(state, from_outer, from_inner, snap, near, near_back, flag, blank)
     partner_far = lax.ppermute(far, "row", partner)
 
     restart, velocity, stress = pl.pallas_call(

time: 46 us -> 45.8 us (level)
    pallas_call x2 -> x1, Pallas kernels: 4.99 us -> 4.76 us  [step(): pl.pallas_call(stencil_kernel, out_shape=(shape(2, ROWS, LANES), shape(3,...]
where the time goes in v11:
time: 45.8 us; the launch traced here: 45.7 us
  waiting for transfers between devices  18.6 us (41%)
  starting transfers between devices  18.4 us (40%)
  Pallas kernels  7.9 us (17%)
  between operations  0.71 us (2%)
    ppermute x1, starting transfers between devices, step(): from_east = lax.ppermute(to_west, 'col', westward)  6.39 us
    ppermute x1, waiting for transfers between devices, step(): near = lax.ppermute(snap, 'row', along)  6.29 us
    ppermute x1, waiting for transfers between devices, step(): far = lax.ppermute(near, 'row', along)  5.73 us
    pallas_call x1, Pallas kernels, step(): pl.pallas_call(stencil_kernel, out_shape=(shape(2, ROWS, LANES), shape(3,...  4.76 us
    ppermute x1, starting transfers between devices, step(): from_outer = lax.ppermute(outer, ('row', 'col'), across)  4.59 us
    ppermute x1, waiting for transfers between devices, step(): from_outer = lax.ppermute(outer, ('row', 'col'), across)  2.27 us
    ppermute x1, waiting for transfers between devices, step(): near_back = lax.ppermute(snap, 'row', against)  2.22 us
    ppermute x1, starting transfers between devices, step(): partner_far = lax.ppermute(far, 'row', partner)  2.16 us
  transfers between devices with their start and end apart: 9, of which 5 were waited for; matrix products, arithmetic and copies ran while one was open for 0% of the time, Pallas kernels for 13%

profile of v11, /device:TPU:7, one launch (start us, length us, event | category | flops | bytes accessed | tf_op | source)
XLA Modules:
  0.0 45.7 jit_solution(9303320161083232202)
XLA Ops:
  0.6 1.7 %prepare.1 = (f32[12,64,128]{2,1,0:T(8,128)S(1)}, f32[96,128]{1,0:T(8,128)S(1)}, f32[96,128]{1,0:T(8,128)S(1)}, f32[10,64,128]{2,1,0:T(8,128)S(1)}, s32[8,128]{1,0:T(8,128)S(1)}, /*index=5*/f32[10,64,128]{2,1,0:T(8,128)S(1)}) custom-call(f32[2,64,128]{2,1,0:T(8,128)} %vel_hbm.1, f32[3,64,128]{2,1,0:T(8,128)} %stress_hbm.1, f32[2,64,128]{2,1,0:T(8,128)} %wind_hbm.1, ...), custom_call_target="tpu_custom_call" | custom-call | tf_op jit(solution)/shard_map/prepare/pallas_call | solution.py:505
  2.4 0.1 collective-permute-start.4
  2.5 1.5 %collective-permute-start.5 = (f32[10,64,128]{2,1,0:T(8,128)S(1)}, f32[10,64,128]{2,1,0:T(8,128)S(1)}, u32[]{:S(2)}, u32[]{:S(2)}) collective-permute-start(f32[10,64,128]{2,1,0:T(8,128)S(1)} %get-tuple-element.22.snap.own), channel_id=1, source_target_pairs={{0,64},{32,224},{64,128},{96,32},{128,192},{160,96},{192,0},{224,1... | collective-permute-start | bytes 983048 | tf_op jit(solution)/shard_map/ppermute | solution.py:563
  3.9 6.3 %collective-permute-done.4.near = f32[10,64,128]{2,1,0:T(8,128)S(1)} collective-permute-done((f32[10,64,128]{2,1,0:T(8,128)S(1)}, f32[10,64,128]{2,1,0:T(8,128)S(1)}, u32[]{:S(2)}, u32[]{:S(2)}) %collective-permute-start.4) | collective-permute-done | bytes 327712 | tf_op jit(solution)/shard_map/ppermute | solution.py:560
  10.2 2.2 %collective-permute-done.5.near_back = f32[10,64,128]{2,1,0:T(8,128)S(1)} collective-permute-done((f32[10,64,128]{2,1,0:T(8,128)S(1)}, f32[10,64,128]{2,1,0:T(8,128)S(1)}, u32[]{:S(2)}, u32[]{:S(2)}) %collective-permute-start.5) | collective-permute-done | bytes 327712 | tf_op jit(solution)/shard_map/ppermute | solution.py:563
  12.4 0.1 join.1
  12.5 1.5 %collective-permute-start.7 = (f32[3,10,64,128]{3,2,1,0:T(8,128)S(1)}, f32[3,10,64,128]{3,2,1,0:T(8,128)S(1)}, u32[]{:S(2)}, u32[]{:S(2)}) collective-permute-start(f32[3,10,64,128]{3,2,1,0:T(8,128)S(1)} %join.1), channel_id=1, source_target_pairs={{0,32},{32,0},{64,96},{96,64},{128,160},{160,128},{192,224},{224,1... | collective-permute-start | bytes 2949128 | tf_op jit(solution)/shard_map/ppermute | solution.py:596
  14.0 0.5 %collective-permute-start.6 = (f32[10,64,128]{2,1,0:T(8,128)S(1)}, f32[10,64,128]{2,1,0:T(8,128)S(1)}, u32[]{:S(2)}, u32[]{:S(2)}) collective-permute-start(f32[10,64,128]{2,1,0:T(8,128)S(1)} %collective-permute-done.4.near), channel_id=1, source_target_pairs={{0,192},{32,96},{64,0},{96,160},{128,64},{160,224},{192,128},{224,... | collective-permute-start | bytes 983048 | tf_op jit(solution)/shard_map/ppermute | solution.py:576
  14.5 5.7 %collective-permute-done.6.far = f32[10,64,128]{2,1,0:T(8,128)S(1)} collective-permute-done((f32[10,64,128]{2,1,0:T(8,128)S(1)}, f32[10,64,128]{2,1,0:T(8,128)S(1)}, u32[]{:S(2)}, u32[]{:S(2)}) %collective-permute-start.6) | collective-permute-done | bytes 327712 | tf_op jit(solution)/shard_map/ppermute | solution.py:576
  20.3 2.2 %collective-permute-start.8 = (f32[10,64,128]{2,1,0:T(8,128)S(1)}, f32[10,64,128]{2,1,0:T(8,128)S(1)}, u32[]{:S(2)}, u32[]{:S(2)}) collective-permute-start(f32[10,64,128]{2,1,0:T(8,128)S(1)} %collective-permute-done.6.far), channel_id=1, source_target_pairs={{0,32},{32,0},{64,96},{96,64},{128,160},{160,128},{192,224},{224,1... | collective-permute-start | bytes 983048 | tf_op jit(solution)/shard_map/ppermute | solution.py:614
  22.4 1.7 %collective-permute-start = (f32[96,128]{1,0:T(8,128)S(1)}, f32[96,128]{1,0:T(8,128)S(1)}, u32[]{:S(2)}, u32[]{:S(2)}) collective-permute-start(f32[96,128]{1,0:T(8,128)S(1)} %get-tuple-element.18), channel_id=1, source_target_pairs={{0,1},{1,2},{2,3},{3,4},{4,5},{5,6},{6,7},{7,8},{8,9},{9,10},{10,1... | collective-permute-start | bytes 147464 | tf_op jit(solution)/shard_map/ppermute | solution.py:561
  24.2 6.4 %collective-permute-start.1 = (f32[96,128]{1,0:T(8,128)S(1)}, f32[96,128]{1,0:T(8,128)S(1)}, u32[]{:S(2)}, u32[]{:S(2)}) collective-permute-start(f32[96,128]{1,0:T(8,128)S(1)} %get-tuple-element.19), channel_id=1, source_target_pairs={{0,31},{1,0},{2,1},{3,2},{4,3},{5,4},{6,5},{7,6},{8,7},{9,8},{10,9... | collective-permute-start | bytes 147464 | tf_op jit(solution)/shard_map/ppermute | solution.py:562
  30.6 2.1 %collective-permute-done.from_west = f32[96,128]{1,0:T(8,128)S(1)} collective-permute-done((f32[96,128]{1,0:T(8,128)S(1)}, f32[96,128]{1,0:T(8,128)S(1)}, u32[]{:S(2)}, u32[]{:S(2)}) %collective-permute-start) | collective-permute-done | bytes 49184 | tf_op jit(solution)/shard_map/ppermute | solution.py:561
  32.7 0.0 collective-permute-done.1.from_east
  32.7 0.1 rows.1
  32.8 4.6 %collective-permute-start.2 = (f32[240,128]{1,0:T(8,128)S(1)}, f32[240,128]{1,0:T(8,128)S(1)}, u32[]{:S(2)}, u32[]{:S(2)}) collective-permute-start(f32[240,128]{1,0:T(8,128)S(1)} %get-tuple-element.20), channel_id=1, source_target_pairs={{224,255},{225,254},{226,253},{227,252},{228,251},{229,250},{230,2... | collective-permute-start | bytes 368648 | tf_op jit(solution)/shard_map/ppermute | solution.py:574
  37.4 0.0 collective-permute-start.3
  37.4 0.3 own.1.state
  37.7 2.3 %collective-permute-done.2.from_outer = f32[240,128]{1,0:T(8,128)S(1)} collective-permute-done((f32[240,128]{1,0:T(8,128)S(1)}, f32[240,128]{1,0:T(8,128)S(1)}, u32[]{:S(2)}, u32[]{:S(2)}) %collective-permute-start.2) | collective-permute-done | bytes 122912 | tf_op jit(solution)/shard_map/ppermute | solution.py:574
  39.9 0.0 collective-permute-done.3.from_inner
  39.9 4.8 %stencil.1 = (f32[2,64,128]{2,1,0:T(8,128)S(1)}, f32[3,64,128]{2,1,0:T(8,128)S(1)}, f32[23,2,112,128]{3,2,1,0:T(8,128)S(1)}, f32[1,10,512,128]{3,2,1,0:T(8,128)}) custom-call(f32[23,2,112,128]{3,2,1,0:T(8,128)S(1)} %own.1.state, f32[240,128]{1,0:T(8,128)S(1)} %collective-permute-done.2.from_outer, ...), custom_call_target="tpu_custom_call", output_to_operand_aliasing={{2}: (0, {})} | custom-call | flops 40000000 | bytes 2000000 | tf_op jit(solution)/shard_map/stencil/pallas_call | solution.py:598
  44.7 0.0 collective-permute-done.7.partner
  44.7 0.7 %late.1 = (f32[1,10,512,128]{3,2,1,0:T(8,128)}, f32[2,64,128]{2,1,0:T(8,128)}, f32[3,64,128]{2,1,0:T(8,128)}) custom-call(f32[1,10,512,128]{3,2,1,0:T(8,128)} %get-tuple-element.25.out_in, s32[8,128]{1,0:T(8,128)S(1)} %get-tuple-element.23.flag, f32[2,64,128]{2,1,0:T(8,128)S(1)} %get-tuple-element.26.vel, ...), custom_call_target="tpu_custom_call", output_to_operand_aliasing={{0}: (0, {})} | custom-call | flops 1000000 | bytes 1000000 | tf_op jit(solution)/shard_map/late/pallas_call | solution.py:616
  45.4 0.0 collective-permute-done.8.partner_far
  45.4 0.2 last.1
Async XLA Ops:
  2.4 7.8 %collective-permute-start.4 = (f32[10,64,128]{2,1,0:T(8,128)S(1)}, f32[10,64,128]{2,1,0:T(8,128)S(1)}, u32[]{:S(2)}, u32[]{:S(2)}) collective-permute-start(f32[10,64,128]{2,1,0:T(8,128)S(1)} %get-tuple-element.22.snap.own), channel_id=1, source_target_pairs={{0,192},{32,96},{64,0},{96,160},{128,64},{160,224},{192,128},{224,... | collective-permute-start | bytes 983048 | tf_op jit(solution)/shard_map/ppermute | solution.py:560
  2.5 10.0 %collective-permute-start.5 = (f32[10,64,128]{2,1,0:T(8,128)S(1)}, f32[10,64,128]{2,1,0:T(8,128)S(1)}, u32[]{:S(2)}, u32[]{:S(2)}) collective-permute-start(f32[10,64,128]{2,1,0:T(8,128)S(1)} %get-tuple-element.22.snap.own), channel_id=1, source_target_pairs={{0,64},{32,224},{64,128},{96,32},{128,192},{160,96},{192,0},{224,1... | collective-permute-start | bytes 983048 | tf_op jit(solution)/shard_map/ppermute | solution.py:563
  12.5 32.2 %collective-permute-start.7 = (f32[3,10,64,128]{3,2,1,0:T(8,128)S(1)}, f32[3,10,64,128]{3,2,1,0:T(8,128)S(1)}, u32[]{:S(2)}, u32[]{:S(2)}) collective-permute-start(f32[3,10,64,128]{3,2,1,0:T(8,128)S(1)} %join.1), channel_id=1, source_target_pairs={{0,32},{32,0},{64,96},{96,64},{128,160},{160,128},{192,224},{224,1... | collective-permute-start | bytes 2949128 | tf_op jit(solution)/shard_map/ppermute | solution.py:596
  14.0 6.2 %collective-permute-start.6 = (f32[10,64,128]{2,1,0:T(8,128)S(1)}, f32[10,64,128]{2,1,0:T(8,128)S(1)}, u32[]{:S(2)}, u32[]{:S(2)}) collective-permute-start(f32[10,64,128]{2,1,0:T(8,128)S(1)} %collective-permute-done.4.near), channel_id=1, source_target_pairs={{0,192},{32,96},{64,0},{96,160},{128,64},{160,224},{192,128},{224,... | collective-permute-start | bytes 983048 | tf_op jit(solution)/shard_map/ppermute | solution.py:576
  20.3 25.2 %collective-permute-start.8 = (f32[10,64,128]{2,1,0:T(8,128)S(1)}, f32[10,64,128]{2,1,0:T(8,128)S(1)}, u32[]{:S(2)}, u32[]{:S(2)}) collective-permute-start(f32[10,64,128]{2,1,0:T(8,128)S(1)} %collective-permute-done.6.far), channel_id=1, source_target_pairs={{0,32},{32,0},{64,96},{96,64},{128,160},{160,128},{192,224},{224,1... | collective-permute-start | bytes 983048 | tf_op jit(solution)/shard_map/ppermute | solution.py:614
  22.4 10.2 %collective-permute-start = (f32[96,128]{1,0:T(8,128)S(1)}, f32[96,128]{1,0:T(8,128)S(1)}, u32[]{:S(2)}, u32[]{:S(2)}) collective-permute-start(f32[96,128]{1,0:T(8,128)S(1)} %get-tuple-element.18), channel_id=1, source_target_pairs={{0,1},{1,2},{2,3},{3,4},{4,5},{5,6},{6,7},{7,8},{8,9},{9,10},{10,1... | collective-permute-start | bytes 147464 | tf_op jit(solution)/shard_map/ppermute | solution.py:561
  24.2 8.5 %collective-permute-start.1 = (f32[96,128]{1,0:T(8,128)S(1)}, f32[96,128]{1,0:T(8,128)S(1)}, u32[]{:S(2)}, u32[]{:S(2)}) collective-permute-start(f32[96,128]{1,0:T(8,128)S(1)} %get-tuple-element.19), channel_id=1, source_target_pairs={{0,31},{1,0},{2,1},{3,2},{4,3},{5,4},{6,5},{7,6},{8,7},{9,8},{10,9... | collective-permute-start | bytes 147464 | tf_op jit(solution)/shard_map/ppermute | solution.py:562
  32.8 7.1 %collective-permute-start.2 = (f32[240,128]{1,0:T(8,128)S(1)}, f32[240,128]{1,0:T(8,128)S(1)}, u32[]{:S(2)}, u32[]{:S(2)}) collective-permute-start(f32[240,128]{1,0:T(8,128)S(1)} %get-tuple-element.20), channel_id=1, source_target_pairs={{224,255},{225,254},{226,253},{227,252},{228,251},{229,250},{230,2... | collective-permute-start | bytes 368648 | tf_op jit(solution)/shard_map/ppermute | solution.py:574
  37.4 2.6 %collective-permute-start.3 = (f32[240,128]{1,0:T(8,128)S(1)}, f32[240,128]{1,0:T(8,128)S(1)}, u32[]{:S(2)}, u32[]{:S(2)}) collective-permute-start(f32[240,128]{1,0:T(8,128)S(1)} %get-tuple-element.21), channel_id=1, source_target_pairs={{0,32},{32,0},{64,96},{96,64},{128,160},{160,128},{192,224},{224,1... | collective-permute-start | bytes 368648 | tf_op jit(solution)/shard_map/ppermute | solution.py:575
